TPU v7x, 8 devices: a whole 2x2x1 slice. The times are simulated.
8 devices in a mesh: dp: 1 (over z), tp: 8 (over y, x, core).
Axes of the slice: x: 2, y: 2, z: 1, core: 2. Of those that a mesh axis runs over, the one named last changes fastest.
Arguments:
- x_saved: bfloat16 [2, 1024, 4096], P('dp')
- h1_saved: bfloat16 [2, 1024, 4096], P('dp')
- grad_y: bfloat16 [2, 1024, 4096], P('dp')
- mean_one: float32 [2, 1024], P('dp')
- rstd_one: float32 [2, 1024], P('dp')
- mean_two: float32 [2, 1024], P('dp')
- rstd_two: float32 [2, 1024], P('dp')
- gain_one: bfloat16 [4096], replicated
- gain_two: bfloat16 [4096], replicated
- w_qkv: bfloat16 [4096, 32, 3, 128], P(None, 'tp')
- w_out: bfloat16 [32, 128, 4096], P('tp')
- w_up: bfloat16 [4096, 16384], P(None, 'tp')
- w_down: bfloat16 [16384, 4096], P('tp')
Outputs:
- output 1: bfloat16 [2, 1024, 4096], P('dp')
- output 2: bfloat16 [4096, 32, 3, 128], P('dp', 'tp')
- output 3: bfloat16 [32, 128, 4096], P(('dp', 'tp'))
- output 4: bfloat16 [4096, 16384], P('dp', 'tp')
- output 5: bfloat16 [16384, 4096], P(('dp', 'tp'))
All inputs are finite; a program needn't handle non-finite values.
Results may differ from a plain program's by a relative error of at most 0.0170333.
Values are sent between devices in bfloat16 or wider.
A program may use at most 1 GiB of HBM per device.

v0:
```python
import jax
import jax.numpy as jnp
from jax import lax
from jax.sharding import PartitionSpec as P
from functools import partial

GELU_C = 0.7978845608028654
GELU_A = 0.044715
wide_einsum = partial(jnp.einsum, preferred_element_type=jnp.float32)


def gelu_tanh(pre_act):
    inner_arg = GELU_C * (pre_act + GELU_A * pre_act * pre_act * pre_act)
    return 0.5 * pre_act * (1.0 + jnp.tanh(inner_arg))


def gelu_slope(pre_act):
    inner_arg = GELU_C * (pre_act + GELU_A * pre_act * pre_act * pre_act)
    tanh_val = jnp.tanh(inner_arg)
    return (0.5 * (1.0 + tanh_val)
            + 0.5 * pre_act * (1.0 - tanh_val * tanh_val) * GELU_C * (1.0 + 3.0 * GELU_A * pre_act * pre_act))


def norm_backward(grad_norm, value_a4, gain, rstd):
    scaled = grad_norm * gain.astype(jnp.float32)
    mean_scaled = jnp.mean(scaled, axis=-1, keepdims=True)
    mean_cross = jnp.mean(scaled * value_a4, axis=-1, keepdims=True)
    return rstd[..., None] * (scaled - mean_scaled - value_a4 * mean_cross)


def attention_backward(q_heads, k_heads, v_heads, grad_o, score_scale):
    seq_len = q_heads.shape[1]
    scores = wide_einsum('bqnd,bknd->bnqk', q_heads, k_heads) * score_scale
    causal = jnp.arange(seq_len)[:, None] >= jnp.arange(seq_len)[None, :]
    attn_prob = jax.nn.softmax(jnp.where(causal, scores, -1e30), axis=-1)
    prob_bf16 = attn_prob.astype(jnp.bfloat16)
    attn_out = wide_einsum('bnqk,bknd->bqnd', prob_bf16, v_heads).astype(jnp.bfloat16)
    grad_v = wide_einsum('bnqk,bqnd->bknd', prob_bf16, grad_o).astype(jnp.bfloat16)
    grad_p = wide_einsum('bqnd,bknd->bnqk', grad_o, v_heads)
    row_dot = jnp.sum(attn_prob * grad_p, axis=-1, keepdims=True)
    grad_s = (attn_prob * (grad_p - row_dot) * score_scale).astype(jnp.bfloat16)
    grad_q = wide_einsum('bnqk,bknd->bqnd', grad_s, k_heads).astype(jnp.bfloat16)
    grad_k = wide_einsum('bnqk,bqnd->bknd', grad_s, q_heads).astype(jnp.bfloat16)
    return attn_out, jnp.stack([grad_q, grad_k, grad_v], axis=3)


def solution(mesh):
    act_spec = P('dp', None, None)
    stat_spec = P('dp', None)
    in_specs = (act_spec, act_spec, act_spec, stat_spec, stat_spec, stat_spec, stat_spec, P(), P(),
                P(None, 'tp', None, None), P('tp', None, None), P(None, 'tp'), P('tp', None))
    out_specs = (act_spec, P('dp', 'tp', None, None), P(('dp', 'tp'), None, None), P('dp', 'tp'),
                 P(('dp', 'tp'), None))

    def local_backward(x_saved, h1_saved, grad_y, mean_one, rstd_one, mean_two, rstd_two,
                       gain_one, gain_two, w_qkv, w_out, w_up, w_down):
        score_scale = w_qkv.shape[3] ** -0.5
        array_b8 = (h1_saved.astype(jnp.float32) - mean_two[..., None]) * rstd_two[..., None]
        norm_two = (array_b8 * gain_two.astype(jnp.float32)).astype(jnp.bfloat16)
        pre_act = wide_einsum('msh,hf->msf', norm_two, w_up)
        act_out = gelu_tanh(pre_act).astype(jnp.bfloat16)
        grad_down = wide_einsum('msf,msh->fh', act_out, grad_y).astype(jnp.bfloat16)
        grad_pre = (wide_einsum('msh,fh->msf', grad_y, w_down) * gelu_slope(pre_act)).astype(jnp.bfloat16)
        grad_up = wide_einsum('msh,msf->hf', norm_two, grad_pre).astype(jnp.bfloat16)
        part_two = wide_einsum('msf,hf->msh', grad_pre, w_up).astype(jnp.bfloat16)
        grad_norm_two = lax.psum(part_two, 'tp').astype(jnp.float32)
        grad_h1 = (grad_y.astype(jnp.float32)
                   + norm_backward(grad_norm_two, array_b8, gain_two, rstd_two)).astype(jnp.bfloat16)
        value_a8 = (x_saved.astype(jnp.float32) - mean_one[..., None]) * rstd_one[..., None]
        norm_one = (value_a8 * gain_one.astype(jnp.float32)).astype(jnp.bfloat16)
        qkv_acts = wide_einsum('msh,hncd->msncd', norm_one, w_qkv).astype(jnp.bfloat16)
        grad_o = wide_einsum('msh,ndh->msnd', grad_h1, w_out).astype(jnp.bfloat16)
        attn_out, grad_qkv = attention_backward(qkv_acts[:, :, :, 0], qkv_acts[:, :, :, 1], qkv_acts[:, :, :, 2],
                                                grad_o, score_scale)
        grad_out_w = wide_einsum('msnd,msh->ndh', attn_out, grad_h1).astype(jnp.bfloat16)
        grad_qkv_w = wide_einsum('msh,msncd->hncd', norm_one, grad_qkv).astype(jnp.bfloat16)
        part_one = wide_einsum('msncd,hncd->msh', grad_qkv, w_qkv).astype(jnp.bfloat16)
        grad_norm_one = lax.psum(part_one, 'tp').astype(jnp.float32)
        grad_x = (grad_h1.astype(jnp.float32)
                  + norm_backward(grad_norm_one, value_a8, gain_one, rstd_one)).astype(jnp.bfloat16)
        return grad_x, grad_qkv_w, grad_out_w, grad_up, grad_down

    return jax.shard_map(local_backward, mesh=mesh, in_specs=in_specs, out_specs=out_specs, check_vma=False)
```

profile of v0, /device:TPU:0, one launch (start us, length us, event | category | flops | bytes accessed | tf_op | source)
XLA Modules:
  0.0 819.4 jit_solution(16701799847604268470)
XLA Ops:
  7.2 0.0 all-reduce.3.cloned.1.call-start
  7.2 0.7 convert_element_type.100
  7.9 43.4 %fusion.25 = f32[2,1024,2048]{2,1,0:T(8,128)} fusion(bf16[4096,2048]{1,0:T(8,128)(2,1)} %param.24, bf16[2,1024,4096]{2,1,0:T(8,128)(2,1)} %param.14, f32[4096]{0:T(1024)S(1)} %convert_element_type.100, f32[2,1024]{1,0:T(2,128)} %param.18, f32[2,1024]{1,0:T(2,128)} %param.19), kind=kOutput, calls=%fused_computation.43 | convolution fusion | flops 34401681408 | bytes 50364416 | tf_op jit(solution)/shard_map/msh,hf->msf/dot_general | solution.py:60
  51.3 55.0 %fusion.14 = bf16[2,1024,2048]{2,1,0:T(8,128)(2,1)} fusion(f32[2,1024,2048]{2,1,0:T(8,128)} %fusion.25, bf16[2,1024,4096]{2,1,0:T(8,128)(2,1)} %param.15, bf16[2048,4096]{1,0:T(8,128)(2,1)} %param.25), kind=kOutput, calls=%fused_computation.32 | convolution fusion | flops 34439430144 | bytes 58720256 | tf_op jit(solution)/shard_map/msh,fh->msf/dot_general | solution.py:63
  106.3 42.2 %fusion.43 = bf16[2,1024,4096]{2,1,0:T(8,128)(2,1)} fusion(bf16[2,1024,2048]{2,1,0:T(8,128)(2,1)} %fusion.14, bf16[4096,2048]{1,0:T(8,128)(2,1)} %param.24), kind=kOutput, calls=%fused_computation.59 | convolution fusion | flops 34368126976 | bytes 41943040 | tf_op jit(solution)/shard_map/msf,hf->msh/dot_general | solution.py:65
  148.5 0.0 all-reduce.3.cloned.1.call-update
  148.5 0.0 all-reduce.5.cloned.1.call-start
  148.6 0.3 iota_compare_fusion
  148.9 0.3 copy-done.5
  149.3 43.6 %bitcast_convert_fusion.2 = bf16[4096,2048]{1,0:T(8,128)(2,1)} fusion(bf16[2,1024,2048]{2,1,0:T(8,128)(2,1)} %fusion.14, bf16[2,1024,4096]{2,1,0:T(8,128)(2,1)} %param.14, f32[4096]{0:T(1024)S(1)} %copy-done.5, f32[2,1024]{1,0:T(2,128)S(1)} %copy-done.7, f32[2,1024]{1,0:T(2,128)S(1)} %copy-done.9), kind=kOutput, calls=%fused_computation.4 | convolution fusion | flops 34410070016 | bytes 41975808 | tf_op jit(solution)/shard_map/msh,msf->hf/dot_general | solution.py:64
  192.9 0.6 copy-done.2
  193.5 33.9 %fusion.60 = bf16[2,1024,4,3,128]{4,1,3,2,0:T(8,128)(2,1)} fusion(bf16[4096,4,3,128]{3,1,2,0:T(4,128)(2,1)} %param.22, f32[4096]{0:T(1024)S(1)} %convert_element_type.108, f32[2,1024]{1,0:T(2,128)S(1)} %copy-done.11, f32[2,1024]{1,0:T(2,128)S(1)} %copy-done.13, bf16[2,1024,4096]{2,1,0:T(8,128)(2,1)} %param.13), kind=kOutput, calls=%fused_computation.70 | convolution fusion | flops 25814892544 | bytes 35684352 | tf_op jit(solution)/shard_map/msh,hncd->msncd/dot_general | solution.py:71
  227.4 19.8 %fusion.98 = (f32[2,4,1024]{2,1,0:T(4,128)S(1)}, f32[2,4,1024,1024]{2,3,1,0:T(8,128)}) fusion(pred[1024,1024]{0,1:T(8,128)(4,1)S(1)} %iota_compare_fusion, bf16[2,1024,4,3,128]{4,1,3,2,0:T(8,128)(2,1)} %fusion.60), kind=kOutput, calls=%fused_computation.98 | convolution fusion | flops 2181039104 | bytes 38830080 | tf_op jit(solution)/shard_map/sub | solution.py:35
  247.2 17.8 %fusion.97 = bf16[2,4,1024,1024]{2,3,1,0:T(8,128)(2,1)} fusion(f32[2,4,1024,1024]{2,3,1,0:T(8,128)} %get-tuple-element.15, f32[2,4,1024]{2,1,0:T(4,128)S(1)} %get-tuple-element.14), kind=kLoop, calls=%fused_computation.97 | loop fusion | flops 16777216 | bytes 50364416 | tf_op jit(solution)/shard_map/convert_element_type | solution.py:36
  265.0 48.1 %bitcast_convert_fusion.1 = bf16[2048,4096]{1,0:T(8,128)(2,1)} fusion(bf16[2,1024,4096]{2,1,0:T(8,128)(2,1)} %param.15, f32[2,1024,2048]{2,1,0:T(8,128)} %fusion.25), kind=kOutput, calls=%fused_computation.3 | convolution fusion | flops 34405875712 | bytes 50331648 | tf_op jit(solution)/shard_map/msf,msh->fh/dot_general | solution.py:62
  313.1 44.6 %all-reduce.3.cloned.1.call-done = bf16[2,1024,4096]{2,1,0:T(8,128)(2,1)} async-done(((bf16[2,1024,4096]{2,1,0:T(8,128)(2,1)}), bf16[2,1024,4096]{2,1,0:T(8,128)(2,1)}) %all-reduce.3.cloned.1.call-update) | async-done | bytes 16777232 | tf_op jit(solution)/shard_map/psum | solution.py:66
  357.8 16.1 %fusion.4 = (f32[2,1024]{1,0:T(2,128)S(1)}, f32[2,1024]{1,0:T(2,128)S(1)}) fusion(bf16[2,1024,4096]{2,1,0:T(8,128)(2,1)} %all-reduce.3.cloned.1.call-done, f32[4096]{0:T(1024)S(1)} %copy-done.6, f32[2,1024]{1,0:T(2,128)S(1)} %copy-done.10, f32[2,1024]{1,0:T(2,128)S(1)} %copy-done.8, bf16[2,1024,4096]{2,1,0:T(8,128)(2,1)} %param.14), kind=kLoop, calls=%fused_computation.19 | loop fusion | flops 67104768 | bytes 33603584 | tf_op jit(solution)/shard_map/reduce_sum | solution.py:26
  374.0 28.3 %add_convert_fusion.1 = bf16[2,1024,4096]{2,1,0:T(8,128)(2,1)} fusion(bf16[2,1024,4096]{2,1,0:T(8,128)(2,1)} %all-reduce.3.cloned.1.call-done, bf16[2,1024,4096]{2,1,0:T(8,128)(2,1)} %param.14, bf16[2,1024,4096]{2,1,0:T(8,128)(2,1)} %param.15, f32[2,1024]{1,0:T(2,128)S(1)} %get-tuple-element.16, f32[2,1024]{1,0:T(2,128)S(1)} %get-tuple-element.17, ...), kind=kLoop, calls=%fused_computation.16 | loop fusion | flops 100663296 | bytes 67158016 | tf_op jit(solution)/shard_map/convert_element_type | solution.py:68
  402.3 12.5 %fusion.80 = bf16[2,1024,4,128]{3,1,2,0:T(8,128)(2,1)S(1)} fusion(bf16[4,128,4096]{2,1,0:T(8,128)(2,1)S(1)} %copy-done.16, bf16[2,1024,4096]{2,1,0:T(8,128)(2,1)} %add_convert_fusion.1), kind=kOutput, calls=%fused_computation.80 | convolution fusion | flops 8590983168 | bytes 23068672 | tf_op jit(solution)/shard_map/msh,ndh->msnd/dot_general | solution.py:72
  414.8 14.8 %fusion.96 = f32[2,4,1024,1024]{2,3,1,0:T(8,128)} fusion(bf16[2,1024,4,128]{3,1,2,0:T(8,128)(2,1)S(1)} %fusion.80, bf16[2,1024,4,3,128]{4,1,3,2,0:T(8,128)(2,1)} %fusion.60), kind=kOutput, calls=%fused_computation.96 | convolution fusion | flops 2147483648 | bytes 37748736 | tf_op jit(solution)/shard_map/bqnd,bknd->bnqk/dot_general | solution.py:39
  429.6 43.9 %convert_bitcast_fusion.2 = bf16[2,1024,4,1,128]{1,4,2,0,3:T(8,128)(2,1)} fusion(f32[2,4,1024,1024]{2,3,1,0:T(8,128)} %fusion.96, bf16[2,1024,4,3,128]{4,1,3,2,0:T(8,128)(2,1)} %fusion.60, f32[2,4,1024,1024]{2,3,1,0:T(8,128)} %get-tuple-element.15, f32[2,4,1024]{2,1,0:T(4,128)S(1)} %get-tuple-element.14), kind=kOutput, calls=%fused_computation.79 | convolution fusion | flops 2207261696 | bytes 138477568 | tf_op jit(solution)/shard_map/bnqk,bknd->bqnd/dot_general | solution.py:42
  473.5 44.5 %convert_bitcast_fusion.1 = bf16[2,1024,4,1,128]{1,4,2,0,3:T(8,128)(2,1)} fusion(f32[2,4,1024,1024]{2,3,1,0:T(8,128)} %fusion.96, bf16[2,1024,4,3,128]{4,1,3,2,0:T(8,128)(2,1)} %fusion.60, f32[2,4,1024,1024]{2,3,1,0:T(8,128)} %get-tuple-element.15, f32[2,4,1024]{2,1,0:T(4,128)S(1)} %get-tuple-element.14), kind=kOutput, calls=%fused_computation.78 | convolution fusion | flops 2207261696 | bytes 138477568 | tf_op jit(solution)/shard_map/bnqk,bqnd->bknd/dot_general | solution.py:43
  517.9 9.5 %convert_bitcast_fusion = bf16[2,1024,4,1,128]{1,4,2,0,3:T(8,128)(2,1)S(1)} fusion(bf16[2,1024,4,128]{3,1,2,0:T(8,128)(2,1)S(1)} %fusion.80, bf16[2,4,1024,1024]{2,3,1,0:T(8,128)(2,1)} %fusion.97), kind=kOutput, calls=%fused_computation.77 | convolution fusion | flops 2148532224 | bytes 20971520 | tf_op jit(solution)/shard_map/bnqk,bqnd->bknd/dot_general | solution.py:38
  527.5 3.2 fusion.112
  530.6 31.3 %bitcast_convert_fusion = bf16[2,1024,4096]{2,1,0:T(8,128)(2,1)} fusion(bf16[4096,4,3,128,1]{3,1,2,0,4:T(4,128)(2,1)} %bitcast.118, bf16[2,1024,4,1,128]{1,4,2,0,3:T(8,128)(2,1)S(1)} %convert_bitcast_fusion, bf16[2,1024,4,1,128]{1,4,2,0,3:T(8,128)(2,1)S(1)} %copy-done.1, bf16[2,1024,4,1,128]{1,4,2,0,3:T(8,128)(2,1)S(1)} %copy-done), kind=kOutput, calls=%fused_computation.2 | convolution fusion | flops 25784483840 | bytes 35651584 | tf_op jit(solution)/shard_map/msncd,hncd->msh/dot_general | solution.py:77
  561.9 0.7 copy-done.3
  562.6 35.3 %bitcast_convert_fusion.3 = bf16[4096,4,3,128]{3,0,2,1:T(8,128)(2,1)} fusion(f32[4096]{0:T(1024)S(1)} %copy-done.3, f32[2,1024]{1,0:T(2,128)S(1)} %copy-done.12, f32[2,1024]{1,0:T(2,128)S(1)} %copy-done.14, bf16[2,1024,4096]{2,1,0:T(8,128)(2,1)} %param.13, bf16[2,1024,4,3,128]{1,4,0,3,2:T(8,128)(2,1)} %fusion.112), kind=kOutput, calls=%fused_computation.23 | convolution fusion | flops 25818038272 | bytes 35684352 | tf_op jit(solution)/shard_map/msh,msncd->hncd/dot_general | solution.py:76
  597.9 17.1 %copy.31 = bf16[4096,4,3,128]{3,1,2,0:T(4,128)(2,1)} copy(bf16[4096,4,3,128]{3,0,2,1:T(8,128)(2,1)} %bitcast_convert_fusion.3) | data formatting | bytes 25165824
  615.1 21.4 %bitcast_convert_fusion.4 = bf16[4,128,4096]{2,1,0:T(8,128)(2,1)} fusion(bf16[2,1024,4096]{2,1,0:T(8,128)(2,1)} %add_convert_fusion.1, bf16[2,4,1024,1024]{2,3,1,0:T(8,128)(2,1)} %fusion.97, bf16[2,1024,4,3,128]{4,1,3,2,0:T(8,128)(2,1)} %fusion.60), kind=kOutput, calls=%fused_computation.60 | convolution fusion | flops 10740563968 | bytes 39845888 | tf_op jit(solution)/shard_map/msnd,msh->ndh/dot_general | solution.py:75
  636.5 131.8 %all-reduce.5.cloned.1.call-done = bf16[2,1024,4096]{2,1,0:T(8,128)(2,1)} async-done(((bf16[2,1024,4096]{2,1,0:T(8,128)(2,1)}), bf16[2,1024,4096]{2,1,0:T(8,128)(2,1)}) %all-reduce.5.cloned.1.call-update) | async-done | bytes 16777232 | tf_op jit(solution)/shard_map/psum | solution.py:78
  768.3 15.7 %fusion.2 = (f32[2,1024]{1,0:T(2,128)S(1)}, f32[2,1024]{1,0:T(2,128)S(1)}) fusion(bf16[2,1024,4096]{2,1,0:T(8,128)(2,1)} %all-reduce.5.cloned.1.call-done, f32[4096]{0:T(1024)S(1)} %copy-done.3, f32[2,1024]{1,0:T(2,128)S(1)} %copy-done.12, f32[2,1024]{1,0:T(2,128)S(1)} %copy-done.14, bf16[2,1024,4096]{2,1,0:T(8,128)(2,1)} %param.13), kind=kLoop, calls=%fused_computation.8 | loop fusion | flops 67104768 | bytes 33603584 | tf_op jit(solution)/shard_map/reduce_sum | solution.py:26
  784.1 28.2 %add_convert_fusion = bf16[2,1024,4096]{2,1,0:T(8,128)(2,1)} fusion(bf16[2,1024,4096]{2,1,0:T(8,128)(2,1)} %all-reduce.5.cloned.1.call-done, bf16[2,1024,4096]{2,1,0:T(8,128)(2,1)} %param.13, bf16[2,1024,4096]{2,1,0:T(8,128)(2,1)} %add_convert_fusion.1, f32[2,1024]{1,0:T(2,128)S(1)} %broadcast_multiply_fusion, f32[2,1024]{1,0:T(2,128)S(1)} %broadcast_multiply_fusion.1, ...), kind=kLoop, calls=%fused_computation.5 | loop fusion | flops 100663296 | bytes 67158016 | tf_op jit(solution)/shard_map/convert_element_type | solution.py:80
  (36 shorter events, 0.1 us)
Async XLA Ops:
  7.2 350.6 %all-reduce.3.cloned.1.call-start = ((), (), s32[]{:S(2)}) async-start(), calls=%async_computation | async-start | bytes 33554432 | tf_op jit(solution)/shard_map/psum | solution.py:66
  7.9 43.4 %copy-start.4 = (f32[4096]{0:T(1024)}, f32[4096]{0:T(1024)S(1)}, u32[]{:S(2)}) copy-start(f32[4096]{0:T(1024)S(1)} %convert_element_type.100) | copy-start | bytes 49156
  148.5 0.7 copy-start.5
  148.5 0.7 copy-start.7
  148.5 0.7 copy-start.9
  148.5 619.8 %all-reduce.5.cloned.1.call-start = ((), (), s32[]{:S(2)}) async-start(), calls=%async_computation.1 | async-start | bytes 33554432 | tf_op jit(solution)/shard_map/psum | solution.py:78
  149.2 43.7 %copy-start.15 = (bf16[4096]{0:T(1024)(128)(2,1)S(1)}, bf16[4096]{0:T(1024)(128)(2,1)}, u32[]{:S(2)}) copy-start(bf16[4096]{0:T(1024)(128)(2,1)} %param.20) | copy-start | bytes 24580
  149.2 44.3 %copy-start.11 = (f32[2,1024]{1,0:T(2,128)S(1)}, f32[2,1024]{1,0:T(2,128)}, u32[]{:S(2)}) copy-start(f32[2,1024]{1,0:T(2,128)} %param.17) | copy-start | bytes 24580
  149.2 44.3 %copy-start.13 = (f32[2,1024]{1,0:T(2,128)S(1)}, f32[2,1024]{1,0:T(2,128)}, u32[]{:S(2)}) copy-start(f32[2,1024]{1,0:T(2,128)} %param.16) | copy-start | bytes 24580
  192.9 0.6 copy-start.2
  265.0 92.8 %copy-start.6 = (f32[4096]{0:T(1024)S(1)}, f32[4096]{0:T(1024)}, u32[]{:S(2)}) copy-start(f32[4096]{0:T(1024)} %copy-done.4) | copy-start | bytes 49156
  265.0 92.8 %copy-start.8 = (f32[2,1024]{1,0:T(2,128)S(1)}, f32[2,1024]{1,0:T(2,128)}, u32[]{:S(2)}) copy-start(f32[2,1024]{1,0:T(2,128)} %param.18) | copy-start | bytes 24580
  265.0 92.8 %copy-start.10 = (f32[2,1024]{1,0:T(2,128)S(1)}, f32[2,1024]{1,0:T(2,128)}, u32[]{:S(2)}) copy-start(f32[2,1024]{1,0:T(2,128)} %param.19) | copy-start | bytes 24580
  373.9 28.4 %copy-start.16 = (bf16[4,128,4096]{2,1,0:T(8,128)(2,1)S(1)}, bf16[4,128,4096]{2,1,0:T(8,128)(2,1)}, u32[]{:S(2)}) copy-start(bf16[4,128,4096]{2,1,0:T(8,128)(2,1)} %param.23) | copy-start | bytes 12582916
  517.9 9.5 %copy-start = (bf16[2,1024,4,1,128]{1,4,2,0,3:T(8,128)(2,1)S(1)}, bf16[2,1024,4,1,128]{1,4,2,0,3:T(8,128)(2,1)}, u32[]{:S(2)}) copy-start(bf16[2,1024,4,1,128]{1,4,2,0,3:T(8,128)(2,1)} %convert_bitcast_fusion.2) | copy-start | bytes 6291460
  517.9 9.5 %copy-start.1 = (bf16[2,1024,4,1,128]{1,4,2,0,3:T(8,128)(2,1)S(1)}, bf16[2,1024,4,1,128]{1,4,2,0,3:T(8,128)(2,1)}, u32[]{:S(2)}) copy-start(bf16[2,1024,4,1,128]{1,4,2,0,3:T(8,128)(2,1)} %convert_bitcast_fusion.1) | copy-start | bytes 6291460
  561.9 0.7 copy-start.3
  561.9 0.7 copy-start.12
  561.9 0.7 copy-start.14
Sparse Core Ops, SparseCore 0:
  148.7 209.0 all-reduce.2
  562.1 206.2 all-reduce.4
where the time goes:
time: 825 us; the launch traced here: 819 us
  matrix products  499 us (60%)
  waiting for transfers between devices  176 us (21%)
  other arithmetic  110 us (13%)
  local copies, waits for them, and re-layouts  18.8 us (2%)
  between operations  14.4 us (2%)
    psum x1, waiting for transfers between devices, local_backward(): grad_norm_one = lax.psum(part_one, 'tp').astype(jnp.float32)  132 us
    dot_general x1, matrix products, local_backward(): wide_einsum('msh,fh->msf', grad_y, w_down) * gelu_slope(pre_act)  55 us
    dot_general x1, matrix products, local_backward(): grad_down = wide_einsum('msf,msh->fh', act_out, grad_y).astype(jnp.bfloat16)  48.1 us
    psum x1, waiting for transfers between devices, local_backward(): grad_norm_two = lax.psum(part_two, 'tp').astype(jnp.float32)  44.6 us
    dot_general x1, matrix products, attention_backward(): wide_einsum('bnqk,bqnd->bknd', grad_s, q_heads).astype(jnp.bfloat16)  44.5 us
    dot_general x1, matrix products, attention_backward(): wide_einsum('bnqk,bknd->bqnd', grad_s, k_heads).astype(jnp.bfloat16)  43.9 us
    dot_general x1, matrix products, local_backward(): wide_einsum('msh,msf->hf', norm_two, grad_pre).astype(jnp.bfloat16)  43.6 us
    dot_general x1, matrix products, local_backward(): pre_act = wide_einsum('msh,hf->msf', norm_two, w_up)  43.4 us
  transfers between devices with their start and end apart: 2, of which 2 were waited for; matrix products, arithmetic and copies ran while one was open for 29% of the time, Pallas kernels for 0%

commit v1 on v0

v1 whole, which is shorter than its diff:
```python
import jax
import jax.numpy as jnp
from jax import lax
from jax.sharding import PartitionSpec as P
from jax.experimental import pallas as pl
from jax.experimental.pallas import tpu as pltpu
from functools import partial

GELU_C = 0.7978845608028654
GELU_A = 0.044715
F32 = jnp.float32
BF16 = jnp.bfloat16
BQ = 256
NT = (((1,), (1,)), ((), ()))
TN = (((0,), (0,)), ((), ()))
ANY = pl.BlockSpec(memory_space=pl.ANY)
TOKEN = jax.ShapeDtypeStruct((8, 128), F32)


def mm(a, b, dims=(((1,), (0,)), ((), ()))):
    return lax.dot_general(a, b, dims, preferred_element_type=F32)


def call(body, grid, in_specs, args, out_specs, outs, token, flops, scratch=(), pos=None, name=None):
    n_in, n_out, n_pos = len(args), len(outs), 0 if pos is None else 1

    def kernel(*refs):
        head, refs = refs[:n_pos], refs[n_pos:]
        body(*head, *refs[:n_in], *refs[n_in + 1:n_in + 1 + n_out], *refs[n_in + 2 + n_out:])

    size = sum(o.size * o.dtype.itemsize for o in outs) + sum(a.size * a.dtype.itemsize for a in args)
    results = pl.pallas_call(
        kernel,
        grid_spec=pltpu.PrefetchScalarGridSpec(
            num_scalar_prefetch=n_pos, grid=grid, in_specs=list(in_specs) + [ANY],
            out_specs=list(out_specs) + [ANY], scratch_shapes=list(scratch)),
        out_shape=list(outs) + [TOKEN],
        compiler_params=pltpu.CompilerParams(vmem_limit_bytes=60 * 1024 * 1024),
        cost_estimate=pl.CostEstimate(flops=int(flops), bytes_accessed=int(size), transcendentals=0),
        name=name,
    )(*([] if pos is None else [pos]), *args, token)
    return results


def sds(shape, dtype=BF16):
    return jax.ShapeDtypeStruct(shape, dtype)


def normed(rows, stats, gain):
    return ((rows.astype(F32) - stats[:, 0:1]) * stats[:, 1:2] * gain.astype(F32)).astype(BF16)


def mlp_kernel(h_ref, dy_ref, st_ref, g_ref, up_ref, down_ref, n_ref, act_ref, dpre_ref):
    @pl.when(pl.program_id(1) == 0)
    def _():
        n_ref[...] = normed(h_ref[0], st_ref[0], g_ref[...])

    for j in range(up_ref.shape[1] // 256):
        cols = pl.ds(j * 256, 256)
        a = mm(n_ref[...], up_ref[:, cols])
        b = mm(dy_ref[0], down_ref[cols, :], NT)
        tanh = jnp.tanh(GELU_C * (a + GELU_A * a * a * a))
        act_ref[:, cols] = (0.5 * a * (1.0 + tanh)).astype(BF16)
        slope = (0.5 * (1.0 + tanh)
                 + 0.5 * a * (1.0 - tanh * tanh) * GELU_C * (1.0 + 3.0 * GELU_A * a * a))
        dpre_ref[:, cols] = (b * slope).astype(BF16)


def mlp(m, h1, dy, stats, gain, w_up, w_down, token):
    _, seq, hid = h1.shape
    ffn = w_up.shape[1]
    bm, bn = 512, 512
    row = pl.BlockSpec((1, bm, hid), lambda i, j: (m, i, 0))
    tile = pl.BlockSpec((bm, bn), lambda i, j: (i, j))
    return call(
        mlp_kernel, (seq // bm, ffn // bn),
        [row, row, pl.BlockSpec((1, bm, 2), lambda i, j: (m, i, 0)), pl.BlockSpec((1, hid), lambda i, j: (0, 0)),
         pl.BlockSpec((hid, bn), lambda i, j: (0, j)), pl.BlockSpec((bn, hid), lambda i, j: (j, 0))],
        [h1, dy, stats, gain, w_up, w_down],
        [pl.BlockSpec((bm, hid), lambda i, j: (i, 0)), tile, tile],
        [sds((seq, hid)), sds((seq, ffn)), sds((seq, ffn))], token, 4 * seq * hid * ffn, name='mlp')


def qkv_kernel(x_ref, st_ref, g_ref, w_ref, n_ref, out_ref):
    @pl.when(pl.program_id(1) == 0)
    def _():
        n_ref[...] = normed(x_ref[0], st_ref[0], g_ref[...])

    out_ref[...] = mm(n_ref[...], w_ref[...]).astype(BF16)


def qkv_proj(m, x, stats, gain, w, token):
    _, seq, hid = x.shape
    bm, bn = 512, 512
    return call(
        qkv_kernel, (seq // bm, w.shape[1] // bn),
        [pl.BlockSpec((1, bm, hid), lambda i, j: (m, i, 0)), pl.BlockSpec((1, bm, 2), lambda i, j: (m, i, 0)),
         pl.BlockSpec((1, hid), lambda i, j: (0, 0)), pl.BlockSpec((hid, bn), lambda i, j: (0, j))],
        [x, stats, gain, w],
        [pl.BlockSpec((bm, hid), lambda i, j: (i, 0)), pl.BlockSpec((bm, bn), lambda i, j: (i, j))],
        [sds((seq, hid)), sds((seq, w.shape[1]))], token, 2 * seq * hid * w.shape[1], name='qkv')


def part_kernel(own, n_lhs, pos_ref, *refs):
    lhs, w_ref, rest = refs[:n_lhs], refs[n_lhs], refs[n_lhs + 1:]
    rows_ref = rest[-1]
    chip, core = pos_ref[1], pos_ref[2]
    blk = rows_ref.shape[0] // 4

    @pl.when(pl.program_id(0) == 0)
    def _():
        for k in range(4):
            start = (2 * jnp.bitwise_xor(chip, k) + (core if own else 1 - core)) * blk
            at = 0
            for ref in lhs:
                rows_ref[pl.ds(k * blk, blk), pl.ds(at, ref.shape[1])] = ref[pl.ds(start, blk), :]
                at += ref.shape[1]

    prod = mm(rows_ref[...], w_ref[...], NT)
    if own:
        got_ref, keep_ref = rest[0], rest[1]
        prod = prod + got_ref[...].astype(F32)
        keep_ref[...] = prod[:blk]
        for k in range(1, 4):
            rest[1 + k][...] = prod[k * blk:(k + 1) * blk].astype(BF16)
    else:
        rest[0][...] = prod.astype(BF16)


def partial_product(own, lhs, w, got, pos, token):
    seq = lhs[0].shape[0]
    hid, depth = w.shape
    bn, blk = 512, seq // 8
    in_specs = [pl.BlockSpec(l.shape, lambda j, p: (0, 0)) for l in lhs] + [pl.BlockSpec((bn, depth), lambda j, p: (j, 0))]
    args = list(lhs) + [w]
    if own:
        in_specs.append(pl.BlockSpec((4 * blk, bn), lambda j, p: (0, j)))
        args.append(got)
        out_specs = [pl.BlockSpec((blk, bn), lambda j, p: (0, j))] * 4
        outs = [sds((blk, hid), F32)] + [sds((blk, hid))] * 3
    else:
        out_specs = [pl.BlockSpec((4 * blk, bn), lambda j, p: (0, j))]
        outs = [sds((4 * blk, hid))]
    return call(partial(part_kernel, own, len(lhs)), (hid // bn,), in_specs, args, out_specs, outs, token,
                2 * seq // 2 * hid * depth, scratch=[pltpu.VMEM((4 * blk, depth), BF16)], pos=pos,
                name='own' if own else 'other')


def norm_kernel(pos_ref, keep_ref, r1_ref, r2_ref, r3_ref, act_ref, res_ref, st_ref, g_ref, out_ref):
    total = keep_ref[...] + r1_ref[...].astype(F32) + r2_ref[...].astype(F32) + r3_ref[...].astype(F32)
    rstd = st_ref[0, :, 1:2]
    hat = (act_ref[0].astype(F32) - st_ref[0, :, 0:1]) * rstd
    scaled = total * g_ref[...].astype(F32)
    mean_scaled = jnp.mean(scaled, axis=-1, keepdims=True)
    mean_cross = jnp.mean(scaled * hat, axis=-1, keepdims=True)
    res = res_ref[...].reshape(hat.shape).astype(F32)
    out_ref[...] = (res + rstd * (scaled - mean_scaled - hat * mean_cross)).astype(BF16)


def norm_shard(m, keep, got, acts, resid, stats, gain, pos, token):
    blk, hid = keep.shape
    bm = 32
    n = blk // bm
    local = pl.BlockSpec((bm, hid), lambda i, p: (i, 0))
    row = pl.BlockSpec((1, bm, hid), lambda i, p: (m, p[0] * n + i, 0))
    return call(
        norm_kernel, (n,),
        [local] * 4 + [row, row if resid.ndim == 3 else local,
                       pl.BlockSpec((1, bm, 2), lambda i, p: (m, p[0] * n + i, 0)), pl.BlockSpec((1, hid), lambda i, p: (0, 0))],
        [keep, *got, acts, resid, stats, gain], [local], [sds((blk, hid))], token, 20 * blk * hid, pos=pos, name='norm')


def proj_kernel(x_ref, w_ref, out_ref):
    out_ref[...] = mm(x_ref[...], w_ref[...], NT).astype(BF16)


def out_proj(dh, w, token):
    seq, hid = dh.shape
    bm = 256
    return call(proj_kernel, (seq // bm,),
                [pl.BlockSpec((bm, hid), lambda i: (i, 0)), pl.BlockSpec(w.shape, lambda i: (0, 0))], [dh, w],
                [pl.BlockSpec((bm, w.shape[0]), lambda i: (i, 0))], [sds((seq, w.shape[0]))], token,
                2 * seq * hid * w.shape[0], name='dout')


def attn_kernel(scale, q_ref, k_ref, v_ref, do_ref, o_ref, dq_ref, dk_ref, dv_ref, dk_acc, dv_acc):
    seq, dim = do_ref.shape
    k_all, v_all = k_ref[...], v_ref[...]
    k_t, v_t = k_all.T, v_all.T
    nblk = seq // BQ
    for i in reversed(range(nblk)):
        rows = pl.ds(i * BQ, BQ)
        width = (i + 1) * BQ
        q, do = q_ref[rows, :], do_ref[rows, :]
        s_t = mm(k_all[:width], q, NT) * scale
        kpos = lax.broadcasted_iota(jnp.int32, (width, BQ), 0)
        qpos = lax.broadcasted_iota(jnp.int32, (width, BQ), 1) + i * BQ
        s_t = jnp.where(qpos >= kpos, s_t, -1e30)
        top = jnp.max(s_t, axis=0, keepdims=True)
        p_t = jnp.exp(s_t - top)
        p_t = p_t * (1.0 / jnp.sum(p_t, axis=0, keepdims=True))
        p_b = p_t.astype(BF16)
        o_ref[rows, :] = mm(v_t[:, :width], p_b).T.astype(BF16)
        dp_t = mm(v_all[:width], do, NT)
        dot = jnp.sum(p_t * dp_t, axis=0, keepdims=True)
        ds_t = (p_t * (dp_t - dot) * scale).astype(BF16)
        dq_ref[rows, :] = mm(k_t[:, :width], ds_t).T.astype(BF16)
        dv, dk = mm(p_b, do), mm(ds_t, q)
        if i == nblk - 1:
            dv_acc[...] = dv
            dk_acc[...] = dk
        else:
            dv_acc[:width] += dv
            dk_acc[:width] += dk
    dk_ref[...] = dk_acc[...].astype(BF16)
    dv_ref[...] = dv_acc[...].astype(BF16)


def attention(qkv, do, dim, scale, token):
    seq, width = do.shape
    n = width // dim
    head = lambda c: pl.BlockSpec((seq, dim), lambda i: (0, c * n + i))
    return call(partial(attn_kernel, scale), (n,), [head(0), head(1), head(2), head(0)], [qkv, qkv, qkv, do],
                [head(0)] * 4, [sds((seq, width))] * 4, token, 24 * n * seq * seq * dim,
                scratch=[pltpu.VMEM((seq, dim), F32)] * 2, name='attn')


def grad_kernel(a0_ref, a1_ref, b0_ref, b1_ref, out_ref):
    left = lambda ref: ref[0] if len(ref.shape) == 3 else ref[...]
    acc = mm(left(a0_ref), left(b0_ref), TN) + mm(left(a1_ref), left(b1_ref), TN)
    out_ref[...] = acc.astype(BF16)


def weight_grad(lhs, rhs, token, ba, bb, name):
    def split(v, size, axis):
        if isinstance(v, (list, tuple)):
            spec = pl.BlockSpec((v[0].shape[0], size), lambda i, j: (0, (i, j)[axis]))
            return list(v), [spec] * 2, v[0].shape
        specs = [pl.BlockSpec((1, v.shape[1], size), lambda i, j, m=m: (m, 0, (i, j)[axis])) for m in range(2)]
        return [v, v], specs, v.shape[1:]

    la, ls, (seq, wa) = split(lhs, ba, 0)
    ra, rs, (_, wb) = split(rhs, bb, 1)
    return call(grad_kernel, (wa // ba, wb // bb), ls + rs, la + ra, [pl.BlockSpec((ba, bb), lambda i, j: (i, j))],
                [sds((wa, wb))], token, 4 * seq * wa * wb, name=name)


def qkv_grad_kernel(a0_ref, a1_ref, *refs):
    out_ref = refs[-1]
    rows, _, heads, dim = out_ref.shape
    for c in range(3):
        acc = mm(a0_ref[...], refs[c][...], TN) + mm(a1_ref[...], refs[3 + c][...], TN)
        out_ref[:, c] = acc.reshape(rows, heads, dim).astype(BF16)


def qkv_grad(norms, grads, heads, dim, token):
    seq, hid = norms[0].shape
    ba = 256
    lhs = pl.BlockSpec((seq, ba), lambda i: (0, i))
    whole = pl.BlockSpec((seq, heads * dim), lambda i: (0, 0))
    return call(qkv_grad_kernel, (hid // ba,), [lhs] * 2 + [whole] * 6, [*norms, *grads[0], *grads[1]],
                [pl.BlockSpec((ba, 3, heads, dim), lambda i: (i, 0, 0, 0))], [sds((hid, 3, heads, dim))], token,
                12 * seq * hid * heads * dim, name='dqkvw')


def flat_kernel(w_ref, out_ref):
    rows, _, heads, dim = w_ref.shape
    for c in range(3):
        out_ref[:, pl.ds(c * heads * dim, heads * dim)] = w_ref[:, c].reshape(rows, heads * dim)


def flat_weight(w, token):
    hid, three, heads, dim = w.shape
    bm = 256
    return call(flat_kernel, (hid // bm,), [pl.BlockSpec((bm, three, heads, dim), lambda i: (i, 0, 0, 0))], [w],
                [pl.BlockSpec((bm, three * heads * dim), lambda i: (i, 0))], [sds((hid, three * heads * dim))], token,
                w.size, name='flat')


def swap(arr, bit):
    return lax.ppermute(arr, 'tp', [(i, i ^ bit) for i in range(8)])


def solution(mesh):
    act_spec = P('dp', None, None)
    stat_spec = P('dp', None)
    in_specs = (act_spec, act_spec, act_spec, stat_spec, stat_spec, stat_spec, stat_spec, P(), P(),
                P(None, 'tp', None, None), P('tp', None, None), P(None, 'tp'), P('tp', None))
    out_specs = (act_spec, P('dp', 'tp', None, None), P(('dp', 'tp'), None, None), P('dp', 'tp'),
                 P(('dp', 'tp'), None))

    def local_backward(x_saved, h1_saved, grad_y, mean_one, rstd_one, mean_two, rstd_two,
                       gain_one, gain_two, w_qkv, w_out, w_up, w_down):
        hid, heads, _, dim = w_qkv.shape
        scale = dim ** -0.5
        idx = lax.axis_index('tp')
        pos = jnp.stack([idx, idx // 2, idx % 2]).astype(jnp.int32)
        stats_one = jnp.stack([mean_one, rstd_one], axis=-1)
        stats_two = jnp.stack([mean_two, rstd_two], axis=-1)
        g1, g2 = gain_one.reshape(1, hid), gain_two.reshape(1, hid)
        w_out = w_out.reshape(heads * dim, hid)
        tok = jnp.zeros((8, 128), F32)

        def gather(shard):
            return lax.all_gather(shard, 'tp', axis=0, tiled=True)

        def exchange(sends):
            return [swap(s, bit) for s, bit in zip(sends, (2, 4, 6))]

        w_flat, tok = flat_weight(w_qkv.transpose(0, 2, 1, 3), tok)
        n2, act, dpre, n1, qkv = [0, 0], [0, 0], [0, 0], [0, 0], [0, 0]
        dh_shard, dh, out, grads, dx = [0, 0], [0, 0], [0, 0], [0, 0], [0, 0]

        n2[0], act[0], dpre[0], tok = mlp(0, h1_saved, grad_y, stats_two, g2, w_up, w_down, tok)
        send, tok = partial_product(False, [dpre[0]], w_up, None, pos, tok)
        got = swap(send, 1)
        n1[0], qkv[0], tok = qkv_proj(0, x_saved, stats_one, g1, w_flat, tok)
        keep_a, *send, tok = partial_product(True, [dpre[0]], w_up, got, pos, tok)
        got_a = exchange(send)
        n2[1], act[1], dpre[1], tok = mlp(1, h1_saved, grad_y, stats_two, g2, w_up, w_down, tok)
        send, tok = partial_product(False, [dpre[1]], w_up, None, pos, tok)
        got = swap(send, 1)
        dh_shard[0], tok = norm_shard(0, keep_a, got_a, h1_saved, grad_y, stats_two, g2, pos, tok)
        dh[0] = gather(dh_shard[0])
        n1[1], qkv[1], tok = qkv_proj(1, x_saved, stats_one, g1, w_flat, tok)
        keep_b, *send, tok = partial_product(True, [dpre[1]], w_up, got, pos, tok)
        got_b = exchange(send)
        grad_down, tok = weight_grad(act, grad_y, tok, 512, 1024, 'dw2')
        grad_o, tok = out_proj(dh[0], w_out, tok)
        out[0], *grads[0], tok = attention(qkv[0], grad_o, dim, scale, tok)
        send, tok = partial_product(False, grads[0], w_flat, None, pos, tok)
        got = swap(send, 1)
        dh_shard[1], tok = norm_shard(1, keep_b, got_b, h1_saved, grad_y, stats_two, g2, pos, tok)
        dh[1] = gather(dh_shard[1])
        keep_a, *send, tok = partial_product(True, grads[0], w_flat, got, pos, tok)
        got_a = exchange(send)
        grad_up, tok = weight_grad(n2, dpre, tok, 512, 1024, 'dw1')
        grad_o, tok = out_proj(dh[1], w_out, tok)
        out[1], *grads[1], tok = attention(qkv[1], grad_o, dim, scale, tok)
        send, tok = partial_product(False, grads[1], w_flat, None, pos, tok)
        got = swap(send, 1)
        dx_shard, tok = norm_shard(0, keep_a, got_a, x_saved, dh_shard[0], stats_one, g1, pos, tok)
        dx[0] = gather(dx_shard)
        keep_b, *send, tok = partial_product(True, grads[1], w_flat, got, pos, tok)
        got_b = exchange(send)
        grad_qkv_w, tok = qkv_grad(n1, grads, heads, dim, tok)
        dx_shard, tok = norm_shard(1, keep_b, got_b, x_saved, dh_shard[1], stats_one, g1, pos, tok)
        dx[1] = gather(dx_shard)
        grad_out_w, tok = weight_grad(out, dh, tok, 512, 512, 'dwo')
        return (jnp.stack(dx), grad_qkv_w.transpose(0, 2, 1, 3), grad_out_w.reshape(heads, dim, hid), grad_up, grad_down)

    return jax.shard_map(local_backward, mesh=mesh, in_specs=in_specs, out_specs=out_specs, check_vma=False)
```

time: 825 us -> 701 us (0.85)
  Pallas kernels: 0 us -> 532 us
  matrix products: 499 us -> 0 us
  other arithmetic: 110 us -> 17.1 us
  waiting for transfers between devices: 176 us -> 98.9 us
  starting transfers between devices: 0.08 us -> 15.8 us
    pallas_call x0 -> x25, Pallas kernels: none -> 532 us  [call(): pl.pallas_call(kernel, grid_spec=pltpu.PrefetchScalarGridSpec(num_scalar_...]
    dot_general x14 -> x0, matrix products: 479 us -> none  [the longest x1 55 us: local_backward(): wide_einsum('msh,fh->msf', grad_y, w_down) * gelu_slope(pre_act)]
    psum x2 -> x0, waiting for transfers between devices: 176 us -> none  [the longest x1 132 us: local_backward(): grad_norm_one = lax.psum(part_one, 'tp').astype(jnp.float32)]
    convert_element_type x5 -> x0, other arithmetic: 75 us -> none  [the longest x1 28.3 us: local_backward(): grad_h1 = (grad_y.astype(jnp.float32) + norm_backward(grad_norm_two, arra...]
    all_gather x0 -> x4, waiting for transfers between devices: none -> 54.2 us  [gather(): return lax.all_gather(shard, 'tp', axis=0, tiled=True)]
    ppermute x0 -> x16, waiting for transfers between devices: none -> 44.6 us  [swap(): return lax.ppermute(arr, 'tp', [(i, i ^ bit) for i in range(8)])]
    reduce_sum x2 -> x0, other arithmetic: 31.9 us -> none  [norm_backward(): mean_scaled = jnp.mean(scaled, axis=-1, keepdims=True)]
    sub x1 -> x0, matrix products: 19.8 us -> none  [attention_backward(): attn_prob = jax.nn.softmax(jnp.where(causal, scores, -1e+30), axis=-1)]
  transfers between devices with their start and end apart: 2 -> 20, of which waited for: 2 -> 7; matrix products, arithmetic and copies ran while one was open for 29% -> 0% of each run, Pallas kernels for 0% -> 59%
where the time goes in v1:
time: 701 us; the launch traced here: 690 us
  Pallas kernels  532 us (76%)
  waiting for transfers between devices  98.9 us (14%)
  other arithmetic  17.1 us (2%)
  starting transfers between devices  15.8 us (2%)
  between operations  14.4 us (2%)
  local copies, waits for them, and re-layouts  11.3 us (2%)
    pallas_call x25, Pallas kernels, call(): pl.pallas_call(kernel, grid_spec=pltpu.PrefetchScalarGridSpec(num_scalar_...  532 us
    all_gather x4, waiting for transfers between devices, gather(): return lax.all_gather(shard, 'tp', axis=0, tiled=True)  54.2 us
    ppermute x16, waiting for transfers between devices, swap(): return lax.ppermute(arr, 'tp', [(i, i ^ bit) for i in range(8)])  44.6 us
    ppermute x16, starting transfers between devices, swap(): return lax.ppermute(arr, 'tp', [(i, i ^ bit) for i in range(8)])  15.7 us
  transfers between devices with their start and end apart: 20, of which 7 were waited for; matrix products, arithmetic and copies ran while one was open for 0% of the time, Pallas kernels for 59%

profile of v1, /device:TPU:0, one launch (start us, length us, event | category | flops | bytes accessed | tf_op | source)
XLA Modules:
  0.0 689.6 jit_solution(9312626251968520780)
XLA Ops:
  12.6 16.5 %flat.1 = (bf16[4096,1536]{1,0:T(8,128)(2,1)}, f32[8,128]{1,0:T(8,128)}) custom-call(bf16[4096,3,4,128]{3,2,1,0:T(4,128)(2,1)} %bitcast.13, f32[8,128]{1,0:T(8,128)} %broadcast_in_dim.3.refs_1_), custom_call_target="tpu_custom_call" | custom-call | flops 6291456 | bytes 25165824 | tf_op jit(solution)/shard_map/flat/pallas_call | solution.py:32
  29.7 54.6 %mlp.2 = (bf16[1024,4096]{1,0:T(8,128)(2,1)}, bf16[1024,2048]{1,0:T(8,128)(2,1)}, bf16[1024,2048]{1,0:T(8,128)(2,1)}, f32[8,128]{1,0:T(8,128)}) custom-call(bf16[2,1024,4096]{2,1,0:T(8,128)(2,1)} %refs_5_.9, bf16[2,1024,4096]{2,1,0:T(8,128)(2,1)} %refs_6_.3, f32[2,1024,2]{2,1,0:T(8,128)} %pad_maximum_fusion.2.refs_2_.refs_7_, ...), custom_call_target="tpu_custom_call" | custom-call | flops 34359738368 | bytes 83910656 | tf_op jit(solution)/shard_map/mlp/pallas_call | solution.py:32
  84.3 16.7 %other.4 = (bf16[512,4096]{1,0:T(8,128)(2,1)}, f32[8,128]{1,0:T(8,128)}) custom-call(s32[3]{0:T(128)} %pad_add_fusion.refs_0_, bf16[1024,2048]{1,0:T(8,128)(2,1)} %get-tuple-element.80.refs_1_.refs_2_, bf16[4096,2048]{1,0:T(8,128)(2,1)} %refs_2_.8, f32[8,128]{1,0:T(8,128)} %get-tuple-element.81.refs_3_), custom_call_target="tpu_custom_call" | custom-call | flops 8589934592 | bytes 25165824 | tf_op jit(solution)/shard_map/other/pallas_call | solution.py:32
  104.5 24.5 %qkv.2 = (bf16[1024,4096]{1,0:T(8,128)(2,1)}, bf16[1024,1536]{1,0:T(8,128)(2,1)}, f32[8,128]{1,0:T(8,128)}) custom-call(bf16[2,1024,4096]{2,1,0:T(8,128)(2,1)} %refs_5_.11, f32[2,1024,2]{2,1,0:T(8,128)} %pad_maximum_fusion.1.refs_1_.refs_7_, bf16[1,4096]{1,0:T(2,128)(2,1)} %reshape.22.refs_2_.refs_8_, bf16[4096,1536]{1,0:T(8,128)(2,1)} %get-tuple-element.78.refs_3_.refs_4_, ...), custom_call_target="tpu_custom_call" | custom-call | flops 12884901888 | bytes 40919040 | tf_op jit(solution)/shard_map/qkv/pallas_call | solution.py:32
  129.0 17.0 %own.4 = (f32[128,4096]{1,0:T(8,128)}, bf16[128,4096]{1,0:T(8,128)(2,1)}, bf16[128,4096]{1,0:T(8,128)(2,1)}, bf16[128,4096]{1,0:T(8,128)(2,1)}, f32[8,128]{1,0:T(8,128)}) custom-call(s32[3]{0:T(128)} %pad_add_fusion.refs_0_, bf16[1024,2048]{1,0:T(8,128)(2,1)} %get-tuple-element.80.refs_1_.refs_2_, bf16[4096,2048]{1,0:T(8,128)(2,1)} %refs_2_.8, ...), custom_call_target="tpu_custom_call" | custom-call | flops 8589934592 | bytes 30408704 | tf_op jit(solution)/shard_map/own/pallas_call | solution.py:32
  150.0 55.1 %mlp.3 = (bf16[1024,4096]{1,0:T(8,128)(2,1)}, bf16[1024,2048]{1,0:T(8,128)(2,1)}, bf16[1024,2048]{1,0:T(8,128)(2,1)}, f32[8,128]{1,0:T(8,128)}) custom-call(bf16[2,1024,4096]{2,1,0:T(8,128)(2,1)} %refs_5_.9, bf16[2,1024,4096]{2,1,0:T(8,128)(2,1)} %refs_6_.3, f32[2,1024,2]{2,1,0:T(8,128)} %pad_maximum_fusion.2.refs_2_.refs_7_, ...), custom_call_target="tpu_custom_call" | custom-call | flops 34359738368 | bytes 83910656 | tf_op jit(solution)/shard_map/mlp/pallas_call | solution.py:32
  205.1 16.5 %other.5 = (bf16[512,4096]{1,0:T(8,128)(2,1)}, f32[8,128]{1,0:T(8,128)}) custom-call(s32[3]{0:T(128)} %pad_add_fusion.refs_0_, bf16[1024,2048]{1,0:T(8,128)(2,1)} %get-tuple-element.91.refs_1_.refs_3_, bf16[4096,2048]{1,0:T(8,128)(2,1)} %refs_2_.8, f32[8,128]{1,0:T(8,128)} %get-tuple-element.92.refs_3_), custom_call_target="tpu_custom_call" | custom-call | flops 8589934592 | bytes 25165824 | tf_op jit(solution)/shard_map/other/pallas_call | solution.py:32
  223.4 6.2 norm.4
  229.6 24.7 %qkv.3 = (bf16[1024,4096]{1,0:T(8,128)(2,1)}, bf16[1024,1536]{1,0:T(8,128)(2,1)}, f32[8,128]{1,0:T(8,128)}) custom-call(bf16[2,1024,4096]{2,1,0:T(8,128)(2,1)} %refs_5_.11, f32[2,1024,2]{2,1,0:T(8,128)} %pad_maximum_fusion.1.refs_1_.refs_7_, bf16[1,4096]{1,0:T(2,128)(2,1)} %reshape.22.refs_2_.refs_8_, bf16[4096,1536]{1,0:T(8,128)(2,1)} %get-tuple-element.78.refs_3_.refs_4_, ...), custom_call_target="tpu_custom_call" | custom-call | flops 12884901888 | bytes 40919040 | tf_op jit(solution)/shard_map/qkv/pallas_call | solution.py:32
  254.3 17.0 %own.5 = (f32[128,4096]{1,0:T(8,128)}, bf16[128,4096]{1,0:T(8,128)(2,1)}, bf16[128,4096]{1,0:T(8,128)(2,1)}, bf16[128,4096]{1,0:T(8,128)(2,1)}, f32[8,128]{1,0:T(8,128)}) custom-call(s32[3]{0:T(128)} %pad_add_fusion.refs_0_, bf16[1024,2048]{1,0:T(8,128)(2,1)} %get-tuple-element.91.refs_1_.refs_3_, bf16[4096,2048]{1,0:T(8,128)(2,1)} %refs_2_.8, ...), custom_call_target="tpu_custom_call" | custom-call | flops 8589934592 | bytes 30408704 | tf_op jit(solution)/shard_map/own/pallas_call | solution.py:32
  274.8 45.4 %dw2.1 = (bf16[2048,4096]{1,0:T(8,128)(2,1)}, f32[8,128]{1,0:T(8,128)}) custom-call(bf16[1024,2048]{1,0:T(8,128)(2,1)} %get-tuple-element.95.refs_0_, bf16[1024,2048]{1,0:T(8,128)(2,1)} %get-tuple-element.96.refs_1_, bf16[2,1024,4096]{2,1,0:T(8,128)(2,1)} %refs_6_.3, bf16[2,1024,4096]{2,1,0:T(8,128)(2,1)} %refs_6_.3, f32[8,128]{1,0:T(8,128)} %get-tuple-element.100.refs_4_), custom_call_target="tpu_custom_call" | custom-call | flops 34359738368 | bytes 58720256 | tf_op jit(solution)/shard_map/dw2/pallas_call | solution.py:32
  320.3 9.2 %dout.2 = (bf16[1024,512]{1,0:T(8,128)(2,1)}, f32[8,128]{1,0:T(8,128)}) custom-call(bf16[1024,4096]{1,0:T(8,128)(2,1)} %all-gather.5.cloned.1.call-done.refs_0_.refs_2_, bf16[512,4096]{1,0:T(8,128)(2,1)} %bitcast.20, f32[8,128]{1,0:T(8,128)} %get-tuple-element.101.refs_2_), custom_call_target="tpu_custom_call" | custom-call | flops 4294967296 | bytes 13631488 | tf_op jit(solution)/shard_map/dout/pallas_call | solution.py:32
  329.4 22.0 %attn.2 = (bf16[1024,512]{1,0:T(8,128)(2,1)}, bf16[1024,512]{1,0:T(8,128)(2,1)}, bf16[1024,512]{1,0:T(8,128)(2,1)}, bf16[1024,512]{1,0:T(8,128)(2,1)}, f32[8,128]{1,0:T(8,128)}) custom-call(bf16[1024,1536]{1,0:T(8,128)(2,1)} %get-tuple-element.83.refs_0_.refs_1_.refs_2_, bf16[1024,1536]{1,0:T(8,128)(2,1)} %get-tuple-element.83.refs_0_.refs_1_.refs_2_, ...), custom_call_target="tpu_custom_call" | custom-call | flops 12884901888 | bytes 14680064 | tf_op jit(solution)/shard_map/attn/pallas_call | solution.py:32
  351.4 14.1 %other.6 = (bf16[512,4096]{1,0:T(8,128)(2,1)}, f32[8,128]{1,0:T(8,128)}) custom-call(s32[3]{0:T(128)} %pad_add_fusion.refs_0_, bf16[1024,512]{1,0:T(8,128)(2,1)} %get-tuple-element.104.refs_1_.refs_2_, bf16[1024,512]{1,0:T(8,128)(2,1)} %get-tuple-element.105.refs_2_.refs_3_, bf16[1024,512]{1,0:T(8,128)(2,1)} %get-tuple-element.106.refs_3_.refs_4_, ...), custom_call_target="tpu_custom_call" | custom-call | flops 6442450944 | bytes 19922944 | tf_op jit(solution)/shard_map/other/pallas_call | solution.py:32
  367.2 6.2 norm.5
  373.5 7.1 %collective-permute-done.5.refs_5_ = bf16[512,4096]{1,0:T(8,128)(2,1)} collective-permute-done((bf16[512,4096]{1,0:T(8,128)(2,1)}, bf16[512,4096]{1,0:T(8,128)(2,1)}, u32[]{:S(2)}, u32[]{:S(2)}) %collective-permute-start.5) | collective-permute-done | bytes 4194336 | tf_op jit(solution)/shard_map/ppermute | solution.py:281
  380.6 14.9 %own.6 = (f32[128,4096]{1,0:T(8,128)}, bf16[128,4096]{1,0:T(8,128)(2,1)}, bf16[128,4096]{1,0:T(8,128)(2,1)}, bf16[128,4096]{1,0:T(8,128)(2,1)}, f32[8,128]{1,0:T(8,128)}) custom-call(s32[3]{0:T(128)} %pad_add_fusion.refs_0_, bf16[1024,512]{1,0:T(8,128)(2,1)} %get-tuple-element.104.refs_1_.refs_2_, bf16[1024,512]{1,0:T(8,128)(2,1)} %get-tuple-element.105.refs_2_.refs_3_, ...), custom_call_target="tpu_custom_call" | custom-call | flops 6442450944 | bytes 25165824 | tf_op jit(solution)/shard_map/own/pallas_call | solution.py:32
  399.0 47.9 %dw1.1 = (bf16[4096,2048]{1,0:T(8,128)(2,1)}, f32[8,128]{1,0:T(8,128)}) custom-call(bf16[1024,4096]{1,0:T(8,128)(2,1)} %get-tuple-element.121.refs_0_, bf16[1024,4096]{1,0:T(8,128)(2,1)} %get-tuple-element.122.refs_1_, bf16[1024,2048]{1,0:T(8,128)(2,1)} %get-tuple-element.80.refs_1_.refs_2_, bf16[1024,2048]{1,0:T(8,128)(2,1)} %get-tuple-element.91.refs_1_.refs_3_, ...), custom_call_target="tpu_custom_call" | custom-call | flops 34359738368 | bytes 41943040 | tf_op jit(solution)/shard_map/dw1/pallas_call | solution.py:32
  446.9 20.9 %all-gather.7.cloned.1.call-done.refs_0_.refs_3_ = bf16[1024,4096]{1,0:T(8,128)(2,1)} async-done(((bf16[128,4096]{1,0:T(8,128)(2,1)}), bf16[1024,4096]{1,0:T(8,128)(2,1)}) %all-gather.7.cloned.1.call-update) | async-done | bytes 8388624 | tf_op jit(solution)/shard_map/all_gather | solution.py:305
  467.8 9.2 %dout.3 = (bf16[1024,512]{1,0:T(8,128)(2,1)}, f32[8,128]{1,0:T(8,128)}) custom-call(bf16[1024,4096]{1,0:T(8,128)(2,1)} %all-gather.7.cloned.1.call-done.refs_0_.refs_3_, bf16[512,4096]{1,0:T(8,128)(2,1)} %bitcast.21, f32[8,128]{1,0:T(8,128)} %get-tuple-element.124.refs_2_), custom_call_target="tpu_custom_call" | custom-call | flops 4294967296 | bytes 13631488 | tf_op jit(solution)/shard_map/dout/pallas_call | solution.py:32
  476.9 22.0 %attn.3 = (bf16[1024,512]{1,0:T(8,128)(2,1)}, bf16[1024,512]{1,0:T(8,128)(2,1)}, bf16[1024,512]{1,0:T(8,128)(2,1)}, bf16[1024,512]{1,0:T(8,128)(2,1)}, f32[8,128]{1,0:T(8,128)}) custom-call(bf16[1024,1536]{1,0:T(8,128)(2,1)} %get-tuple-element.119.refs_0_.refs_1_.refs_2_, bf16[1024,1536]{1,0:T(8,128)(2,1)} %get-tuple-element.119.refs_0_.refs_1_.refs_2_, ...), custom_call_target="tpu_custom_call" | custom-call | flops 12884901888 | bytes 14680064 | tf_op jit(solution)/shard_map/attn/pallas_call | solution.py:32
  498.9 14.1 %other.7 = (bf16[512,4096]{1,0:T(8,128)(2,1)}, f32[8,128]{1,0:T(8,128)}) custom-call(s32[3]{0:T(128)} %pad_add_fusion.refs_0_, bf16[1024,512]{1,0:T(8,128)(2,1)} %get-tuple-element.127.refs_1_.refs_5_, bf16[1024,512]{1,0:T(8,128)(2,1)} %get-tuple-element.128.refs_2_.refs_6_, bf16[1024,512]{1,0:T(8,128)(2,1)} %get-tuple-element.129.refs_3_.refs_7_, ...), custom_call_target="tpu_custom_call" | custom-call | flops 6442450944 | bytes 19922944 | tf_op jit(solution)/shard_map/other/pallas_call | solution.py:32
  514.8 6.3 norm.6
  521.4 6.9 collective-permute-done.12.refs_5_
  528.2 14.9 %own.7 = (f32[128,4096]{1,0:T(8,128)}, bf16[128,4096]{1,0:T(8,128)(2,1)}, bf16[128,4096]{1,0:T(8,128)(2,1)}, bf16[128,4096]{1,0:T(8,128)(2,1)}, f32[8,128]{1,0:T(8,128)}) custom-call(s32[3]{0:T(128)} %pad_add_fusion.refs_0_, bf16[1024,512]{1,0:T(8,128)(2,1)} %get-tuple-element.127.refs_1_.refs_5_, bf16[1024,512]{1,0:T(8,128)(2,1)} %get-tuple-element.128.refs_2_.refs_6_, ...), custom_call_target="tpu_custom_call" | custom-call | flops 6442450944 | bytes 25165824 | tf_op jit(solution)/shard_map/own/pallas_call | solution.py:32
  546.6 36.0 %dqkvw.1 = (bf16[4096,3,4,128]{3,2,1,0:T(4,128)(2,1)}, f32[8,128]{1,0:T(8,128)}) custom-call(bf16[1024,4096]{1,0:T(8,128)(2,1)} %get-tuple-element.139.refs_0_, bf16[1024,4096]{1,0:T(8,128)(2,1)} %get-tuple-element.140.refs_1_, bf16[1024,512]{1,0:T(8,128)(2,1)} %get-tuple-element.104.refs_1_.refs_2_, bf16[1024,512]{1,0:T(8,128)(2,1)} %get-tuple-element.105.refs_2_.refs_3_, ...), custom_call_target="tpu_custom_call" | custom-call | flops 25769803776 | bytes 35651584 | tf_op jit(solution)/shard_map/dqkvw/pallas_call | solution.py:32
  582.7 7.9 %collective-permute-done.13.refs_2_ = bf16[128,4096]{1,0:T(8,128)(2,1)S(1)} collective-permute-done((bf16[128,4096]{1,0:T(8,128)(2,1)}, bf16[128,4096]{1,0:T(8,128)(2,1)S(1)}, u32[]{:S(2)}, u32[]{:S(2)}) %collective-permute-start.13) | collective-permute-done | bytes 1048608 | tf_op jit(solution)/shard_map/ppermute | solution.py:281
  591.1 22.2 %collective-permute-done.15.refs_4_ = bf16[128,4096]{1,0:T(8,128)(2,1)S(1)} collective-permute-done((bf16[128,4096]{1,0:T(8,128)(2,1)}, bf16[128,4096]{1,0:T(8,128)(2,1)S(1)}, u32[]{:S(2)}, u32[]{:S(2)}) %collective-permute-start.15) | collective-permute-done | bytes 1048608 | tf_op jit(solution)/shard_map/ppermute | solution.py:281
  614.3 6.3 norm.7
  620.6 14.9 %dwo.1 = (bf16[512,4096]{1,0:T(8,128)(2,1)}, f32[8,128]{1,0:T(8,128)}) custom-call(bf16[1024,512]{1,0:T(8,128)(2,1)} %get-tuple-element.145.refs_0_, bf16[1024,512]{1,0:T(8,128)(2,1)} %get-tuple-element.146.refs_1_, bf16[1024,4096]{1,0:T(8,128)(2,1)} %all-gather.5.cloned.1.call-done.refs_0_.refs_2_, ...), custom_call_target="tpu_custom_call" | custom-call | flops 8589934592 | bytes 23068672 | tf_op jit(solution)/shard_map/dwo/pallas_call | solution.py:32
  635.5 33.4 %all-gather.11.cloned.1.call-done = bf16[1024,4096]{1,0:T(8,128)(2,1)} async-done(((bf16[128,4096]{1,0:T(8,128)(2,1)}), bf16[1024,4096]{1,0:T(8,128)(2,1)}) %all-gather.11.cloned.1.call-update) | async-done | bytes 8388624 | tf_op jit(solution)/shard_map/all_gather | solution.py:305
  668.9 13.8 %pad_maximum_fusion = bf16[2,1024,4096]{2,1,0:T(8,128)(2,1)} fusion(bf16[1,1024,4096]{2,1,0:T(8,128)(2,1)} %bitcast.15, bf16[1,1024,4096]{2,1,0:T(8,128)(2,1)} %bitcast.14), kind=kLoop, calls=%fused_computation | loop fusion | flops 8388608 | bytes 33554432 | tf_op jit(solution)/shard_map/stack | solution.py:350
  (78 shorter events, 31.0 us)
Async XLA Ops:
  7.2 313.1 %all-gather.5.cloned.1.call-start = ((), (), s32[]{:S(2)}) async-start(), calls=%async_computation | async-start | bytes 9437184 | tf_op jit(solution)/shard_map/all_gather | solution.py:305
  84.3 17.6 %copy-start.12 = (f32[2,1024]{1,0:T(2,128)S(1)}, f32[2,1024]{1,0:T(2,128)}, u32[]{:S(2)}) copy-start(f32[2,1024]{1,0:T(2,128)} %param.16) | copy-start | bytes 24580
  84.3 17.9 %copy-start.13 = (f32[2,1024]{1,0:T(2,128)S(1)}, f32[2,1024]{1,0:T(2,128)}, u32[]{:S(2)}) copy-start(f32[2,1024]{1,0:T(2,128)} %param.17) | copy-start | bytes 24580
  84.3 18.3 %copy-start.14 = (bf16[4096]{0:T(1024)(128)(2,1)S(1)}, bf16[4096]{0:T(1024)(128)(2,1)}, u32[]{:S(2)}) copy-start(bf16[4096]{0:T(1024)(128)(2,1)} %param.20) | copy-start | bytes 24580
  101.0 28.0 %collective-permute-start = (bf16[512,4096]{1,0:T(8,128)(2,1)}, bf16[512,4096]{1,0:T(8,128)(2,1)}, u32[]{:S(2)}, u32[]{:S(2)}) collective-permute-start(bf16[512,4096]{1,0:T(8,128)(2,1)} %get-tuple-element.84), channel_id=1, source_target_pairs={{0,1},{1,0},{2,3},{3,2},{4,5},{5,4},{6,7},{7,6}} | collective-permute-start | bytes 12582920 | tf_op jit(solution)/shard_map/ppermute | solution.py:281
  146.0 75.7 %collective-permute-start.1 = (bf16[128,4096]{1,0:T(8,128)(2,1)}, bf16[128,4096]{1,0:T(8,128)(2,1)S(1)}, u32[]{:S(2)}, u32[]{:S(2)}) collective-permute-start(bf16[128,4096]{1,0:T(8,128)(2,1)} %get-tuple-element.87), channel_id=1, source_target_pairs={{0,2},{1,3},{2,0},{3,1},{4,6},{5,7},{6,4},{7,5}} | collective-permute-start | bytes 3145736 | tf_op jit(solution)/shard_map/ppermute | solution.py:281
  148.5 73.2 %collective-permute-start.2 = (bf16[128,4096]{1,0:T(8,128)(2,1)}, bf16[128,4096]{1,0:T(8,128)(2,1)S(1)}, u32[]{:S(2)}, u32[]{:S(2)}) collective-permute-start(bf16[128,4096]{1,0:T(8,128)(2,1)} %get-tuple-element.88), channel_id=1, source_target_pairs={{0,4},{1,5},{2,6},{3,7},{4,0},{5,1},{6,2},{7,3}} | collective-permute-start | bytes 3145736 | tf_op jit(solution)/shard_map/ppermute | solution.py:281
  150.0 71.7 %collective-permute-start.3 = (bf16[128,4096]{1,0:T(8,128)(2,1)}, bf16[128,4096]{1,0:T(8,128)(2,1)S(1)}, u32[]{:S(2)}, u32[]{:S(2)}) collective-permute-start(bf16[128,4096]{1,0:T(8,128)(2,1)} %get-tuple-element.89), channel_id=1, source_target_pairs={{0,6},{1,7},{2,4},{3,5},{4,2},{5,3},{6,0},{7,1}} | collective-permute-start | bytes 3145736 | tf_op jit(solution)/shard_map/ppermute | solution.py:281
  221.7 1.4 copy-start.10
  221.7 1.7 copy-start.11
  229.6 238.2 %all-gather.7.cloned.1.call-start = ((), (), s32[]{:S(2)}) async-start(), calls=%async_computation.1 | async-start | bytes 9437184 | tf_op jit(solution)/shard_map/all_gather | solution.py:305
  229.6 24.7 %collective-permute-start.4 = (bf16[512,4096]{1,0:T(8,128)(2,1)}, bf16[512,4096]{1,0:T(8,128)(2,1)}, u32[]{:S(2)}, u32[]{:S(2)}) collective-permute-start(bf16[512,4096]{1,0:T(8,128)(2,1)} %get-tuple-element.97), channel_id=1, source_target_pairs={{0,1},{1,0},{2,3},{3,2},{4,5},{5,4},{6,7},{7,6}} | collective-permute-start | bytes 12582920 | tf_op jit(solution)/shard_map/ppermute | solution.py:281
  271.3 94.2 %collective-permute-start.6 = (bf16[128,4096]{1,0:T(8,128)(2,1)}, bf16[128,4096]{1,0:T(8,128)(2,1)S(1)}, u32[]{:S(2)}, u32[]{:S(2)}) collective-permute-start(bf16[128,4096]{1,0:T(8,128)(2,1)} %get-tuple-element.110), channel_id=1, source_target_pairs={{0,2},{1,3},{2,0},{3,1},{4,6},{5,7},{6,4},{7,5}} | collective-permute-start | bytes 3145736 | tf_op jit(solution)/shard_map/ppermute | solution.py:281
  273.2 92.4 %collective-permute-start.7 = (bf16[128,4096]{1,0:T(8,128)(2,1)}, bf16[128,4096]{1,0:T(8,128)(2,1)S(1)}, u32[]{:S(2)}, u32[]{:S(2)}) collective-permute-start(bf16[128,4096]{1,0:T(8,128)(2,1)} %get-tuple-element.111), channel_id=1, source_target_pairs={{0,4},{1,5},{2,6},{3,7},{4,0},{5,1},{6,2},{7,3}} | collective-permute-start | bytes 3145736 | tf_op jit(solution)/shard_map/ppermute | solution.py:281
  274.7 90.9 %collective-permute-start.8 = (bf16[128,4096]{1,0:T(8,128)(2,1)}, bf16[128,4096]{1,0:T(8,128)(2,1)S(1)}, u32[]{:S(2)}, u32[]{:S(2)}) collective-permute-start(bf16[128,4096]{1,0:T(8,128)(2,1)} %get-tuple-element.112), channel_id=1, source_target_pairs={{0,6},{1,7},{2,4},{3,5},{4,2},{5,3},{6,0},{7,1}} | collective-permute-start | bytes 3145736 | tf_op jit(solution)/shard_map/ppermute | solution.py:281
  365.6 1.4 copy-start.7
  365.6 1.6 copy-start.8
  373.4 262.1 %all-gather.9.cloned.1.call-start = ((), (), s32[]{:S(2)}) async-start(), calls=%async_computation.2 | async-start | bytes 9437184 | tf_op jit(solution)/shard_map/all_gather | solution.py:305
  373.5 7.1 %collective-permute-start.5 = (bf16[512,4096]{1,0:T(8,128)(2,1)}, bf16[512,4096]{1,0:T(8,128)(2,1)}, u32[]{:S(2)}, u32[]{:S(2)}) collective-permute-start(bf16[512,4096]{1,0:T(8,128)(2,1)} %get-tuple-element.108), channel_id=1, source_target_pairs={{0,1},{1,0},{2,3},{3,2},{4,5},{5,4},{6,7},{7,6}} | collective-permute-start | bytes 12582920 | tf_op jit(solution)/shard_map/ppermute | solution.py:281
  395.5 117.5 %collective-permute-start.10 = (bf16[128,4096]{1,0:T(8,128)(2,1)}, bf16[128,4096]{1,0:T(8,128)(2,1)S(1)}, u32[]{:S(2)}, u32[]{:S(2)}) collective-permute-start(bf16[128,4096]{1,0:T(8,128)(2,1)} %get-tuple-element.117), channel_id=1, source_target_pairs={{0,4},{1,5},{2,6},{3,7},{4,0},{5,1},{6,2},{7,3}} | collective-permute-start | bytes 3145736 | tf_op jit(solution)/shard_map/ppermute | solution.py:281
  397.5 115.6 %collective-permute-start.11 = (bf16[128,4096]{1,0:T(8,128)(2,1)}, bf16[128,4096]{1,0:T(8,128)(2,1)S(1)}, u32[]{:S(2)}, u32[]{:S(2)}) collective-permute-start(bf16[128,4096]{1,0:T(8,128)(2,1)} %get-tuple-element.118), channel_id=1, source_target_pairs={{0,6},{1,7},{2,4},{3,5},{4,2},{5,3},{6,0},{7,1}} | collective-permute-start | bytes 3145736 | tf_op jit(solution)/shard_map/ppermute | solution.py:281
  398.9 114.2 %collective-permute-start.9 = (bf16[128,4096]{1,0:T(8,128)(2,1)}, bf16[128,4096]{1,0:T(8,128)(2,1)S(1)}, u32[]{:S(2)}, u32[]{:S(2)}) collective-permute-start(bf16[128,4096]{1,0:T(8,128)(2,1)} %get-tuple-element.116), channel_id=1, source_target_pairs={{0,2},{1,3},{2,0},{3,1},{4,6},{5,7},{6,4},{7,5}} | collective-permute-start | bytes 3145736 | tf_op jit(solution)/shard_map/ppermute | solution.py:281
  513.0 1.0 copy-start
  513.0 1.3 copy-start.1
  513.1 1.7 copy-start.2
  521.0 147.8 %all-gather.11.cloned.1.call-start = ((), (), s32[]{:S(2)}) async-start(), calls=%async_computation.3 | async-start | bytes 9437184 | tf_op jit(solution)/shard_map/all_gather | solution.py:305
  521.1 7.1 %collective-permute-start.12 = (bf16[512,4096]{1,0:T(8,128)(2,1)}, bf16[512,4096]{1,0:T(8,128)(2,1)}, u32[]{:S(2)}, u32[]{:S(2)}) collective-permute-start(bf16[512,4096]{1,0:T(8,128)(2,1)} %get-tuple-element.133), channel_id=1, source_target_pairs={{0,1},{1,0},{2,3},{3,2},{4,5},{5,4},{6,7},{7,6}} | collective-permute-start | bytes 12582920 | tf_op jit(solution)/shard_map/ppermute | solution.py:281
  543.1 47.5 %collective-permute-start.13 = (bf16[128,4096]{1,0:T(8,128)(2,1)}, bf16[128,4096]{1,0:T(8,128)(2,1)S(1)}, u32[]{:S(2)}, u32[]{:S(2)}) collective-permute-start(bf16[128,4096]{1,0:T(8,128)(2,1)} %get-tuple-element.136), channel_id=1, source_target_pairs={{0,2},{1,3},{2,0},{3,1},{4,6},{5,7},{6,4},{7,5}} | collective-permute-start | bytes 3145736 | tf_op jit(solution)/shard_map/ppermute | solution.py:281
  544.8 46.3 %collective-permute-start.14 = (bf16[128,4096]{1,0:T(8,128)(2,1)}, bf16[128,4096]{1,0:T(8,128)(2,1)S(1)}, u32[]{:S(2)}, u32[]{:S(2)}) collective-permute-start(bf16[128,4096]{1,0:T(8,128)(2,1)} %get-tuple-element.137), channel_id=1, source_target_pairs={{0,4},{1,5},{2,6},{3,7},{4,0},{5,1},{6,2},{7,3}} | collective-permute-start | bytes 3145736 | tf_op jit(solution)/shard_map/ppermute | solution.py:281
  545.1 68.2 %collective-permute-start.15 = (bf16[128,4096]{1,0:T(8,128)(2,1)}, bf16[128,4096]{1,0:T(8,128)(2,1)S(1)}, u32[]{:S(2)}, u32[]{:S(2)}) collective-permute-start(bf16[128,4096]{1,0:T(8,128)(2,1)} %get-tuple-element.138), channel_id=1, source_target_pairs={{0,6},{1,7},{2,4},{3,5},{4,2},{5,3},{6,0},{7,1}} | collective-permute-start | bytes 3145736 | tf_op jit(solution)/shard_map/ppermute | solution.py:281
  590.6 22.7 %copy-start.3 = (bf16[128,4096]{1,0:T(8,128)(2,1)}, bf16[128,4096]{1,0:T(8,128)(2,1)S(1)}, u32[]{:S(2)}) copy-start(bf16[128,4096]{1,0:T(8,128)(2,1)S(1)} %collective-permute-done.13.refs_2_) | copy-start | bytes 3145732
  591.1 22.2 %copy-start.4 = (bf16[128,4096]{1,0:T(8,128)(2,1)}, bf16[128,4096]{1,0:T(8,128)(2,1)S(1)}, u32[]{:S(2)}) copy-start(bf16[128,4096]{1,0:T(8,128)(2,1)S(1)} %collective-permute-done.14.refs_3_) | copy-start | bytes 3145732
  (3 other events, 2.9 us)
Sparse Core Ops, SparseCore 0:
  229.7 52.8 all-gather.4
  373.5 94.1 all-gather.6
  521.2 70.3 all-gather.8
  620.7 48.1 all-gather.10

commit v2 on v1

v2 whole, which is shorter than its diff:
```python
import jax
import jax.numpy as jnp
from jax import lax
from jax.sharding import PartitionSpec as P
from jax.experimental import pallas as pl
from jax.experimental.pallas import tpu as pltpu
from functools import partial

GELU_C = 0.7978845608028654
GELU_A = 0.044715
F32 = jnp.float32
BF16 = jnp.bfloat16
BQ = 256
NT = (((1,), (1,)), ((), ()))
TN = (((0,), (0,)), ((), ()))
ANY = pl.BlockSpec(memory_space=pl.ANY)
TOKEN = jax.ShapeDtypeStruct((8, 128), F32)


def mm(a, b, dims=(((1,), (0,)), ((), ()))):
    return lax.dot_general(a, b, dims, preferred_element_type=F32)


def call(body, grid, in_specs, args, out_specs, outs, token, flops, scratch=(), pos=None, name=None, alias=None, cid=None):
    n_in, n_out, n_pos = len(args), len(outs), 0 if pos is None else 1

    def kernel(*refs):
        head, refs = refs[:n_pos], refs[n_pos:]
        body(*head, *refs[:n_in], *refs[n_in + 1:n_in + 1 + n_out], *refs[n_in + 2 + n_out:])

    size = sum(o.size * o.dtype.itemsize for o in outs) + sum(a.size * a.dtype.itemsize for a in args)
    results = pl.pallas_call(
        kernel,
        grid_spec=pltpu.PrefetchScalarGridSpec(
            num_scalar_prefetch=n_pos, grid=grid, in_specs=list(in_specs) + [ANY],
            out_specs=list(out_specs) + [ANY], scratch_shapes=list(scratch)),
        out_shape=list(outs) + [TOKEN],
        compiler_params=pltpu.CompilerParams(vmem_limit_bytes=62 * 1024 * 1024, collective_id=cid, has_side_effects=cid is not None),
        cost_estimate=pl.CostEstimate(flops=int(flops), bytes_accessed=int(size), transcendentals=0),
        input_output_aliases=alias or {},
        name=name,
    )(*([] if pos is None else [pos]), *args, token)
    return results


def sds(shape, dtype=BF16):
    return jax.ShapeDtypeStruct(shape, dtype)


def normed(rows, stats, gain):
    return ((rows.astype(F32) - stats[:, 0:1]) * stats[:, 1:2] * gain.astype(F32)).astype(BF16)


class Split:
    def __init__(self, lhs, w_hbm, outs, wrow, prod, got, w_sem, send_sem, recv_sem):
        self.lhs, self.w_hbm, self.outs = lhs, w_hbm, outs
        self.wrow, self.prod, self.got = wrow, prod, got
        self.w_sem, self.send_sem, self.recv_sem = w_sem, send_sem, recv_sem
        self.wide = wrow.shape[1]
        self.tiles = w_hbm.shape[0] // self.wide
        self.blk = prod.shape[1] // 8
        idx = lax.axis_index('tp')
        self.chip, self.core = lax.div(idx, 2), lax.rem(idx, 2)
        self.partner = 2 * self.chip + 1 - self.core

    def load(self, t):
        return pltpu.make_async_copy(self.w_hbm.at[pl.ds(t * self.wide, self.wide), :], self.wrow.at[t % 2],
                                     self.w_sem.at[t % 2])

    def rows(self, k, core):
        return pl.ds(pl.multiple_of((2 * lax.bitwise_xor(self.chip, k) + core) * self.blk, self.blk), self.blk)

    def send(self, t, k):
        return pltpu.make_async_remote_copy(
            src_ref=self.prod.at[t % 2, self.rows(k, 1 - self.core)], dst_ref=self.got.at[t, k],
            send_sem=self.send_sem.at[t, k], recv_sem=self.recv_sem.at[t, k],
            device_id={'tp': self.partner}, device_id_type=pl.DeviceIdType.MESH)

    def greet(self):
        barrier = pltpu.get_barrier_semaphore()
        pl.semaphore_signal(barrier, inc=1, device_id={'tp': self.partner}, device_id_type=pl.DeviceIdType.MESH)
        pl.semaphore_wait(barrier, 1)

    def tile(self, t):
        @pl.when(t < self.tiles)
        def _():
            self.load(t).wait()

            @pl.when(t >= 2)
            def _():
                for k in range(4):
                    self.send(t - 2, k).wait_send()

            self.prod[t % 2] = mm(self.lhs[...], self.wrow[t % 2], NT).astype(BF16)
            for k in range(4):
                self.send(t, k).start()

            @pl.when(t + 2 < self.tiles)
            def _():
                self.load(t + 2).start()

        @pl.when(t > 0)
        def _():
            for k in range(4):
                self.send(t - 1, k).wait_recv()
                total = self.prod[(t - 1) % 2, self.rows(k, self.core)].astype(F32) + self.got[t - 1, k].astype(F32)
                self.outs[k][...] = total.astype(self.outs[k].dtype)

        @pl.when(t == self.tiles)
        def _():
            for u in range(self.tiles - 2, self.tiles):
                for k in range(4):
                    self.send(u, k).wait_send()

    @staticmethod
    def scratch(seq, depth, hid, wide):
        tiles = hid // wide
        return [pltpu.VMEM((2, wide, depth), BF16), pltpu.VMEM((2, seq, wide), BF16),
                pltpu.VMEM((tiles, 4, seq // 8, wide), BF16), pltpu.SemaphoreType.DMA((2,)),
                pltpu.SemaphoreType.DMA((tiles, 4)), pltpu.SemaphoreType.DMA((tiles, 4))]

    @staticmethod
    def out(seq, hid, wide, first):
        last = hid // wide - 1
        spec = pl.BlockSpec((seq // 8, wide), lambda j: (0, jnp.clip(j - first - 1, 0, last)))
        return [spec] * 4, [sds((seq // 8, hid), F32)] + [sds((seq // 8, hid))] * 3


def gelu_pair(a, b):
    tanh = jnp.tanh(GELU_C * (a + GELU_A * a * a * a))
    slope = (0.5 * (1.0 + tanh)
             + 0.5 * a * (1.0 - tanh * tanh) * GELU_C * (1.0 + 3.0 * GELU_A * a * a))
    return (0.5 * a * (1.0 + tanh)).astype(BF16), (b * slope).astype(BF16)


def mlp_kernel(m, nt, h_ref, dy_ref, st_ref, g_ref, up_ref, down_ref, up_hbm,
               n_hbm, act_ref, dpre_hbm, keep_ref, s1_ref, s2_ref, s3_ref,
               n_v, dy_v, dpre_v, h_sem, dy_sem, out_sem, *split_refs):
    step = pl.program_id(0)
    bn = up_ref.shape[1]
    chunks = h_sem.shape[0]
    part = n_v.shape[0] // chunks
    split = Split(dpre_v, up_hbm, (keep_ref, s1_ref, s2_ref, s3_ref), *split_refs)
    n_out = pltpu.make_async_copy(n_v, n_hbm, out_sem.at[0])
    d_out = pltpu.make_async_copy(dpre_v, dpre_hbm, out_sem.at[1])

    def load(r):
        rows = pl.ds(pl.multiple_of(r * part, part), part)
        return (pltpu.make_async_copy(h_ref.at[m, rows], n_v.at[rows], h_sem.at[r]),
                pltpu.make_async_copy(dy_ref.at[m, rows], dy_v.at[rows], dy_sem.at[r]))

    @pl.when(step == 0)
    def _():
        for r in range(chunks):
            for copy in load(r):
                copy.start()
        split.greet()

        @pl.loop(0, chunks)
        def _(r):
            rows = pl.ds(pl.multiple_of(r * part, part), part)
            h_copy, dy_copy = load(r)
            h_copy.wait()
            n_v[rows, :] = normed(n_v[rows, :], st_ref[0, rows, :], g_ref[...])
            dy_copy.wait()
            act, dpre = gelu_pair(mm(n_v[rows, :], up_ref[...]), mm(dy_v[rows, :], down_ref[...], NT))
            act_ref[rows, :] = act
            dpre_v[rows, pl.ds(0, bn)] = dpre
        n_out.start()

    @pl.when(jnp.logical_and(step > 0, step < nt))
    def _():
        act, dpre = gelu_pair(mm(n_v[...], up_ref[...]), mm(dy_v[...], down_ref[...], NT))
        act_ref[...] = act
        dpre_v[:, pl.ds(pl.multiple_of(step * bn, bn), bn)] = dpre

    @pl.when(step == nt - 2)
    def _():
        split.load(0).start()
        split.load(1).start()

    @pl.when(step == nt)
    def _():
        d_out.start()

    @pl.when(step >= nt)
    def _():
        split.tile(step - nt)

    @pl.when(step == nt + split.tiles)
    def _():
        n_out.wait()
        d_out.wait()


def mlp(m, h1, dy, stats, gain, w_up, w_down, token):
    _, seq, hid = h1.shape
    ffn = w_up.shape[1]
    bn, wide, chunks = 256, 1024, 4
    nt, tiles = ffn // bn, hid // wide
    col = lambda j: jnp.minimum(j, nt - 1)
    sum_specs, sums = Split.out(seq, hid, wide, nt)
    return call(
        partial(mlp_kernel, m, nt), (nt + tiles + 1,),
        [ANY, ANY, pl.BlockSpec((1, seq, 2), lambda j: (m, 0, 0)), pl.BlockSpec((1, hid), lambda j: (0, 0)),
         pl.BlockSpec((hid, bn), lambda j: (0, col(j))), pl.BlockSpec((bn, hid), lambda j: (col(j), 0)), ANY],
        [h1, dy, stats, gain, w_up, w_down, w_up],
        [ANY, pl.BlockSpec((seq, bn), lambda j: (0, col(j))), ANY] + sum_specs,
        [sds((seq, hid)), sds((seq, ffn)), sds((seq, ffn))] + sums, token, 6 * seq * hid * ffn,
        scratch=[pltpu.VMEM((seq, hid), BF16), pltpu.VMEM((seq, hid), BF16), pltpu.VMEM((seq, ffn), BF16),
                 pltpu.SemaphoreType.DMA((chunks,)), pltpu.SemaphoreType.DMA((chunks,)), pltpu.SemaphoreType.DMA((2,)),
                 *Split.scratch(seq, ffn, hid, wide)],
        name='mlp', cid=m)


def qkv_kernel(m, x_ref, st_ref, g_ref, w_ref, n_hbm, out_ref, n_v, x_sem, out_sem):
    step = pl.program_id(0)
    chunks = x_sem.shape[0]
    part = n_v.shape[0] // chunks
    n_out = pltpu.make_async_copy(n_v, n_hbm, out_sem)

    def load(r):
        rows = pl.ds(pl.multiple_of(r * part, part), part)
        return pltpu.make_async_copy(x_ref.at[m, rows], n_v.at[rows], x_sem.at[r])

    @pl.when(step == 0)
    def _():
        for r in range(chunks):
            load(r).start()

        @pl.loop(0, chunks)
        def _(r):
            rows = pl.ds(pl.multiple_of(r * part, part), part)
            load(r).wait()
            n_v[rows, :] = normed(n_v[rows, :], st_ref[0, rows, :], g_ref[...])
            out_ref[rows, :] = mm(n_v[rows, :], w_ref[...]).astype(BF16)
        n_out.start()

    @pl.when(step > 0)
    def _():
        out_ref[...] = mm(n_v[...], w_ref[...]).astype(BF16)

    @pl.when(step == pl.num_programs(0) - 1)
    def _():
        n_out.wait()


def qkv_proj(m, x, stats, gain, w, token):
    _, seq, hid = x.shape
    bn, chunks = 256, 4
    return call(
        partial(qkv_kernel, m), (w.shape[1] // bn,),
        [ANY, pl.BlockSpec((1, seq, 2), lambda j: (m, 0, 0)), pl.BlockSpec((1, hid), lambda j: (0, 0)),
         pl.BlockSpec((hid, bn), lambda j: (0, j))],
        [x, stats, gain, w], [ANY, pl.BlockSpec((seq, bn), lambda j: (0, j))],
        [sds((seq, hid)), sds((seq, w.shape[1]))], token, 2 * seq * hid * w.shape[1],
        scratch=[pltpu.VMEM((seq, hid), BF16), pltpu.SemaphoreType.DMA((chunks,)), pltpu.SemaphoreType.DMA],
        name='qkv')


def norm_kernel(pos_ref, keep_ref, r1_ref, r2_ref, r3_ref, act_ref, res_ref, st_ref, g_ref, out_ref):
    step = 16
    gain = g_ref[...].astype(F32)
    for i in range(keep_ref.shape[0] // step):
        rows = pl.ds(i * step, step)
        total = (keep_ref[rows, :] + r1_ref[rows, :].astype(F32) + r2_ref[rows, :].astype(F32)
                 + r3_ref[rows, :].astype(F32))
        rstd = st_ref[0, rows, 1:2]
        hat = (act_ref[0, rows, :].astype(F32) - st_ref[0, rows, 0:1]) * rstd
        scaled = total * gain
        mean_scaled = jnp.mean(scaled, axis=-1, keepdims=True)
        mean_cross = jnp.mean(scaled * hat, axis=-1, keepdims=True)
        res = (res_ref[0, rows, :] if len(res_ref.shape) == 3 else res_ref[rows, :]).astype(F32)
        out_ref[rows, :] = (res + rstd * (scaled - mean_scaled - hat * mean_cross)).astype(BF16)


def norm_shard(m, keep, got, acts, resid, stats, gain, pos, token):
    blk, hid = keep.shape
    bm = blk
    n = blk // bm
    local = pl.BlockSpec((bm, hid), lambda i, p: (i, 0))
    row = pl.BlockSpec((1, bm, hid), lambda i, p: (m, p[0] * n + i, 0))
    return call(
        norm_kernel, (n,),
        [local] * 4 + [row, row if resid.ndim == 3 else local,
                       pl.BlockSpec((1, bm, 2), lambda i, p: (m, p[0] * n + i, 0)), pl.BlockSpec((1, hid), lambda i, p: (0, 0))],
        [keep, *got, acts, resid, stats, gain], [local], [sds((blk, hid))], token, 20 * blk * hid, pos=pos, name='norm')


def head_backward(scale, q_ref, k_ref, v_ref, do_ref, o_ref, dq_ref, dk_ref, dv_ref, dk_acc, dv_acc):
    seq = do_ref.shape[0]
    k_all, v_all = k_ref[...], v_ref[...]
    k_t, v_t = k_all.T, v_all.T
    nblk = seq // BQ
    for i in reversed(range(nblk)):
        rows = pl.ds(i * BQ, BQ)
        width = (i + 1) * BQ
        q, do = q_ref[rows, :], do_ref[rows, :]
        s_t = mm(k_all[:width], q, NT) * scale
        kpos = lax.broadcasted_iota(jnp.int32, (width, BQ), 0)
        qpos = lax.broadcasted_iota(jnp.int32, (width, BQ), 1) + i * BQ
        s_t = jnp.where(qpos >= kpos, s_t, -1e30)
        top = jnp.max(s_t, axis=0, keepdims=True)
        p_t = jnp.exp(s_t - top)
        p_t = p_t * (1.0 / jnp.sum(p_t, axis=0, keepdims=True))
        p_b = p_t.astype(BF16)
        o_ref[rows, :] = mm(v_t[:, :width], p_b).T.astype(BF16)
        dp_t = mm(v_all[:width], do, NT)
        dot = jnp.sum(p_t * dp_t, axis=0, keepdims=True)
        ds_t = (p_t * (dp_t - dot) * scale).astype(BF16)
        dq_ref[rows, :] = mm(k_t[:, :width], ds_t).T.astype(BF16)
        dv, dk = mm(p_b, do), mm(ds_t, q)
        if i == nblk - 1:
            dv_acc[...] = dv
            dk_acc[...] = dk
        else:
            dv_acc[:width] += dv
            dk_acc[:width] += dk
    dk_ref[...] = dk_acc[...].astype(BF16)
    dv_ref[...] = dv_acc[...].astype(BF16)


def attn_kernel(scale, n, dh_ref, wo_ref, q_ref, k_ref, v_ref, w_hbm,
                o_ref, dq_ref, dk_ref, dv_ref, keep_ref, s1_ref, s2_ref, s3_ref,
                dh_v, do_v, g_v, dk_acc, dv_acc, dh_sem, *split_refs):
    step = pl.program_id(0)
    seq, dim = q_ref.shape
    chunks = dh_sem.shape[0]
    part = seq // chunks
    split = Split(g_v, w_hbm, (keep_ref, s1_ref, s2_ref, s3_ref), *split_refs)

    def load(r):
        rows = pl.ds(pl.multiple_of(r * part, part), part)
        return pltpu.make_async_copy(dh_ref.at[rows], dh_v.at[rows], dh_sem.at[r])

    @pl.when(step == 0)
    def _():
        for r in range(chunks):
            load(r).start()
        split.greet()

        @pl.loop(0, chunks)
        def _(r):
            rows = pl.ds(pl.multiple_of(r * part, part), part)
            load(r).wait()
            grad_o = mm(dh_v[rows, :], wo_ref[...], NT).astype(BF16)
            for h in range(n):
                do_v[h, rows, :] = grad_o[:, h * dim:(h + 1) * dim]
        split.load(0).start()
        split.load(1).start()

    @pl.when(step < n)
    def _():
        head_backward(scale, q_ref, k_ref, v_ref, do_v.at[step], o_ref, dq_ref, dk_ref, dv_ref, dk_acc, dv_acc)
        for c, ref in enumerate((dq_ref, dk_ref, dv_ref)):
            g_v[:, pl.ds(pl.multiple_of((c * n + step) * dim, dim), dim)] = ref[...]

    @pl.when(step >= n)
    def _():
        split.tile(step - n)


def attention(m, dh, w_out, qkv, w_flat, dim, scale, token):
    seq, hid = dh.shape
    width = w_out.shape[0]
    n = width // dim
    wide, chunks = 1024, 4
    head = lambda c: pl.BlockSpec((seq, dim), lambda i: (0, c * n + jnp.minimum(i, n - 1)))
    sum_specs, sums = Split.out(seq, hid, wide, n)
    return call(
        partial(attn_kernel, scale, n), (n + hid // wide + 1,),
        [ANY, pl.BlockSpec((width, hid), lambda i: (0, 0)), head(0), head(1), head(2), ANY],
        [dh, w_out, qkv, qkv, qkv, w_flat],
        [head(0)] * 4 + sum_specs, [sds((seq, width))] * 4 + sums, token,
        24 * n * seq * seq * dim + 8 * seq * hid * width,
        scratch=[pltpu.VMEM((seq, hid), BF16), pltpu.VMEM((n, seq, dim), BF16), pltpu.VMEM((seq, 3 * width), BF16),
                 pltpu.VMEM((seq, dim), F32), pltpu.VMEM((seq, dim), F32), pltpu.SemaphoreType.DMA((chunks,)),
                 *Split.scratch(seq, 3 * width, hid, wide)],
        name='attn', cid=2 + m)


def copy_kernel(src_ref, *refs):
    refs[-1][0] = src_ref[...]


def write_out(m, src, buf, count, token):
    seq, hid = src.shape
    bm = 256
    args, specs, alias = [src], [pl.BlockSpec((bm, hid), lambda i: (i, 0))], None
    if buf is not None:
        args, specs, alias = [src, buf], specs + [ANY], {1: 0}
    return call(copy_kernel, (seq // bm,), specs, args, [pl.BlockSpec((1, bm, hid), lambda i: (m, i, 0))],
                [sds((count, seq, hid))], token, src.size, alias=alias, name='copy')


def grad_kernel(a0_ref, a1_ref, b0_ref, b1_ref, out_ref):
    left = lambda ref: ref[0] if len(ref.shape) == 3 else ref[...]
    acc = mm(left(a0_ref), left(b0_ref), TN) + mm(left(a1_ref), left(b1_ref), TN)
    out_ref[...] = acc.astype(BF16)


def weight_grad(lhs, rhs, token, ba, bb, name):
    def split(v, size, axis):
        if isinstance(v, (list, tuple)):
            spec = pl.BlockSpec((v[0].shape[0], size), lambda i, j: (0, (i, j)[axis]))
            return list(v), [spec] * 2, v[0].shape
        specs = [pl.BlockSpec((1, v.shape[1], size), lambda i, j, m=m: (m, 0, (i, j)[axis])) for m in range(2)]
        return [v, v], specs, v.shape[1:]

    la, ls, (seq, wa) = split(lhs, ba, 0)
    ra, rs, (_, wb) = split(rhs, bb, 1)
    return call(grad_kernel, (wa // ba, wb // bb), ls + rs, la + ra, [pl.BlockSpec((ba, bb), lambda i, j: (i, j))],
                [sds((wa, wb))], token, 4 * seq * wa * wb, name=name)


def qkv_grad_kernel(a0_ref, a1_ref, *refs):
    out_ref = refs[-1]
    rows, _, heads, dim = out_ref.shape
    for c in range(3):
        acc = mm(a0_ref[...], refs[c][...], TN) + mm(a1_ref[...], refs[3 + c][...], TN)
        out_ref[:, c] = acc.reshape(rows, heads, dim).astype(BF16)


def qkv_grad(norms, grads, heads, dim, token):
    seq, hid = norms[0].shape
    ba = 1024
    lhs = pl.BlockSpec((seq, ba), lambda i: (0, i))
    whole = pl.BlockSpec((seq, heads * dim), lambda i: (0, 0))
    return call(qkv_grad_kernel, (hid // ba,), [lhs] * 2 + [whole] * 6, [*norms, *grads[0], *grads[1]],
                [pl.BlockSpec((ba, 3, heads, dim), lambda i: (i, 0, 0, 0))], [sds((hid, 3, heads, dim))], token,
                12 * seq * hid * heads * dim, name='dqkvw')


def flat_kernel(w_ref, out_ref):
    rows, _, heads, dim = w_ref.shape
    for c in range(3):
        out_ref[:, pl.ds(c * heads * dim, heads * dim)] = w_ref[:, c].reshape(rows, heads * dim)


def flat_weight(w, token):
    hid, three, heads, dim = w.shape
    bm = 256
    return call(flat_kernel, (hid // bm,), [pl.BlockSpec((bm, three, heads, dim), lambda i: (i, 0, 0, 0))], [w],
                [pl.BlockSpec((bm, three * heads * dim), lambda i: (i, 0))], [sds((hid, three * heads * dim))], token,
                w.size, name='flat')


def swap(arr, bit):
    return lax.ppermute(arr, 'tp', [(i, i ^ bit) for i in range(8)])


def solution(mesh):
    act_spec = P('dp', None, None)
    stat_spec = P('dp', None)
    in_specs = (act_spec, act_spec, act_spec, stat_spec, stat_spec, stat_spec, stat_spec, P(), P(),
                P(None, 'tp', None, None), P('tp', None, None), P(None, 'tp'), P('tp', None))
    out_specs = (act_spec, P('dp', 'tp', None, None), P(('dp', 'tp'), None, None), P('dp', 'tp'),
                 P(('dp', 'tp'), None))

    def local_backward(x_saved, h1_saved, grad_y, mean_one, rstd_one, mean_two, rstd_two,
                       gain_one, gain_two, w_qkv, w_out, w_up, w_down):
        hid, heads, _, dim = w_qkv.shape
        scale = dim ** -0.5
        idx = lax.axis_index('tp')
        pos = jnp.stack([idx, idx // 2, idx % 2]).astype(jnp.int32)
        stats_one = jnp.stack([mean_one, rstd_one], axis=-1)
        stats_two = jnp.stack([mean_two, rstd_two], axis=-1)
        g1, g2 = gain_one.reshape(1, hid), gain_two.reshape(1, hid)
        w_out = w_out.reshape(heads * dim, hid)
        tok = jnp.zeros((8, 128), F32)

        def gather(shard):
            return lax.all_gather(shard, 'tp', axis=0, tiled=True)

        def exchange(sends):
            return [swap(s, bit) for s, bit in zip(sends, (2, 4, 6))]

        n2, act, dpre, n1, qkv = [0, 0], [0, 0], [0, 0], [0, 0], [0, 0]
        dh_shard, dh, out, grads, dx = [0, 0], [0, 0], [0, 0], [0, 0], [0, 0]

        n2[0], act[0], dpre[0], keep_a, *send, tok = mlp(0, h1_saved, grad_y, stats_two, g2, w_up, w_down, tok)
        got_a = exchange(send)
        w_flat, tok = flat_weight(w_qkv.transpose(0, 2, 1, 3), tok)
        n1[0], qkv[0], tok = qkv_proj(0, x_saved, stats_one, g1, w_flat, tok)
        dh_shard[0], tok = norm_shard(0, keep_a, got_a, h1_saved, grad_y, stats_two, g2, pos, tok)
        dh[0] = gather(dh_shard[0])
        n2[1], act[1], dpre[1], keep_b, *send, tok = mlp(1, h1_saved, grad_y, stats_two, g2, w_up, w_down, tok)
        got_b = exchange(send)
        out[0], *g0, keep_a, s1, s2, s3, tok = attention(0, dh[0], w_out, qkv[0], w_flat, dim, scale, tok)
        got_a = exchange((s1, s2, s3))
        dh_shard[1], tok = norm_shard(1, keep_b, got_b, h1_saved, grad_y, stats_two, g2, pos, tok)
        dh[1] = gather(dh_shard[1])
        n1[1], qkv[1], tok = qkv_proj(1, x_saved, stats_one, g1, w_flat, tok)
        grad_down, tok = weight_grad(act, grad_y, tok, 1024, 1024, 'dw2')
        out[1], *g1s, keep_b, s1, s2, s3, tok = attention(1, dh[1], w_out, qkv[1], w_flat, dim, scale, tok)
        got_b = exchange((s1, s2, s3))
        dx_shard, tok = norm_shard(0, keep_a, got_a, x_saved, dh_shard[0], stats_one, g1, pos, tok)
        dx[0] = gather(dx_shard)
        grad_up, tok = weight_grad(n2, dpre, tok, 1024, 1024, 'dw1')
        dx_shard, tok = norm_shard(1, keep_b, got_b, x_saved, dh_shard[1], stats_one, g1, pos, tok)
        dx[1] = gather(dx_shard)
        grad_qkv_w, tok = qkv_grad(n1, [g0, g1s], heads, dim, tok)
        grad_out_w, tok = weight_grad(out, dh, tok, 512, 1024, 'dwo')
        grad_x, tok = write_out(0, dx[0], None, 2, tok)
        grad_x, tok = write_out(1, dx[1], grad_x, 2, tok)
        return grad_x, grad_qkv_w.transpose(0, 2, 1, 3), grad_out_w.reshape(heads, dim, hid), grad_up, grad_down

    return jax.shard_map(local_backward, mesh=mesh, in_specs=in_specs, out_specs=out_specs, check_vma=False)
```

time: 701 us -> 585 us (0.83)
  Pallas kernels: 532 us -> 475 us
  waiting for transfers between devices: 98.9 us -> 60.9 us
  other arithmetic: 17.1 us -> 3.25 us
    pallas_call x25 -> x17, Pallas kernels: 532 us -> 475 us  [call(): pl.pallas_call(kernel, grid_spec=pltpu.PrefetchScalarGridSpec(num_scalar_...]
    all_gather x4, waiting for transfers between devices: 54.2 us -> 19 us  [gather(): return lax.all_gather(shard, 'tp', axis=0, tiled=True)]
    another operation x1 -> x0, other arithmetic: 13.8 us -> none  [local_backward(): jnp.stack(dx)]
    ppermute x16 -> x12, waiting for transfers between devices: 44.6 us -> 41.8 us  [swap(): return lax.ppermute(arr, 'tp', [(i, i ^ bit) for i in range(8)])]
    ppermute x16 -> x12, starting transfers between devices: 15.7 us -> 14.6 us  [swap(): return lax.ppermute(arr, 'tp', [(i, i ^ bit) for i in range(8)])]
  transfers between devices with their start and end apart: 20 -> 16, of which waited for: 7 -> 3; matrix products, arithmetic and copies ran while one was open for 0% -> 1% of each run, Pallas kernels for 59% -> 65%
where the time goes in v2:
time: 585 us; the launch traced here: 576 us
  Pallas kernels  475 us (81%)
  waiting for transfers between devices  60.9 us (10%)
  starting transfers between devices  14.8 us (3%)
  between operations  14.2 us (2%)
  local copies, waits for them, and re-layouts  7.26 us (1%)
    pallas_call x17, Pallas kernels, call(): pl.pallas_call(kernel, grid_spec=pltpu.PrefetchScalarGridSpec(num_scalar_...  475 us
    ppermute x12, waiting for transfers between devices, swap(): return lax.ppermute(arr, 'tp', [(i, i ^ bit) for i in range(8)])  41.8 us
    all_gather x4, waiting for transfers between devices, gather(): return lax.all_gather(shard, 'tp', axis=0, tiled=True)  19 us
    ppermute x12, starting transfers between devices, swap(): return lax.ppermute(arr, 'tp', [(i, i ^ bit) for i in range(8)])  14.6 us
  transfers between devices with their start and end apart: 16, of which 3 were waited for; matrix products, arithmetic and copies ran while one was open for 1% of the time, Pallas kernels for 65%

profile of v2, /device:TPU:0, one launch (start us, length us, event | category | flops | bytes accessed | tf_op | source)
XLA Modules:
  0.0 575.5 jit_solution(10673956535917392410)
XLA Ops:
  7.2 1.3 reshape.22.refs_3_.refs_8_
  9.6 1.1 copy.38
  10.7 1.3 pad_maximum_fusion.refs_2_.refs_7_
  12.6 72.4 %mlp.2 = (bf16[1024,4096]{1,0:T(8,128)(2,1)}, bf16[1024,2048]{1,0:T(8,128)(2,1)}, bf16[1024,2048]{1,0:T(8,128)(2,1)}, f32[128,4096]{1,0:T(8,128)}, bf16[128,4096...) custom-call(bf16[2,1024,4096]{2,1,0:T(8,128)(2,1)} %refs_5_.9, ...), custom_call_target="tpu_custom_call" | custom-call | flops 51539607552 | bytes 105930752 | tf_op jit(solution)/shard_map/mlp/pallas_call | solution.py:32
  84.9 2.6 collective-permute-start
  87.5 1.5 collective-permute-start.1
  90.4 1.3 pad_maximum_fusion.1.refs_1_.refs_7_
  91.7 16.5 %flat.1 = (bf16[4096,1536]{1,0:T(8,128)(2,1)}, f32[8,128]{1,0:T(8,128)}) custom-call(bf16[4096,3,4,128]{3,2,1,0:T(4,128)(2,1)} %bitcast.11, f32[8,128]{1,0:T(8,128)} %get-tuple-element.70.refs_1_), custom_call_target="tpu_custom_call" | custom-call | flops 6291456 | bytes 25165824 | tf_op jit(solution)/shard_map/flat/pallas_call | solution.py:32
  108.9 21.0 %qkv.2 = (bf16[1024,4096]{1,0:T(8,128)(2,1)}, bf16[1024,1536]{1,0:T(8,128)(2,1)}, f32[8,128]{1,0:T(8,128)}) custom-call(bf16[2,1024,4096]{2,1,0:T(8,128)(2,1)} %refs_5_.11, f32[2,1024,2]{2,1,0:T(8,128)} %pad_maximum_fusion.1.refs_1_.refs_7_, bf16[1,4096]{1,0:T(2,128)(2,1)} %reshape.23.refs_2_.refs_8_, bf16[4096,1536]{1,0:T(8,128)(2,1)} %get-tuple-element.71.refs_3_.refs_5_, ...), custom_call_target="tpu_custom_call" | custom-call | flops 12884901888 | bytes 40919040 | tf_op jit(solution)/shard_map/qkv/pallas_call | solution.py:32
  129.9 5.3 collective-permute-done.1.refs_3_
  135.2 6.5 %norm.4 = (bf16[128,4096]{1,0:T(8,128)(2,1)}, f32[8,128]{1,0:T(8,128)}) custom-call(s32[3]{0:T(128)} %pad_add_fusion.refs_0_, f32[128,4096]{1,0:T(8,128)} %get-tuple-element.66.refs_1_, bf16[128,4096]{1,0:T(8,128)(2,1)} %copy-done.2, bf16[128,4096]{1,0:T(8,128)(2,1)} %collective-permute-done.1.refs_3_, bf16[128,4096]{1,0:T(8,128)(2,1)} %collective-permute-done.2.refs_4_, ...), custom_call_target="tpu_custom_call" | custom-call | flops 10485760 | bytes 39870464 | tf_op jit(solution)/shard_map/norm/pallas_call | solution.py:32
  141.8 71.6 %mlp.3 = (bf16[1024,4096]{1,0:T(8,128)(2,1)}, bf16[1024,2048]{1,0:T(8,128)(2,1)}, bf16[1024,2048]{1,0:T(8,128)(2,1)}, f32[128,4096]{1,0:T(8,128)}, bf16[128,4096...) custom-call(bf16[2,1024,4096]{2,1,0:T(8,128)(2,1)} %refs_5_.9, ...), custom_call_target="tpu_custom_call" | custom-call | flops 51539607552 | bytes 105930752 | tf_op jit(solution)/shard_map/mlp/pallas_call | solution.py:32
  213.4 1.5 collective-permute-start.3
  215.5 1.4 collective-permute-start.5
  216.9 49.5 %attn.2 = (bf16[1024,512]{1,0:T(8,128)(2,1)}, bf16[1024,512]{1,0:T(8,128)(2,1)}, bf16[1024,512]{1,0:T(8,128)(2,1)}, bf16[1024,512]{1,0:T(8,128)(2,1)}, f32[128,4...) custom-call(bf16[1024,4096]{1,0:T(8,128)(2,1)} %all-gather.5.cloned., ...), custom_call_target="tpu_custom_call" | custom-call | flops 30064771072 | bytes 44040192 | tf_op jit(solution)/shard_map/attn/pallas_call | solution.py:32
  267.4 6.5 %norm.5 = (bf16[128,4096]{1,0:T(8,128)(2,1)}, f32[8,128]{1,0:T(8,128)}) custom-call(s32[3]{0:T(128)} %pad_add_fusion.refs_0_, f32[128,4096]{1,0:T(8,128)} %get-tuple-element.75.refs_1_, bf16[128,4096]{1,0:T(8,128)(2,1)} %copy-done.3, bf16[128,4096]{1,0:T(8,128)(2,1)} %collective-permute-done.4.refs_3_, bf16[128,4096]{1,0:T(8,128)(2,1)} %collective-permute-done.5.refs_4_, ...), custom_call_target="tpu_custom_call" | custom-call | flops 10485760 | bytes 39870464 | tf_op jit(solution)/shard_map/norm/pallas_call | solution.py:32
  273.9 1.5 collective-permute-start.9
  276.1 1.4 collective-permute-start.11
  277.5 20.9 %qkv.3 = (bf16[1024,4096]{1,0:T(8,128)(2,1)}, bf16[1024,1536]{1,0:T(8,128)(2,1)}, f32[8,128]{1,0:T(8,128)}) custom-call(bf16[2,1024,4096]{2,1,0:T(8,128)(2,1)} %refs_5_.11, f32[2,1024,2]{2,1,0:T(8,128)} %pad_maximum_fusion.1.refs_1_.refs_7_, bf16[1,4096]{1,0:T(2,128)(2,1)} %reshape.23.refs_2_.refs_8_, bf16[4096,1536]{1,0:T(8,128)(2,1)} %get-tuple-element.71.refs_3_.refs_5_, ...), custom_call_target="tpu_custom_call" | custom-call | flops 12884901888 | bytes 40919040 | tf_op jit(solution)/shard_map/qkv/pallas_call | solution.py:32
  298.3 41.4 %dw2.1 = (bf16[2048,4096]{1,0:T(8,128)(2,1)}, f32[8,128]{1,0:T(8,128)}) custom-call(bf16[1024,2048]{1,0:T(8,128)(2,1)} %get-tuple-element.86.refs_0_, bf16[1024,2048]{1,0:T(8,128)(2,1)} %get-tuple-element.87.refs_1_, bf16[2,1024,4096]{2,1,0:T(8,128)(2,1)} %refs_3_.1, bf16[2,1024,4096]{2,1,0:T(8,128)(2,1)} %refs_3_.1, f32[8,128]{1,0:T(8,128)} %get-tuple-element.88.refs_4_), custom_call_target="tpu_custom_call" | custom-call | flops 34359738368 | bytes 58720256 | tf_op jit(solution)/shard_map/dw2/pallas_call | solution.py:32
  339.7 19.0 %all-gather.7.cloned.1.call-done.refs_0_.refs_3_ = bf16[1024,4096]{1,0:T(8,128)(2,1)} async-done(((bf16[128,4096]{1,0:T(8,128)(2,1)}), bf16[1024,4096]{1,0:T(8,128)(2,1)}) %all-gather.7.cloned.1.call-update) | async-done | bytes 8388624 | tf_op jit(solution)/shard_map/all_gather | solution.py:473
  358.7 49.3 %attn.3 = (bf16[1024,512]{1,0:T(8,128)(2,1)}, bf16[1024,512]{1,0:T(8,128)(2,1)}, bf16[1024,512]{1,0:T(8,128)(2,1)}, bf16[1024,512]{1,0:T(8,128)(2,1)}, f32[128,4...) custom-call(bf16[1024,4096]{1,0:T(8,128)(2,1)} %all-gather.7.cloned., ...), custom_call_target="tpu_custom_call" | custom-call | flops 30064771072 | bytes 44040192 | tf_op jit(solution)/shard_map/attn/pallas_call | solution.py:32
  409.0 6.5 %norm.6 = (bf16[128,4096]{1,0:T(8,128)(2,1)}, f32[8,128]{1,0:T(8,128)}) custom-call(s32[3]{0:T(128)} %pad_add_fusion.refs_0_, f32[128,4096]{1,0:T(8,128)} %get-tuple-element.98.refs_1_, bf16[128,4096]{1,0:T(8,128)(2,1)} %copy-done, bf16[128,4096]{1,0:T(8,128)(2,1)} %collective-permute-done.10.refs_3_, bf16[128,4096]{1,0:T(8,128)(2,1)} %collective-permute-done.11.refs_4_, ...), custom_call_target="tpu_custom_call" | custom-call | flops 10485760 | bytes 24141824 | tf_op jit(solution)/shard_map/norm/pallas_call | solution.py:32
  416.1 1.5 collective-permute-start.7
  417.6 1.4 collective-permute-start.8
  419.0 41.6 %dw1.1 = (bf16[4096,2048]{1,0:T(8,128)(2,1)}, f32[8,128]{1,0:T(8,128)}) custom-call(bf16[1024,4096]{1,0:T(8,128)(2,1)} %get-tuple-element.94.refs_0_, bf16[1024,4096]{1,0:T(8,128)(2,1)} %get-tuple-element.95.refs_1_, bf16[1024,2048]{1,0:T(8,128)(2,1)} %get-tuple-element.96.refs_2_, bf16[1024,2048]{1,0:T(8,128)(2,1)} %get-tuple-element.97.refs_3_, ...), custom_call_target="tpu_custom_call" | custom-call | flops 34359738368 | bytes 41943040 | tf_op jit(solution)/shard_map/dw1/pallas_call | solution.py:32
  460.6 36.5 %collective-permute-done.8.refs_4_ = bf16[128,4096]{1,0:T(8,128)(2,1)} collective-permute-done((bf16[128,4096]{1,0:T(8,128)(2,1)}, bf16[128,4096]{1,0:T(8,128)(2,1)}, u32[]{:S(2)}, u32[]{:S(2)}) %collective-permute-start.8) | collective-permute-done | bytes 1048608 | tf_op jit(solution)/shard_map/ppermute | solution.py:449
  497.1 6.5 %norm.7 = (bf16[128,4096]{1,0:T(8,128)(2,1)}, f32[8,128]{1,0:T(8,128)}) custom-call(s32[3]{0:T(128)} %pad_add_fusion.refs_0_, f32[128,4096]{1,0:T(8,128)} %get-tuple-element.90.refs_1_, bf16[128,4096]{1,0:T(8,128)(2,1)} %copy-done.1, bf16[128,4096]{1,0:T(8,128)(2,1)} %collective-permute-done.7.refs_3_, bf16[128,4096]{1,0:T(8,128)(2,1)} %collective-permute-done.8.refs_4_, ...), custom_call_target="tpu_custom_call" | custom-call | flops 10485760 | bytes 24141824 | tf_op jit(solution)/shard_map/norm/pallas_call | solution.py:32
  503.6 37.3 %dqkvw.1 = (bf16[4096,3,4,128]{3,2,1,0:T(4,128)(2,1)}, f32[8,128]{1,0:T(8,128)}) custom-call(bf16[1024,4096]{1,0:T(8,128)(2,1)} %get-tuple-element.109.refs_0_, bf16[1024,4096]{1,0:T(8,128)(2,1)} %get-tuple-element.110.refs_1_, bf16[1024,512]{1,0:T(8,128)(2,1)} %get-tuple-element.111.refs_2_, bf16[1024,512]{1,0:T(8,128)(2,1)} %get-tuple-element.112.refs_3_, ...), custom_call_target="tpu_custom_call" | custom-call | flops 25769803776 | bytes 35651584 | tf_op jit(solution)/shard_map/dqkvw/pallas_call | solution.py:32
  541.0 13.6 %dwo.1 = (bf16[512,4096]{1,0:T(8,128)(2,1)}, f32[8,128]{1,0:T(8,128)}) custom-call(bf16[1024,512]{1,0:T(8,128)(2,1)} %get-tuple-element.107.refs_0_, bf16[1024,512]{1,0:T(8,128)(2,1)} %get-tuple-element.108.refs_1_, bf16[1024,4096]{1,0:T(8,128)(2,1)} %all-gather.5.cloned.1.call-done.refs_0_.refs_2_, ...), custom_call_target="tpu_custom_call" | custom-call | flops 8589934592 | bytes 23068672 | tf_op jit(solution)/shard_map/dwo/pallas_call | solution.py:32
  554.5 7.1 %copy.42 = (bf16[2,1024,4096]{2,1,0:T(8,128)(2,1)}, f32[8,128]{1,0:T(8,128)}) custom-call(bf16[1024,4096]{1,0:T(8,128)(2,1)} %all-gather.11.cloned.1.call-done.refs_0_, f32[8,128]{1,0:T(8,128)} %get-tuple-element.119.refs_1_), custom_call_target="tpu_custom_call" | custom-call | flops 4194304 | bytes 25165824 | tf_op jit(solution)/shard_map/copy/pallas_call | solution.py:32
  561.7 7.1 %copy.43 = (bf16[2,1024,4096]{2,1,0:T(8,128)(2,1)}, f32[8,128]{1,0:T(8,128)}) custom-call(bf16[1024,4096]{1,0:T(8,128)(2,1)} %all-gather.9.cloned.1.call-done.refs_0_, bf16[2,1024,4096]{2,1,0:T(8,128)(2,1)} %get-tuple-element.120.refs_1_, f32[8,128]{1,0:T(8,128)} %get-tuple-element.121.refs_2_), custom_call_target="tpu_custom_call", output_to_operand_aliasing={{0}: (1, {})} | custom-call | flops 4194304 | bytes 41943040 | tf_op jit(solution)/shard_map/copy/pallas_call | solution.py:32
  (45 shorter events, 7.7 us)
Async XLA Ops:
  7.2 209.8 %all-gather.5.cloned.1.call-start = ((), (), s32[]{:S(2)}) async-start(), calls=%async_computation | async-start | bytes 9437184 | tf_op jit(solution)/shard_map/all_gather | solution.py:473
  12.6 76.5 %copy-start.6 = (bf16[4096]{0:T(1024)(128)(2,1)S(1)}, bf16[4096]{0:T(1024)(128)(2,1)}, u32[]{:S(2)}) copy-start(bf16[4096]{0:T(1024)(128)(2,1)} %param.20) | copy-start | bytes 24580
  12.6 77.1 %copy-start.4 = (f32[2,1024]{1,0:T(2,128)S(1)}, f32[2,1024]{1,0:T(2,128)}, u32[]{:S(2)}) copy-start(f32[2,1024]{1,0:T(2,128)} %param.16) | copy-start | bytes 24580
  12.6 77.5 %copy-start.5 = (f32[2,1024]{1,0:T(2,128)S(1)}, f32[2,1024]{1,0:T(2,128)}, u32[]{:S(2)}) copy-start(f32[2,1024]{1,0:T(2,128)} %param.17) | copy-start | bytes 24580
  84.9 45.0 %collective-permute-start = (bf16[128,4096]{1,0:T(8,128)(2,1)}, bf16[128,4096]{1,0:T(8,128)(2,1)S(1)}, u32[]{:S(2)}, u32[]{:S(2)}) collective-permute-start(bf16[128,4096]{1,0:T(8,128)(2,1)} %get-tuple-element.67), channel_id=1, source_target_pairs={{0,2},{1,3},{2,0},{3,1},{4,6},{5,7},{6,4},{7,5}} | collective-permute-start | bytes 3145736 | tf_op jit(solution)/shard_map/ppermute | solution.py:449
  87.5 47.7 %collective-permute-start.1 = (bf16[128,4096]{1,0:T(8,128)(2,1)}, bf16[128,4096]{1,0:T(8,128)(2,1)}, u32[]{:S(2)}, u32[]{:S(2)}) collective-permute-start(bf16[128,4096]{1,0:T(8,128)(2,1)} %get-tuple-element.68), channel_id=1, source_target_pairs={{0,4},{1,5},{2,6},{3,7},{4,0},{5,1},{6,2},{7,3}} | collective-permute-start | bytes 3145736 | tf_op jit(solution)/shard_map/ppermute | solution.py:449
  89.0 46.2 %collective-permute-start.2 = (bf16[128,4096]{1,0:T(8,128)(2,1)}, bf16[128,4096]{1,0:T(8,128)(2,1)}, u32[]{:S(2)}, u32[]{:S(2)}) collective-permute-start(bf16[128,4096]{1,0:T(8,128)(2,1)} %get-tuple-element.69), channel_id=1, source_target_pairs={{0,6},{1,7},{2,4},{3,5},{4,2},{5,3},{6,0},{7,1}} | collective-permute-start | bytes 3145736 | tf_op jit(solution)/shard_map/ppermute | solution.py:449
  129.9 5.3 copy-start.2
  141.8 216.9 %all-gather.7.cloned.1.call-start = ((), (), s32[]{:S(2)}) async-start(), calls=%async_computation.1 | async-start | bytes 9437184 | tf_op jit(solution)/shard_map/all_gather | solution.py:473
  213.4 53.0 %collective-permute-start.3 = (bf16[128,4096]{1,0:T(8,128)(2,1)}, bf16[128,4096]{1,0:T(8,128)(2,1)S(1)}, u32[]{:S(2)}, u32[]{:S(2)}) collective-permute-start(bf16[128,4096]{1,0:T(8,128)(2,1)} %get-tuple-element.76), channel_id=1, source_target_pairs={{0,2},{1,3},{2,0},{3,1},{4,6},{5,7},{6,4},{7,5}} | collective-permute-start | bytes 3145736 | tf_op jit(solution)/shard_map/ppermute | solution.py:449
  214.9 51.5 %collective-permute-start.4 = (bf16[128,4096]{1,0:T(8,128)(2,1)}, bf16[128,4096]{1,0:T(8,128)(2,1)}, u32[]{:S(2)}, u32[]{:S(2)}) collective-permute-start(bf16[128,4096]{1,0:T(8,128)(2,1)} %get-tuple-element.77), channel_id=1, source_target_pairs={{0,4},{1,5},{2,6},{3,7},{4,0},{5,1},{6,2},{7,3}} | collective-permute-start | bytes 3145736 | tf_op jit(solution)/shard_map/ppermute | solution.py:449
  215.5 50.9 %collective-permute-start.5 = (bf16[128,4096]{1,0:T(8,128)(2,1)}, bf16[128,4096]{1,0:T(8,128)(2,1)}, u32[]{:S(2)}, u32[]{:S(2)}) collective-permute-start(bf16[128,4096]{1,0:T(8,128)(2,1)} %get-tuple-element.78), channel_id=1, source_target_pairs={{0,6},{1,7},{2,4},{3,5},{4,2},{5,3},{6,0},{7,1}} | collective-permute-start | bytes 3145736 | tf_op jit(solution)/shard_map/ppermute | solution.py:449
  266.4 1.0 copy-start.3
  273.9 280.6 %all-gather.11.cloned.1.call-start = ((), (), s32[]{:S(2)}) async-start(), calls=%async_computation.3 | async-start | bytes 9437184 | tf_op jit(solution)/shard_map/all_gather | solution.py:473
  273.9 134.0 %collective-permute-start.9 = (bf16[128,4096]{1,0:T(8,128)(2,1)}, bf16[128,4096]{1,0:T(8,128)(2,1)S(1)}, u32[]{:S(2)}, u32[]{:S(2)}) collective-permute-start(bf16[128,4096]{1,0:T(8,128)(2,1)} %get-tuple-element.99), channel_id=1, source_target_pairs={{0,2},{1,3},{2,0},{3,1},{4,6},{5,7},{6,4},{7,5}} | collective-permute-start | bytes 3145736 | tf_op jit(solution)/shard_map/ppermute | solution.py:449
  275.4 132.6 %collective-permute-start.10 = (bf16[128,4096]{1,0:T(8,128)(2,1)}, bf16[128,4096]{1,0:T(8,128)(2,1)}, u32[]{:S(2)}, u32[]{:S(2)}) collective-permute-start(bf16[128,4096]{1,0:T(8,128)(2,1)} %get-tuple-element.100), channel_id=1, source_target_pairs={{0,4},{1,5},{2,6},{3,7},{4,0},{5,1},{6,2},{7,3}} | collective-permute-start | bytes 3145736 | tf_op jit(solution)/shard_map/ppermute | solution.py:449
  276.1 132.0 %collective-permute-start.11 = (bf16[128,4096]{1,0:T(8,128)(2,1)}, bf16[128,4096]{1,0:T(8,128)(2,1)}, u32[]{:S(2)}, u32[]{:S(2)}) collective-permute-start(bf16[128,4096]{1,0:T(8,128)(2,1)} %get-tuple-element.101), channel_id=1, source_target_pairs={{0,6},{1,7},{2,4},{3,5},{4,2},{5,3},{6,0},{7,1}} | collective-permute-start | bytes 3145736 | tf_op jit(solution)/shard_map/ppermute | solution.py:449
  408.0 1.0 copy-start
  415.5 146.2 %all-gather.9.cloned.1.call-start = ((), (), s32[]{:S(2)}) async-start(), calls=%async_computation.2 | async-start | bytes 9437184 | tf_op jit(solution)/shard_map/all_gather | solution.py:473
  415.5 45.1 %collective-permute-start.6 = (bf16[128,4096]{1,0:T(8,128)(2,1)}, bf16[128,4096]{1,0:T(8,128)(2,1)S(1)}, u32[]{:S(2)}, u32[]{:S(2)}) collective-permute-start(bf16[128,4096]{1,0:T(8,128)(2,1)} %get-tuple-element.91), channel_id=1, source_target_pairs={{0,2},{1,3},{2,0},{3,1},{4,6},{5,7},{6,4},{7,5}} | collective-permute-start | bytes 3145736 | tf_op jit(solution)/shard_map/ppermute | solution.py:449
  416.1 44.5 %collective-permute-start.7 = (bf16[128,4096]{1,0:T(8,128)(2,1)}, bf16[128,4096]{1,0:T(8,128)(2,1)}, u32[]{:S(2)}, u32[]{:S(2)}) collective-permute-start(bf16[128,4096]{1,0:T(8,128)(2,1)} %get-tuple-element.92), channel_id=1, source_target_pairs={{0,4},{1,5},{2,6},{3,7},{4,0},{5,1},{6,2},{7,3}} | collective-permute-start | bytes 3145736 | tf_op jit(solution)/shard_map/ppermute | solution.py:449
  417.6 79.5 %collective-permute-start.8 = (bf16[128,4096]{1,0:T(8,128)(2,1)}, bf16[128,4096]{1,0:T(8,128)(2,1)}, u32[]{:S(2)}, u32[]{:S(2)}) collective-permute-start(bf16[128,4096]{1,0:T(8,128)(2,1)} %get-tuple-element.93), channel_id=1, source_target_pairs={{0,6},{1,7},{2,4},{3,5},{4,2},{5,3},{6,0},{7,1}} | collective-permute-start | bytes 3145736 | tf_op jit(solution)/shard_map/ppermute | solution.py:449
  460.6 36.5 %copy-start.1 = (bf16[128,4096]{1,0:T(8,128)(2,1)}, bf16[128,4096]{1,0:T(8,128)(2,1)S(1)}, u32[]{:S(2)}) copy-start(bf16[128,4096]{1,0:T(8,128)(2,1)S(1)} %collective-permute-done.6.refs_2_) | copy-start | bytes 3145732
Sparse Core Ops, SparseCore 0:
  141.9 48.3 all-gather.4
  274.0 84.6 all-gather.6
  415.6 83.4 all-gather.10
  503.7 48.3 all-gather.8

commit v3 on v2

--- a/solution.py
+++ b/solution.py
@@ -43,12 +43,20 @@
     return results
 
 
+def whole(arr):
+    return pl.BlockSpec(arr.shape, lambda *ids: (0,) * arr.ndim)
+
+
 def sds(shape, dtype=BF16):
     return jax.ShapeDtypeStruct(shape, dtype)
 
 
-def normed(rows, stats, gain):
-    return ((rows.astype(F32) - stats[:, 0:1]) * stats[:, 1:2] * gain.astype(F32)).astype(BF16)
+def column(row):
+    return jnp.broadcast_to(row, (8, row.shape[1])).T[:, 0:1]
+
+
+def normed(rows, mean, rstd, gain):
+    return ((rows.astype(F32) - column(mean)) * column(rstd) * gain.astype(F32)).astype(BF16)
 
 
 class Split:
@@ -133,9 +141,9 @@
     return (0.5 * a * (1.0 + tanh)).astype(BF16), (b * slope).astype(BF16)
 
 
-def mlp_kernel(m, nt, h_ref, dy_ref, st_ref, g_ref, up_ref, down_ref, up_hbm,
+def mlp_kernel(m, nt, h_ref, dy_ref, mu_ref, rs_ref, g_ref, up_ref, down_ref, up_hbm,
                n_hbm, act_ref, dpre_hbm, keep_ref, s1_ref, s2_ref, s3_ref,
-               n_v, dy_v, dpre_v, h_sem, dy_sem, out_sem, *split_refs):
+               n_v, dy_v, dpre_v, a_v, b_v, h_sem, dy_sem, out_sem, *split_refs):
     step = pl.program_id(0)
     bn = up_ref.shape[1]
     chunks = h_sem.shape[0]
@@ -161,18 +169,23 @@
             rows = pl.ds(pl.multiple_of(r * part, part), part)
             h_copy, dy_copy = load(r)
             h_copy.wait()
-            n_v[rows, :] = normed(n_v[rows, :], st_ref[0, rows, :], g_ref[...])
+            n_v[rows, :] = normed(n_v[rows, :], mu_ref[m:m + 1, rows], rs_ref[m:m + 1, rows], g_ref[...])
             dy_copy.wait()
-            act, dpre = gelu_pair(mm(n_v[rows, :], up_ref[...]), mm(dy_v[rows, :], down_ref[...], NT))
-            act_ref[rows, :] = act
-            dpre_v[rows, pl.ds(0, bn)] = dpre
+            a_v[rows, :] = mm(n_v[rows, :], up_ref[...])
+            b_v[rows, :] = mm(dy_v[rows, :], down_ref[...], NT)
+
         n_out.start()
 
+    def finish():
+        act, dpre = gelu_pair(a_v[...], b_v[...])
+        act_ref[...] = act
+        dpre_v[:, pl.ds(pl.multiple_of((step - 1) * bn, bn), bn)] = dpre
+
     @pl.when(jnp.logical_and(step > 0, step < nt))
     def _():
-        act, dpre = gelu_pair(mm(n_v[...], up_ref[...]), mm(dy_v[...], down_ref[...], NT))
-        act_ref[...] = act
-        dpre_v[:, pl.ds(pl.multiple_of(step * bn, bn), bn)] = dpre
+        finish()
+        a_v[...] = mm(n_v[...], up_ref[...])
+        b_v[...] = mm(dy_v[...], down_ref[...], NT)
 
     @pl.when(step == nt - 2)
     def _():
@@ -181,6 +194,7 @@
 
     @pl.when(step == nt)
     def _():
+        finish()
         d_out.start()
 
     @pl.when(step >= nt)
@@ -202,18 +216,19 @@
     sum_specs, sums = Split.out(seq, hid, wide, nt)
     return call(
         partial(mlp_kernel, m, nt), (nt + tiles + 1,),
-        [ANY, ANY, pl.BlockSpec((1, seq, 2), lambda j: (m, 0, 0)), pl.BlockSpec((1, hid), lambda j: (0, 0)),
+        [ANY, ANY, whole(stats[0]), whole(stats[1]), whole(gain),
          pl.BlockSpec((hid, bn), lambda j: (0, col(j))), pl.BlockSpec((bn, hid), lambda j: (col(j), 0)), ANY],
-        [h1, dy, stats, gain, w_up, w_down, w_up],
-        [ANY, pl.BlockSpec((seq, bn), lambda j: (0, col(j))), ANY] + sum_specs,
+        [h1, dy, *stats, gain, w_up, w_down, w_up],
+        [ANY, pl.BlockSpec((seq, bn), lambda j: (0, jnp.clip(j - 1, 0, nt - 1))), ANY] + sum_specs,
         [sds((seq, hid)), sds((seq, ffn)), sds((seq, ffn))] + sums, token, 6 * seq * hid * ffn,
         scratch=[pltpu.VMEM((seq, hid), BF16), pltpu.VMEM((seq, hid), BF16), pltpu.VMEM((seq, ffn), BF16),
+                 pltpu.VMEM((seq, bn), F32), pltpu.VMEM((seq, bn), F32),
                  pltpu.SemaphoreType.DMA((chunks,)), pltpu.SemaphoreType.DMA((chunks,)), pltpu.SemaphoreType.DMA((2,)),
                  *Split.scratch(seq, ffn, hid, wide)],
         name='mlp', cid=m)
 
 
-def qkv_kernel(m, x_ref, st_ref, g_ref, w_ref, n_hbm, out_ref, n_v, x_sem, out_sem):
+def qkv_kernel(m, x_ref, mu_ref, rs_ref, g_ref, w_ref, n_hbm, out_ref, n_v, x_sem, out_sem):
     step = pl.program_id(0)
     chunks = x_sem.shape[0]
     part = n_v.shape[0] // chunks
@@ -232,7 +247,7 @@
         def _(r):
             rows = pl.ds(pl.multiple_of(r * part, part), part)
             load(r).wait()
-            n_v[rows, :] = normed(n_v[rows, :], st_ref[0, rows, :], g_ref[...])
+            n_v[rows, :] = normed(n_v[rows, :], mu_ref[m:m + 1, rows], rs_ref[m:m + 1, rows], g_ref[...])
             out_ref[rows, :] = mm(n_v[rows, :], w_ref[...]).astype(BF16)
         n_out.start()
 
@@ -250,41 +265,56 @@
     bn, chunks = 256, 4
     return call(
         partial(qkv_kernel, m), (w.shape[1] // bn,),
-        [ANY, pl.BlockSpec((1, seq, 2), lambda j: (m, 0, 0)), pl.BlockSpec((1, hid), lambda j: (0, 0)),
+        [ANY, whole(stats[0]), whole(stats[1]), whole(gain),
          pl.BlockSpec((hid, bn), lambda j: (0, j))],
-        [x, stats, gain, w], [ANY, pl.BlockSpec((seq, bn), lambda j: (0, j))],
+        [x, *stats, gain, w], [ANY, pl.BlockSpec((seq, bn), lambda j: (0, j))],
         [sds((seq, hid)), sds((seq, w.shape[1]))], token, 2 * seq * hid * w.shape[1],
         scratch=[pltpu.VMEM((seq, hid), BF16), pltpu.SemaphoreType.DMA((chunks,)), pltpu.SemaphoreType.DMA],
         name='qkv')
 
 
-def norm_kernel(pos_ref, keep_ref, r1_ref, r2_ref, r3_ref, act_ref, res_ref, st_ref, g_ref, out_ref):
-    step = 16
-    gain = g_ref[...].astype(F32)
-    for i in range(keep_ref.shape[0] // step):
-        rows = pl.ds(i * step, step)
-        total = (keep_ref[rows, :] + r1_ref[rows, :].astype(F32) + r2_ref[rows, :].astype(F32)
-                 + r3_ref[rows, :].astype(F32))
-        rstd = st_ref[0, rows, 1:2]
-        hat = (act_ref[0, rows, :].astype(F32) - st_ref[0, rows, 0:1]) * rstd
-        scaled = total * gain
-        mean_scaled = jnp.mean(scaled, axis=-1, keepdims=True)
-        mean_cross = jnp.mean(scaled * hat, axis=-1, keepdims=True)
-        res = (res_ref[0, rows, :] if len(res_ref.shape) == 3 else res_ref[rows, :]).astype(F32)
-        out_ref[rows, :] = (res + rstd * (scaled - mean_scaled - hat * mean_cross)).astype(BF16)
+def norm_kernel(m, pos_ref, keep_ref, r1_ref, r2_ref, r3_ref, act_ref, res_ref, mu_ref, rs_ref, g_ref, out_ref,
+                mu_v, rs_v):
+    blk, hid = keep_ref.shape
+    high, wide = 16, 512
+    mu_v[...] = jnp.broadcast_to(mu_ref[m:m + 1, :], (128, blk)).T
+    rs_v[...] = jnp.broadcast_to(rs_ref[m:m + 1, :], (128, blk)).T
+
+    @pl.loop(0, blk // high)
+    def _(i):
+        rows = pl.ds(pl.multiple_of(i * high, high), high)
+        mean, rstd = mu_v[rows, 0:1], rs_v[rows, 0:1]
+
+        def terms(j):
+            cols = pl.ds(j * wide, wide)
+            total = (keep_ref[rows, cols] + r1_ref[rows, cols].astype(F32) + r2_ref[rows, cols].astype(F32)
+                     + r3_ref[rows, cols].astype(F32))
+            hat = (act_ref[0, rows, cols].astype(F32) - mean) * rstd
+            return cols, total * g_ref[:, cols].astype(F32), hat
+
+        plain = cross = jnp.zeros((high, wide), F32)
+        for j in range(hid // wide):
+            _, scaled, hat = terms(j)
+            plain = plain + scaled
+            cross = cross + scaled * hat
+        mean_scaled = jnp.sum(plain, axis=-1, keepdims=True) * (1.0 / hid)
+        mean_cross = jnp.sum(cross, axis=-1, keepdims=True) * (1.0 / hid)
+        for j in range(hid // wide):
+            cols, scaled, hat = terms(j)
+            res = (res_ref[0, rows, cols] if len(res_ref.shape) == 3 else res_ref[rows, cols]).astype(F32)
+            out_ref[rows, cols] = (res + rstd * (scaled - mean_scaled - hat * mean_cross)).astype(BF16)
 
 
 def norm_shard(m, keep, got, acts, resid, stats, gain, pos, token):
     blk, hid = keep.shape
-    bm = blk
-    n = blk // bm
-    local = pl.BlockSpec((bm, hid), lambda i, p: (i, 0))
-    row = pl.BlockSpec((1, bm, hid), lambda i, p: (m, p[0] * n + i, 0))
+    local = pl.BlockSpec((blk, hid), lambda i, p: (0, 0))
+    row = pl.BlockSpec((1, blk, hid), lambda i, p: (m, p[0], 0))
+    stat = pl.BlockSpec((stats[0].shape[0], blk), lambda i, p: (0, p[0]))
     return call(
-        norm_kernel, (n,),
-        [local] * 4 + [row, row if resid.ndim == 3 else local,
-                       pl.BlockSpec((1, bm, 2), lambda i, p: (m, p[0] * n + i, 0)), pl.BlockSpec((1, hid), lambda i, p: (0, 0))],
-        [keep, *got, acts, resid, stats, gain], [local], [sds((blk, hid))], token, 20 * blk * hid, pos=pos, name='norm')
+        partial(norm_kernel, m), (1,),
+        [local] * 4 + [row, row if resid.ndim == 3 else local, stat, stat, whole(gain)],
+        [keep, *got, acts, resid, *stats, gain], [local], [sds((blk, hid))], token, 20 * blk * hid,
+        scratch=[pltpu.VMEM((blk, 128), F32)] * 2, pos=pos, name='norm')
 
 
 def head_backward(scale, q_ref, k_ref, v_ref, do_ref, o_ref, dq_ref, dk_ref, dv_ref, dk_acc, dv_acc):
@@ -292,16 +322,17 @@
     k_all, v_all = k_ref[...], v_ref[...]
     k_t, v_t = k_all.T, v_all.T
     nblk = seq // BQ
+    kpos = lax.broadcasted_iota(jnp.int32, (BQ, BQ), 0)
+    qpos = lax.broadcasted_iota(jnp.int32, (BQ, BQ), 1)
     for i in reversed(range(nblk)):
         rows = pl.ds(i * BQ, BQ)
         width = (i + 1) * BQ
         q, do = q_ref[rows, :], do_ref[rows, :]
-        s_t = mm(k_all[:width], q, NT) * scale
-        kpos = lax.broadcasted_iota(jnp.int32, (width, BQ), 0)
-        qpos = lax.broadcasted_iota(jnp.int32, (width, BQ), 1) + i * BQ
-        s_t = jnp.where(qpos >= kpos, s_t, -1e30)
+        s_t = mm(k_all[:width], q, NT)
+        last = jnp.where(qpos >= kpos, s_t[i * BQ:], -1e30)
+        s_t = jnp.concatenate([s_t[:i * BQ], last], axis=0) if i else last
         top = jnp.max(s_t, axis=0, keepdims=True)
-        p_t = jnp.exp(s_t - top)
+        p_t = jnp.exp((s_t - top) * scale)
         p_t = p_t * (1.0 / jnp.sum(p_t, axis=0, keepdims=True))
         p_b = p_t.astype(BF16)
         o_ref[rows, :] = mm(v_t[:, :width], p_b).T.astype(BF16)
@@ -379,18 +410,26 @@
         name='attn', cid=2 + m)
 
 
-def copy_kernel(src_ref, *refs):
-    refs[-1][0] = src_ref[...]
-
-
-def write_out(m, src, buf, count, token):
-    seq, hid = src.shape
-    bm = 256
-    args, specs, alias = [src], [pl.BlockSpec((bm, hid), lambda i: (i, 0))], None
-    if buf is not None:
-        args, specs, alias = [src, buf], specs + [ANY], {1: 0}
-    return call(copy_kernel, (seq // bm,), specs, args, [pl.BlockSpec((1, bm, hid), lambda i: (m, i, 0))],
-                [sds((count, seq, hid))], token, src.size, alias=alias, name='copy')
+def copy_kernel(m, src, old, dst, buf, in_sem, out_sem):
+    parts = in_sem.shape[0]
+    part = src.shape[0] // parts
+    at = [pl.ds(r * part, part) for r in range(parts)]
+    loads = [pltpu.make_async_copy(src.at[at[r]], buf.at[at[r]], in_sem.at[r]) for r in range(parts)]
+    stores = [pltpu.make_async_copy(buf.at[at[r]], dst.at[m, at[r]], out_sem.at[r]) for r in range(parts)]
+    for load in loads:
+        load.start()
+    for load, store in zip(loads, stores):
+        load.wait()
+        store.start()
+    for store in stores:
+        store.wait()
+
+
+def write_out(m, src, old, token):
+    parts = 8
+    return call(partial(copy_kernel, m), (1,), [ANY, ANY], [src, old], [ANY], [sds(old.shape)], token, src.size,
+                scratch=[pltpu.VMEM(src.shape, BF16), pltpu.SemaphoreType.DMA((parts,)),
+                         pltpu.SemaphoreType.DMA((parts,))], alias={1: 0}, name='copy')
 
 
 def grad_kernel(a0_ref, a1_ref, b0_ref, b1_ref, out_ref):
@@ -414,21 +453,47 @@
 
 
 def qkv_grad_kernel(a0_ref, a1_ref, *refs):
-    out_ref = refs[-1]
+    src, out_ref, dst, buf, in_sem, out_sem = refs[6], *refs[7:]
     rows, _, heads, dim = out_ref.shape
+    step, steps = pl.program_id(0), pl.num_programs(0)
+    part = src.shape[0] // in_sem.shape[0]
+
+    def move(r, out):
+        at = pl.ds(r * part, part)
+        if out:
+            return pltpu.make_async_copy(buf.at[at], dst.at[0, at], out_sem.at[r])
+        return pltpu.make_async_copy(src.at[at], buf.at[at], in_sem.at[r])
+
+    for r in range(in_sem.shape[0]):
+        @pl.when(step == r)
+        def _():
+            move(r, False).start()
+
+        @pl.when(step == r + 1)
+        def _():
+            move(r, False).wait()
+            move(r, True).start()
+
     for c in range(3):
         acc = mm(a0_ref[...], refs[c][...], TN) + mm(a1_ref[...], refs[3 + c][...], TN)
         out_ref[:, c] = acc.reshape(rows, heads, dim).astype(BF16)
 
-
-def qkv_grad(norms, grads, heads, dim, token):
+    @pl.when(step == steps - 1)
+    def _():
+        for r in range(in_sem.shape[0]):
+            move(r, True).wait()
+
+
+def qkv_grad(norms, grads, heads, dim, dx, count, token):
     seq, hid = norms[0].shape
-    ba = 1024
+    ba, parts = 512, 4
     lhs = pl.BlockSpec((seq, ba), lambda i: (0, i))
-    whole = pl.BlockSpec((seq, heads * dim), lambda i: (0, 0))
-    return call(qkv_grad_kernel, (hid // ba,), [lhs] * 2 + [whole] * 6, [*norms, *grads[0], *grads[1]],
-                [pl.BlockSpec((ba, 3, heads, dim), lambda i: (i, 0, 0, 0))], [sds((hid, 3, heads, dim))], token,
-                12 * seq * hid * heads * dim, name='dqkvw')
+    rhs = pl.BlockSpec((seq, heads * dim), lambda i: (0, 0))
+    return call(qkv_grad_kernel, (hid // ba,), [lhs] * 2 + [rhs] * 6 + [ANY], [*norms, *grads[0], *grads[1], dx],
+                [pl.BlockSpec((ba, 3, heads, dim), lambda i: (i, 0, 0, 0)), ANY],
+                [sds((hid, 3, heads, dim)), sds((count, *dx.shape))], token, 12 * seq * hid * heads * dim,
+                scratch=[pltpu.VMEM(dx.shape, BF16), pltpu.SemaphoreType.DMA((parts,)),
+                         pltpu.SemaphoreType.DMA((parts,))], name='dqkvw')
 
 
 def flat_kernel(w_ref, out_ref):
@@ -463,8 +528,7 @@
         scale = dim ** -0.5
         idx = lax.axis_index('tp')
         pos = jnp.stack([idx, idx // 2, idx % 2]).astype(jnp.int32)
-        stats_one = jnp.stack([mean_one, rstd_one], axis=-1)
-        stats_two = jnp.stack([mean_two, rstd_two], axis=-1)
+        stats_one, stats_two = (mean_one, rstd_one), (mean_two, rstd_two)
         g1, g2 = gain_one.reshape(1, hid), gain_two.reshape(1, hid)
         w_out = w_out.reshape(heads * dim, hid)
         tok = jnp.zeros((8, 128), F32)
@@ -492,17 +556,16 @@
         dh[1] = gather(dh_shard[1])
         n1[1], qkv[1], tok = qkv_proj(1, x_saved, stats_one, g1, w_flat, tok)
         grad_down, tok = weight_grad(act, grad_y, tok, 1024, 1024, 'dw2')
+        dx_shard, tok = norm_shard(0, keep_a, got_a, x_saved, dh_shard[0], stats_one, g1, pos, tok)
+        dx[0] = gather(dx_shard)
         out[1], *g1s, keep_b, s1, s2, s3, tok = attention(1, dh[1], w_out, qkv[1], w_flat, dim, scale, tok)
         got_b = exchange((s1, s2, s3))
-        dx_shard, tok = norm_shard(0, keep_a, got_a, x_saved, dh_shard[0], stats_one, g1, pos, tok)
-        dx[0] = gather(dx_shard)
         grad_up, tok = weight_grad(n2, dpre, tok, 1024, 1024, 'dw1')
         dx_shard, tok = norm_shard(1, keep_b, got_b, x_saved, dh_shard[1], stats_one, g1, pos, tok)
         dx[1] = gather(dx_shard)
-        grad_qkv_w, tok = qkv_grad(n1, [g0, g1s], heads, dim, tok)
         grad_out_w, tok = weight_grad(out, dh, tok, 512, 1024, 'dwo')
-        grad_x, tok = write_out(0, dx[0], None, 2, tok)
-        grad_x, tok = write_out(1, dx[1], grad_x, 2, tok)
+        grad_qkv_w, grad_x, tok = qkv_grad(n1, [g0, g1s], heads, dim, dx[0], 2, tok)
+        grad_x, tok = write_out(1, dx[1], grad_x, tok)
         return grad_x, grad_qkv_w.transpose(0, 2, 1, 3), grad_out_w.reshape(heads, dim, hid), grad_up, grad_down
 
     return jax.shard_map(local_backward, mesh=mesh, in_specs=in_specs, out_specs=out_specs, check_vma=False)

time: 585 us -> 549 us (0.938)
  waiting for transfers between devices: 60.9 us -> 27.7 us
    all_gather x4, waiting for transfers between devices: 19 us -> 0.04 us  [gather(): return lax.all_gather(shard, 'tp', axis=0, tiled=True)]
    ppermute x12, waiting for transfers between devices: 41.8 us -> 27.6 us  [swap(): return lax.ppermute(arr, 'tp', [(i, i ^ bit) for i in range(8)])]
    pallas_call x17 -> x16, Pallas kernels: 475 us -> 479 us  [call(): pl.pallas_call(kernel, grid_spec=pltpu.PrefetchScalarGridSpec(num_scalar_...]
  transfers between devices with their start and end apart: 16 -> 16, of which waited for: 3 -> 4; matrix products, arithmetic and copies ran while one was open for 1% -> 0% of each run, Pallas kernels for 65% -> 71%
where the time goes in v3:
time: 549 us; the launch traced here: 540 us
  Pallas kernels  479 us (87%)
  waiting for transfers between devices  27.7 us (5%)
  starting transfers between devices  14.8 us (3%)
  between operations  14.4 us (3%)
    pallas_call x16, Pallas kernels, call(): pl.pallas_call(kernel, grid_spec=pltpu.PrefetchScalarGridSpec(num_scalar_...  479 us
    ppermute x12, waiting for transfers between devices, swap(): return lax.ppermute(arr, 'tp', [(i, i ^ bit) for i in range(8)])  27.6 us
    ppermute x12, starting transfers between devices, swap(): return lax.ppermute(arr, 'tp', [(i, i ^ bit) for i in range(8)])  14.6 us
  transfers between devices with their start and end apart: 16, of which 4 were waited for; matrix products, arithmetic and copies ran while one was open for 0% of the time, Pallas kernels for 71%

profile of v3, /device:TPU:0, one launch (start us, length us, event | category | flops | bytes accessed | tf_op | source)
XLA Modules:
  0.0 540.0 jit_solution(5240531751620088354)
XLA Ops:
  7.2 1.3 reshape.22.refs_4_.refs_9_
  8.5 0.6 broadcast_in_dim.3.refs_8_
  9.1 73.4 %mlp.2 = (bf16[1024,4096]{1,0:T(8,128)(2,1)}, bf16[1024,2048]{1,0:T(8,128)(2,1)}, bf16[1024,2048]{1,0:T(8,128)(2,1)}, f32[128,4096]{1,0:T(8,128)}, bf16[128,4096...) custom-call(bf16[2,1024,4096]{2,1,0:T(8,128)(2,1)} %refs_5_.9, ...), custom_call_target="tpu_custom_call" | custom-call | flops 51539607552 | bytes 105930752 | tf_op jit(solution)/shard_map/mlp/pallas_call | solution.py:32
  82.5 2.6 collective-permute-start
  85.1 1.5 collective-permute-start.1
  86.6 0.6 reshape.23.refs_3_.refs_9_
  87.2 16.5 %flat.1 = (bf16[4096,1536]{1,0:T(8,128)(2,1)}, f32[8,128]{1,0:T(8,128)}) custom-call(bf16[4096,3,4,128]{3,2,1,0:T(4,128)(2,1)} %bitcast.7, f32[8,128]{1,0:T(8,128)} %get-tuple-element.69.refs_1_), custom_call_target="tpu_custom_call" | custom-call | flops 6291456 | bytes 25165824 | tf_op jit(solution)/shard_map/flat/pallas_call | solution.py:32
  104.3 21.7 %qkv.2 = (bf16[1024,4096]{1,0:T(8,128)(2,1)}, bf16[1024,1536]{1,0:T(8,128)(2,1)}, f32[8,128]{1,0:T(8,128)}) custom-call(bf16[2,1024,4096]{2,1,0:T(8,128)(2,1)} %refs_5_.11, f32[2,1024]{1,0:T(2,128)} %refs_7_.11, f32[2,1024]{1,0:T(2,128)} %refs_8_.7, bf16[1,4096]{1,0:T(2,128)(2,1)} %reshape.23.refs_3_.refs_9_, ...), custom_call_target="tpu_custom_call" | custom-call | flops 12884901888 | bytes 40919040 | tf_op jit(solution)/shard_map/qkv/pallas_call | solution.py:32
  126.0 6.8 %collective-permute-done.1.refs_3_ = bf16[128,4096]{1,0:T(8,128)(2,1)} collective-permute-done((bf16[128,4096]{1,0:T(8,128)(2,1)}, bf16[128,4096]{1,0:T(8,128)(2,1)}, u32[]{:S(2)}, u32[]{:S(2)}) %collective-permute-start.1) | collective-permute-done | bytes 1048608 | tf_op jit(solution)/shard_map/ppermute | solution.py:514
  132.8 7.1 %norm.4 = (bf16[128,4096]{1,0:T(8,128)(2,1)}, f32[8,128]{1,0:T(8,128)}) custom-call(s32[3]{0:T(128)} %pad_add_fusion.refs_0_, f32[128,4096]{1,0:T(8,128)} %get-tuple-element.65.refs_1_, bf16[128,4096]{1,0:T(8,128)(2,1)} %copy-done, bf16[128,4096]{1,0:T(8,128)(2,1)} %collective-permute-done.1.refs_3_, bf16[128,4096]{1,0:T(8,128)(2,1)} %collective-permute-done.2.refs_4_, ...), custom_call_target="tpu_custom_call" | custom-call | flops 10485760 | bytes 39870464 | tf_op jit(solution)/shard_map/norm/pallas_call | solution.py:32
  139.9 72.0 %mlp.3 = (bf16[1024,4096]{1,0:T(8,128)(2,1)}, bf16[1024,2048]{1,0:T(8,128)(2,1)}, bf16[1024,2048]{1,0:T(8,128)(2,1)}, f32[128,4096]{1,0:T(8,128)}, bf16[128,4096...) custom-call(bf16[2,1024,4096]{2,1,0:T(8,128)(2,1)} %refs_5_.9, ...), custom_call_target="tpu_custom_call" | custom-call | flops 51539607552 | bytes 105930752 | tf_op jit(solution)/shard_map/mlp/pallas_call | solution.py:32
  211.9 1.5 collective-permute-start.3
  214.0 1.4 collective-permute-start.5
  215.4 58.8 %attn.2 = (bf16[1024,512]{1,0:T(8,128)(2,1)}, bf16[1024,512]{1,0:T(8,128)(2,1)}, bf16[1024,512]{1,0:T(8,128)(2,1)}, bf16[1024,512]{1,0:T(8,128)(2,1)}, f32[128,4...) custom-call(bf16[1024,4096]{1,0:T(8,128)(2,1)} %all-gather.5.cloned., ...), custom_call_target="tpu_custom_call" | custom-call | flops 30064771072 | bytes 44040192 | tf_op jit(solution)/shard_map/attn/pallas_call | solution.py:32
  274.3 0.9 copy-done.1
  275.2 7.1 %norm.5 = (bf16[128,4096]{1,0:T(8,128)(2,1)}, f32[8,128]{1,0:T(8,128)}) custom-call(s32[3]{0:T(128)} %pad_add_fusion.refs_0_, f32[128,4096]{1,0:T(8,128)} %get-tuple-element.74.refs_1_, bf16[128,4096]{1,0:T(8,128)(2,1)} %copy-done.1, bf16[128,4096]{1,0:T(8,128)(2,1)} %collective-permute-done.4.refs_3_, bf16[128,4096]{1,0:T(8,128)(2,1)} %collective-permute-done.5.refs_4_, ...), custom_call_target="tpu_custom_call" | custom-call | flops 10485760 | bytes 39870464 | tf_op jit(solution)/shard_map/norm/pallas_call | solution.py:32
  282.3 1.5 collective-permute-start.6
  284.4 1.4 collective-permute-start.8
  285.8 21.4 %qkv.3 = (bf16[1024,4096]{1,0:T(8,128)(2,1)}, bf16[1024,1536]{1,0:T(8,128)(2,1)}, f32[8,128]{1,0:T(8,128)}) custom-call(bf16[2,1024,4096]{2,1,0:T(8,128)(2,1)} %refs_5_.11, f32[2,1024]{1,0:T(2,128)} %refs_7_.11, f32[2,1024]{1,0:T(2,128)} %refs_8_.7, bf16[1,4096]{1,0:T(2,128)(2,1)} %reshape.23.refs_3_.refs_9_, ...), custom_call_target="tpu_custom_call" | custom-call | flops 12884901888 | bytes 40919040 | tf_op jit(solution)/shard_map/qkv/pallas_call | solution.py:32
  307.3 41.4 %dw2.1 = (bf16[2048,4096]{1,0:T(8,128)(2,1)}, f32[8,128]{1,0:T(8,128)}) custom-call(bf16[1024,2048]{1,0:T(8,128)(2,1)} %get-tuple-element.89.refs_0_, bf16[1024,2048]{1,0:T(8,128)(2,1)} %get-tuple-element.90.refs_1_, bf16[2,1024,4096]{2,1,0:T(8,128)(2,1)} %refs_3_.5, bf16[2,1024,4096]{2,1,0:T(8,128)(2,1)} %refs_3_.5, f32[8,128]{1,0:T(8,128)} %get-tuple-element.91.refs_4_), custom_call_target="tpu_custom_call" | custom-call | flops 34359738368 | bytes 58720256 | tf_op jit(solution)/shard_map/dw2/pallas_call | solution.py:32
  348.7 16.4 %collective-permute-done.8.refs_4_ = bf16[128,4096]{1,0:T(8,128)(2,1)} collective-permute-done((bf16[128,4096]{1,0:T(8,128)(2,1)}, bf16[128,4096]{1,0:T(8,128)(2,1)}, u32[]{:S(2)}, u32[]{:S(2)}) %collective-permute-start.8) | collective-permute-done | bytes 1048608 | tf_op jit(solution)/shard_map/ppermute | solution.py:514
  365.1 7.1 %norm.6 = (bf16[128,4096]{1,0:T(8,128)(2,1)}, f32[8,128]{1,0:T(8,128)}) custom-call(s32[3]{0:T(128)} %pad_add_fusion.refs_0_, f32[128,4096]{1,0:T(8,128)} %get-tuple-element.85.refs_1_, bf16[128,4096]{1,0:T(8,128)(2,1)} %copy-done.2, bf16[128,4096]{1,0:T(8,128)(2,1)} %collective-permute-done.7.refs_3_, bf16[128,4096]{1,0:T(8,128)(2,1)} %collective-permute-done.8.refs_4_, ...), custom_call_target="tpu_custom_call" | custom-call | flops 10485760 | bytes 24141824 | tf_op jit(solution)/shard_map/norm/pallas_call | solution.py:32
  372.3 49.0 %attn.3 = (bf16[1024,512]{1,0:T(8,128)(2,1)}, bf16[1024,512]{1,0:T(8,128)(2,1)}, bf16[1024,512]{1,0:T(8,128)(2,1)}, bf16[1024,512]{1,0:T(8,128)(2,1)}, f32[128,4...) custom-call(bf16[1024,4096]{1,0:T(8,128)(2,1)} %all-gather.7.cloned., ...), custom_call_target="tpu_custom_call" | custom-call | flops 30064771072 | bytes 44040192 | tf_op jit(solution)/shard_map/attn/pallas_call | solution.py:32
  421.8 1.7 collective-permute-start.11
  423.5 1.3 collective-permute-start.9
  424.8 41.4 %dw1.1 = (bf16[4096,2048]{1,0:T(8,128)(2,1)}, f32[8,128]{1,0:T(8,128)}) custom-call(bf16[1024,4096]{1,0:T(8,128)(2,1)} %get-tuple-element.98.refs_0_, bf16[1024,4096]{1,0:T(8,128)(2,1)} %get-tuple-element.99.refs_1_, bf16[1024,2048]{1,0:T(8,128)(2,1)} %get-tuple-element.100.refs_2_, bf16[1024,2048]{1,0:T(8,128)(2,1)} %get-tuple-element.101.refs_3_, ...), custom_call_target="tpu_custom_call" | custom-call | flops 34359738368 | bytes 41943040 | tf_op jit(solution)/shard_map/dw1/pallas_call | solution.py:32
  466.2 2.9 collective-permute-done.10.refs_3_
  469.1 1.5 collective-permute-done.9.refs_2_
  470.6 7.1 %norm.7 = (bf16[128,4096]{1,0:T(8,128)(2,1)}, f32[8,128]{1,0:T(8,128)}) custom-call(s32[3]{0:T(128)} %pad_add_fusion.refs_0_, f32[128,4096]{1,0:T(8,128)} %get-tuple-element.94.refs_1_, bf16[128,4096]{1,0:T(8,128)(2,1)} %collective-permute-done.9.refs_2_, bf16[128,4096]{1,0:T(8,128)(2,1)} %copy-done.3, bf16[128,4096]{1,0:T(8,128)(2,1)} %collective-permute-done.11.refs_4_, ...), custom_call_target="tpu_custom_call" | custom-call | flops 10485760 | bytes 24141824 | tf_op jit(solution)/shard_map/norm/pallas_call | solution.py:32
  477.6 14.0 %dwo.1 = (bf16[512,4096]{1,0:T(8,128)(2,1)}, f32[8,128]{1,0:T(8,128)}) custom-call(bf16[1024,512]{1,0:T(8,128)(2,1)} %get-tuple-element.114.refs_0_, bf16[1024,512]{1,0:T(8,128)(2,1)} %get-tuple-element.115.refs_1_, bf16[1024,4096]{1,0:T(8,128)(2,1)} %all-gather.5.cloned.1.call-done.refs_0_.refs_2_, ...), custom_call_target="tpu_custom_call" | custom-call | flops 8589934592 | bytes 23068672 | tf_op jit(solution)/shard_map/dwo/pallas_call | solution.py:32
  491.6 34.9 %dqkvw.1 = (bf16[4096,3,4,128]{3,2,1,0:T(4,128)(2,1)}, bf16[2,1024,4096]{2,1,0:T(8,128)(2,1)}, f32[8,128]{1,0:T(8,128)}) custom-call(bf16[1024,4096]{1,0:T(8,128)(2,1)} %get-tuple-element.105.refs_0_, bf16[1024,4096]{1,0:T(8,128)(2,1)} %get-tuple-element.106.refs_1_, bf16[1024,512]{1,0:T(8,128)(2,1)} %get-tuple-element.107.refs_2_, ...), custom_call_target="tpu_custom_call" | custom-call | flops 25769803776 | bytes 60817408 | tf_op jit(solution)/shard_map/dqkvw/pallas_call | solution.py:32
  526.6 6.4 %copy.21 = (bf16[2,1024,4096]{2,1,0:T(8,128)(2,1)}, f32[8,128]{1,0:T(8,128)}) custom-call(bf16[1024,4096]{1,0:T(8,128)(2,1)} %all-gather.9.cloned.1.call-done.refs_0_, bf16[2,1024,4096]{2,1,0:T(8,128)(2,1)} %get-tuple-element.118.refs_1_, f32[8,128]{1,0:T(8,128)} %get-tuple-element.119.refs_2_), custom_call_target="tpu_custom_call", output_to_operand_aliasing={{0}: (1, {})} | custom-call | flops 4194304 | bytes 41943040 | tf_op jit(solution)/shard_map/copy/pallas_call | solution.py:32
  (34 shorter events, 2.5 us)
Async XLA Ops:
  7.2 208.2 %all-gather.5.cloned.1.call-start = ((), (), s32[]{:S(2)}) async-start(), calls=%async_computation | async-start | bytes 9437184 | tf_op jit(solution)/shard_map/all_gather | solution.py:537
  9.1 77.5 %copy-start.4 = (bf16[4096]{0:T(1024)(128)(2,1)S(1)}, bf16[4096]{0:T(1024)(128)(2,1)}, u32[]{:S(2)}) copy-start(bf16[4096]{0:T(1024)(128)(2,1)} %param.20) | copy-start | bytes 24580
  82.5 43.5 %collective-permute-start = (bf16[128,4096]{1,0:T(8,128)(2,1)}, bf16[128,4096]{1,0:T(8,128)(2,1)S(1)}, u32[]{:S(2)}, u32[]{:S(2)}) collective-permute-start(bf16[128,4096]{1,0:T(8,128)(2,1)} %get-tuple-element.66), channel_id=1, source_target_pairs={{0,2},{1,3},{2,0},{3,1},{4,6},{5,7},{6,4},{7,5}} | collective-permute-start | bytes 3145736 | tf_op jit(solution)/shard_map/ppermute | solution.py:514
  85.1 47.7 %collective-permute-start.1 = (bf16[128,4096]{1,0:T(8,128)(2,1)}, bf16[128,4096]{1,0:T(8,128)(2,1)}, u32[]{:S(2)}, u32[]{:S(2)}) collective-permute-start(bf16[128,4096]{1,0:T(8,128)(2,1)} %get-tuple-element.67), channel_id=1, source_target_pairs={{0,4},{1,5},{2,6},{3,7},{4,0},{5,1},{6,2},{7,3}} | collective-permute-start | bytes 3145736 | tf_op jit(solution)/shard_map/ppermute | solution.py:514
  86.6 46.2 %collective-permute-start.2 = (bf16[128,4096]{1,0:T(8,128)(2,1)}, bf16[128,4096]{1,0:T(8,128)(2,1)}, u32[]{:S(2)}, u32[]{:S(2)}) collective-permute-start(bf16[128,4096]{1,0:T(8,128)(2,1)} %get-tuple-element.68), channel_id=1, source_target_pairs={{0,6},{1,7},{2,4},{3,5},{4,2},{5,3},{6,0},{7,1}} | collective-permute-start | bytes 3145736 | tf_op jit(solution)/shard_map/ppermute | solution.py:514
  125.9 6.8 %copy-start = (bf16[128,4096]{1,0:T(8,128)(2,1)}, bf16[128,4096]{1,0:T(8,128)(2,1)S(1)}, u32[]{:S(2)}) copy-start(bf16[128,4096]{1,0:T(8,128)(2,1)S(1)} %collective-permute-done.refs_2_) | copy-start | bytes 3145732
  139.8 232.4 %all-gather.7.cloned.1.call-start = ((), (), s32[]{:S(2)}) async-start(), calls=%async_computation.1 | async-start | bytes 9437184 | tf_op jit(solution)/shard_map/all_gather | solution.py:537
  211.9 62.3 %collective-permute-start.3 = (bf16[128,4096]{1,0:T(8,128)(2,1)}, bf16[128,4096]{1,0:T(8,128)(2,1)S(1)}, u32[]{:S(2)}, u32[]{:S(2)}) collective-permute-start(bf16[128,4096]{1,0:T(8,128)(2,1)} %get-tuple-element.75), channel_id=1, source_target_pairs={{0,2},{1,3},{2,0},{3,1},{4,6},{5,7},{6,4},{7,5}} | collective-permute-start | bytes 3145736 | tf_op jit(solution)/shard_map/ppermute | solution.py:514
  213.4 60.8 %collective-permute-start.4 = (bf16[128,4096]{1,0:T(8,128)(2,1)}, bf16[128,4096]{1,0:T(8,128)(2,1)}, u32[]{:S(2)}, u32[]{:S(2)}) collective-permute-start(bf16[128,4096]{1,0:T(8,128)(2,1)} %get-tuple-element.76), channel_id=1, source_target_pairs={{0,4},{1,5},{2,6},{3,7},{4,0},{5,1},{6,2},{7,3}} | collective-permute-start | bytes 3145736 | tf_op jit(solution)/shard_map/ppermute | solution.py:514
  214.0 60.3 %collective-permute-start.5 = (bf16[128,4096]{1,0:T(8,128)(2,1)}, bf16[128,4096]{1,0:T(8,128)(2,1)}, u32[]{:S(2)}, u32[]{:S(2)}) collective-permute-start(bf16[128,4096]{1,0:T(8,128)(2,1)} %get-tuple-element.77), channel_id=1, source_target_pairs={{0,6},{1,7},{2,4},{3,5},{4,2},{5,3},{6,0},{7,1}} | collective-permute-start | bytes 3145736 | tf_op jit(solution)/shard_map/ppermute | solution.py:514
  274.2 1.0 copy-start.1
  282.3 209.3 %all-gather.11.cloned.1.call-start = ((), (), s32[]{:S(2)}) async-start(), calls=%async_computation.3 | async-start | bytes 9437184 | tf_op jit(solution)/shard_map/all_gather | solution.py:537
  282.3 66.4 %collective-permute-start.6 = (bf16[128,4096]{1,0:T(8,128)(2,1)}, bf16[128,4096]{1,0:T(8,128)(2,1)S(1)}, u32[]{:S(2)}, u32[]{:S(2)}) collective-permute-start(bf16[128,4096]{1,0:T(8,128)(2,1)} %get-tuple-element.86), channel_id=1, source_target_pairs={{0,2},{1,3},{2,0},{3,1},{4,6},{5,7},{6,4},{7,5}} | collective-permute-start | bytes 3145736 | tf_op jit(solution)/shard_map/ppermute | solution.py:514
  283.8 64.8 %collective-permute-start.7 = (bf16[128,4096]{1,0:T(8,128)(2,1)}, bf16[128,4096]{1,0:T(8,128)(2,1)}, u32[]{:S(2)}, u32[]{:S(2)}) collective-permute-start(bf16[128,4096]{1,0:T(8,128)(2,1)} %get-tuple-element.87), channel_id=1, source_target_pairs={{0,4},{1,5},{2,6},{3,7},{4,0},{5,1},{6,2},{7,3}} | collective-permute-start | bytes 3145736 | tf_op jit(solution)/shard_map/ppermute | solution.py:514
  284.4 80.7 %collective-permute-start.8 = (bf16[128,4096]{1,0:T(8,128)(2,1)}, bf16[128,4096]{1,0:T(8,128)(2,1)}, u32[]{:S(2)}, u32[]{:S(2)}) collective-permute-start(bf16[128,4096]{1,0:T(8,128)(2,1)} %get-tuple-element.88), channel_id=1, source_target_pairs={{0,6},{1,7},{2,4},{3,5},{4,2},{5,3},{6,0},{7,1}} | collective-permute-start | bytes 3145736 | tf_op jit(solution)/shard_map/ppermute | solution.py:514
  348.7 16.4 %copy-start.2 = (bf16[128,4096]{1,0:T(8,128)(2,1)}, bf16[128,4096]{1,0:T(8,128)(2,1)S(1)}, u32[]{:S(2)}) copy-start(bf16[128,4096]{1,0:T(8,128)(2,1)S(1)} %collective-permute-done.6.refs_2_) | copy-start | bytes 3145732
  372.2 154.3 %all-gather.9.cloned.1.call-start = ((), (), s32[]{:S(2)}) async-start(), calls=%async_computation.2 | async-start | bytes 9437184 | tf_op jit(solution)/shard_map/all_gather | solution.py:537
  421.3 47.8 %collective-permute-start.10 = (bf16[128,4096]{1,0:T(8,128)(2,1)}, bf16[128,4096]{1,0:T(8,128)(2,1)S(1)}, u32[]{:S(2)}, u32[]{:S(2)}) collective-permute-start(bf16[128,4096]{1,0:T(8,128)(2,1)} %get-tuple-element.96), channel_id=1, source_target_pairs={{0,4},{1,5},{2,6},{3,7},{4,0},{5,1},{6,2},{7,3}} | collective-permute-start | bytes 3145736 | tf_op jit(solution)/shard_map/ppermute | solution.py:514
  421.8 47.3 %collective-permute-start.11 = (bf16[128,4096]{1,0:T(8,128)(2,1)}, bf16[128,4096]{1,0:T(8,128)(2,1)}, u32[]{:S(2)}, u32[]{:S(2)}) collective-permute-start(bf16[128,4096]{1,0:T(8,128)(2,1)} %get-tuple-element.97), channel_id=1, source_target_pairs={{0,6},{1,7},{2,4},{3,5},{4,2},{5,3},{6,0},{7,1}} | collective-permute-start | bytes 3145736 | tf_op jit(solution)/shard_map/ppermute | solution.py:514
  423.5 47.1 %collective-permute-start.9 = (bf16[128,4096]{1,0:T(8,128)(2,1)}, bf16[128,4096]{1,0:T(8,128)(2,1)}, u32[]{:S(2)}, u32[]{:S(2)}) collective-permute-start(bf16[128,4096]{1,0:T(8,128)(2,1)} %get-tuple-element.95), channel_id=1, source_target_pairs={{0,2},{1,3},{2,0},{3,1},{4,6},{5,7},{6,4},{7,5}} | collective-permute-start | bytes 3145736 | tf_op jit(solution)/shard_map/ppermute | solution.py:514
  469.1 1.5 copy-start.3
Sparse Core Ops, SparseCore 0:
  140.0 48.3 all-gather.4
  282.4 84.6 all-gather.6
  372.3 48.3 all-gather.10
  477.8 48.3 all-gather.8

commit v4 on v3

--- a/solution.py
+++ b/solution.py
@@ -504,7 +504,7 @@
 
 def flat_weight(w, token):
     hid, three, heads, dim = w.shape
-    bm = 256
+    bm = 1024
     return call(flat_kernel, (hid // bm,), [pl.BlockSpec((bm, three, heads, dim), lambda i: (i, 0, 0, 0))], [w],
                 [pl.BlockSpec((bm, three * heads * dim), lambda i: (i, 0))], [sds((hid, three * heads * dim))], token,
                 w.size, name='flat')
@@ -544,22 +544,23 @@
 
         n2[0], act[0], dpre[0], keep_a, *send, tok = mlp(0, h1_saved, grad_y, stats_two, g2, w_up, w_down, tok)
         got_a = exchange(send)
+        n2[1], act[1], dpre[1], keep_b, *send, tok = mlp(1, h1_saved, grad_y, stats_two, g2, w_up, w_down, tok)
+        got_b = exchange(send)
+        dh_shard[0], tok = norm_shard(0, keep_a, got_a, h1_saved, grad_y, stats_two, g2, pos, tok)
+        dh[0] = gather(dh_shard[0])
         w_flat, tok = flat_weight(w_qkv.transpose(0, 2, 1, 3), tok)
         n1[0], qkv[0], tok = qkv_proj(0, x_saved, stats_one, g1, w_flat, tok)
-        dh_shard[0], tok = norm_shard(0, keep_a, got_a, h1_saved, grad_y, stats_two, g2, pos, tok)
-        dh[0] = gather(dh_shard[0])
-        n2[1], act[1], dpre[1], keep_b, *send, tok = mlp(1, h1_saved, grad_y, stats_two, g2, w_up, w_down, tok)
-        got_b = exchange(send)
+        n1[1], qkv[1], tok = qkv_proj(1, x_saved, stats_one, g1, w_flat, tok)
+        dh_shard[1], tok = norm_shard(1, keep_b, got_b, h1_saved, grad_y, stats_two, g2, pos, tok)
+        dh[1] = gather(dh_shard[1])
+
         out[0], *g0, keep_a, s1, s2, s3, tok = attention(0, dh[0], w_out, qkv[0], w_flat, dim, scale, tok)
         got_a = exchange((s1, s2, s3))
-        dh_shard[1], tok = norm_shard(1, keep_b, got_b, h1_saved, grad_y, stats_two, g2, pos, tok)
-        dh[1] = gather(dh_shard[1])
-        n1[1], qkv[1], tok = qkv_proj(1, x_saved, stats_one, g1, w_flat, tok)
-        grad_down, tok = weight_grad(act, grad_y, tok, 1024, 1024, 'dw2')
+        out[1], *g1s, keep_b, s1, s2, s3, tok = attention(1, dh[1], w_out, qkv[1], w_flat, dim, scale, tok)
+        got_b = exchange((s1, s2, s3))
         dx_shard, tok = norm_shard(0, keep_a, got_a, x_saved, dh_shard[0], stats_one, g1, pos, tok)
         dx[0] = gather(dx_shard)
-        out[1], *g1s, keep_b, s1, s2, s3, tok = attention(1, dh[1], w_out, qkv[1], w_flat, dim, scale, tok)
-        got_b = exchange((s1, s2, s3))
+        grad_down, tok = weight_grad(act, grad_y, tok, 1024, 1024, 'dw2')
         grad_up, tok = weight_grad(n2, dpre, tok, 1024, 1024, 'dw1')
         dx_shard, tok = norm_shard(1, keep_b, got_b, x_saved, dh_shard[1], stats_one, g1, pos, tok)
         dx[1] = gather(dx_shard)

time: 549 us -> 532 us (0.969)
  Pallas kernels: 479 us -> 466 us
    pallas_call x16, Pallas kernels: 479 us -> 466 us  [call(): pl.pallas_call(kernel, grid_spec=pltpu.PrefetchScalarGridSpec(num_scalar_...]
  transfers between devices with their start and end apart: 16 -> 16, of which waited for: 4 -> 1; matrix products, arithmetic and copies ran while one was open for 0% -> 0% of each run, Pallas kernels for 71% -> 71%
where the time goes in v4:
time: 532 us; the launch traced here: 524 us
  Pallas kernels  466 us (88%)
  waiting for transfers between devices  23.2 us (4%)
  starting transfers between devices  14.8 us (3%)
  between operations  14.4 us (3%)
  local copies, waits for them, and re-layouts  5.36 us (1%)
    pallas_call x16, Pallas kernels, call(): pl.pallas_call(kernel, grid_spec=pltpu.PrefetchScalarGridSpec(num_scalar_...  466 us
    ppermute x12, waiting for transfers between devices, swap(): return lax.ppermute(arr, 'tp', [(i, i ^ bit) for i in range(8)])  23.1 us
    ppermute x12, starting transfers between devices, swap(): return lax.ppermute(arr, 'tp', [(i, i ^ bit) for i in range(8)])  14.6 us
  transfers between devices with their start and end apart: 16, of which 1 were waited for; matrix products, arithmetic and copies ran while one was open for 0% of the time, Pallas kernels for 71%

profile of v4, /device:TPU:0, one launch (start us, length us, event | category | flops | bytes accessed | tf_op | source)
XLA Modules:
  0.0 524.1 jit_solution(4434453099153224100)
XLA Ops:
  7.2 1.3 reshape.22.refs_4_.refs_9_
  8.5 0.6 broadcast_in_dim.3.refs_8_
  9.1 73.3 %mlp.2 = (bf16[1024,4096]{1,0:T(8,128)(2,1)}, bf16[1024,2048]{1,0:T(8,128)(2,1)}, bf16[1024,2048]{1,0:T(8,128)(2,1)}, f32[128,4096]{1,0:T(8,128)}, bf16[128,4096...) custom-call(bf16[2,1024,4096]{2,1,0:T(8,128)(2,1)} %refs_5_.9, ...), custom_call_target="tpu_custom_call" | custom-call | flops 51539607552 | bytes 105930752 | tf_op jit(solution)/shard_map/mlp/pallas_call | solution.py:32
  82.4 2.6 collective-permute-start.3
  85.0 1.5 collective-permute-start.4
  86.5 72.2 %mlp.3 = (bf16[1024,4096]{1,0:T(8,128)(2,1)}, bf16[1024,2048]{1,0:T(8,128)(2,1)}, bf16[1024,2048]{1,0:T(8,128)(2,1)}, f32[128,4096]{1,0:T(8,128)}, bf16[128,4096...) custom-call(bf16[2,1024,4096]{2,1,0:T(8,128)(2,1)} %refs_5_.9, ...), custom_call_target="tpu_custom_call" | custom-call | flops 51539607552 | bytes 105930752 | tf_op jit(solution)/shard_map/mlp/pallas_call | solution.py:32
  158.8 0.6 pad_add_fusion.refs_0_
  159.4 1.0 copy-done
  160.4 7.2 %norm.4 = (bf16[128,4096]{1,0:T(8,128)(2,1)}, f32[8,128]{1,0:T(8,128)}) custom-call(s32[3]{0:T(128)} %pad_add_fusion.refs_0_, f32[128,4096]{1,0:T(8,128)} %get-tuple-element.70.refs_1_, bf16[128,4096]{1,0:T(8,128)(2,1)} %copy-done, bf16[128,4096]{1,0:T(8,128)(2,1)} %collective-permute-done.4.refs_3_, bf16[128,4096]{1,0:T(8,128)(2,1)} %collective-permute-done.5.refs_4_, ...), custom_call_target="tpu_custom_call" | custom-call | flops 10485760 | bytes 39870464 | tf_op jit(solution)/shard_map/norm/pallas_call | solution.py:32
  167.6 2.0 collective-permute-start
  169.6 1.5 collective-permute-start.1
  171.2 0.6 reshape.23.refs_3_.refs_9_
  171.8 13.0 %flat.1 = (bf16[4096,1536]{1,0:T(8,128)(2,1)}, f32[8,128]{1,0:T(8,128)}) custom-call(bf16[4096,3,4,128]{3,2,1,0:T(4,128)(2,1)} %bitcast.7, f32[8,128]{1,0:T(8,128)} %get-tuple-element.75.refs_1_), custom_call_target="tpu_custom_call" | custom-call | flops 6291456 | bytes 25165824 | tf_op jit(solution)/shard_map/flat/pallas_call | solution.py:32
  184.8 21.4 %qkv.2 = (bf16[1024,4096]{1,0:T(8,128)(2,1)}, bf16[1024,1536]{1,0:T(8,128)(2,1)}, f32[8,128]{1,0:T(8,128)}) custom-call(bf16[2,1024,4096]{2,1,0:T(8,128)(2,1)} %refs_5_.11, f32[2,1024]{1,0:T(2,128)} %refs_7_.11, f32[2,1024]{1,0:T(2,128)} %refs_8_.7, bf16[1,4096]{1,0:T(2,128)(2,1)} %reshape.23.refs_3_.refs_9_, ...), custom_call_target="tpu_custom_call" | custom-call | flops 12884901888 | bytes 40919040 | tf_op jit(solution)/shard_map/qkv/pallas_call | solution.py:32
  206.2 21.5 %qkv.3 = (bf16[1024,4096]{1,0:T(8,128)(2,1)}, bf16[1024,1536]{1,0:T(8,128)(2,1)}, f32[8,128]{1,0:T(8,128)}) custom-call(bf16[2,1024,4096]{2,1,0:T(8,128)(2,1)} %refs_5_.11, f32[2,1024]{1,0:T(2,128)} %refs_7_.11, f32[2,1024]{1,0:T(2,128)} %refs_8_.7, bf16[1,4096]{1,0:T(2,128)(2,1)} %reshape.23.refs_3_.refs_9_, ...), custom_call_target="tpu_custom_call" | custom-call | flops 12884901888 | bytes 40919040 | tf_op jit(solution)/shard_map/qkv/pallas_call | solution.py:32
  227.7 23.1 %collective-permute-done.2.refs_4_ = bf16[128,4096]{1,0:T(8,128)(2,1)} collective-permute-done((bf16[128,4096]{1,0:T(8,128)(2,1)}, bf16[128,4096]{1,0:T(8,128)(2,1)}, u32[]{:S(2)}, u32[]{:S(2)}) %collective-permute-start.2) | collective-permute-done | bytes 1048608 | tf_op jit(solution)/shard_map/ppermute | solution.py:514
  250.8 7.1 %norm.5 = (bf16[128,4096]{1,0:T(8,128)(2,1)}, f32[8,128]{1,0:T(8,128)}) custom-call(s32[3]{0:T(128)} %pad_add_fusion.refs_0_, f32[128,4096]{1,0:T(8,128)} %get-tuple-element.66.refs_1_, bf16[128,4096]{1,0:T(8,128)(2,1)} %copy-done.2, bf16[128,4096]{1,0:T(8,128)(2,1)} %collective-permute-done.1.refs_3_, bf16[128,4096]{1,0:T(8,128)(2,1)} %collective-permute-done.2.refs_4_, ...), custom_call_target="tpu_custom_call" | custom-call | flops 10485760 | bytes 39870464 | tf_op jit(solution)/shard_map/norm/pallas_call | solution.py:32
  257.9 49.0 %attn.2 = (bf16[1024,512]{1,0:T(8,128)(2,1)}, bf16[1024,512]{1,0:T(8,128)(2,1)}, bf16[1024,512]{1,0:T(8,128)(2,1)}, bf16[1024,512]{1,0:T(8,128)(2,1)}, f32[128,4...) custom-call(bf16[1024,4096]{1,0:T(8,128)(2,1)} %all-gather.7.cloned., ...), custom_call_target="tpu_custom_call" | custom-call | flops 30064771072 | bytes 44040192 | tf_op jit(solution)/shard_map/attn/pallas_call | solution.py:32
  307.0 2.9 collective-permute-start.11
  310.4 49.0 %attn.3 = (bf16[1024,512]{1,0:T(8,128)(2,1)}, bf16[1024,512]{1,0:T(8,128)(2,1)}, bf16[1024,512]{1,0:T(8,128)(2,1)}, bf16[1024,512]{1,0:T(8,128)(2,1)}, f32[128,4...) custom-call(bf16[1024,4096]{1,0:T(8,128)(2,1)} %all-gather.5.cloned., ...), custom_call_target="tpu_custom_call" | custom-call | flops 30064771072 | bytes 44040192 | tf_op jit(solution)/shard_map/attn/pallas_call | solution.py:32
  359.4 0.9 copy-done.3
  360.4 7.1 %norm.6 = (bf16[128,4096]{1,0:T(8,128)(2,1)}, f32[8,128]{1,0:T(8,128)}) custom-call(s32[3]{0:T(128)} %pad_add_fusion.refs_0_, f32[128,4096]{1,0:T(8,128)} %get-tuple-element.96.refs_1_, bf16[128,4096]{1,0:T(8,128)(2,1)} %collective-permute-done.9.refs_2_, bf16[128,4096]{1,0:T(8,128)(2,1)} %copy-done.3, bf16[128,4096]{1,0:T(8,128)(2,1)} %collective-permute-done.11.refs_4_, ...), custom_call_target="tpu_custom_call" | custom-call | flops 10485760 | bytes 24141824 | tf_op jit(solution)/shard_map/norm/pallas_call | solution.py:32
  367.5 1.6 collective-permute-start.6
  369.1 0.5 collective-permute-start.7
  369.6 1.4 collective-permute-start.8
  371.0 41.6 %dw2.1 = (bf16[2048,4096]{1,0:T(8,128)(2,1)}, f32[8,128]{1,0:T(8,128)}) custom-call(bf16[1024,2048]{1,0:T(8,128)(2,1)} %get-tuple-element.94.refs_0_, bf16[1024,2048]{1,0:T(8,128)(2,1)} %get-tuple-element.95.refs_1_, bf16[2,1024,4096]{2,1,0:T(8,128)(2,1)} %refs_3_.5, bf16[2,1024,4096]{2,1,0:T(8,128)(2,1)} %refs_3_.5, f32[8,128]{1,0:T(8,128)} %get-tuple-element.101.refs_4_), custom_call_target="tpu_custom_call" | custom-call | flops 34359738368 | bytes 58720256 | tf_op jit(solution)/shard_map/dw2/pallas_call | solution.py:32
  412.6 41.4 %dw1.1 = (bf16[4096,2048]{1,0:T(8,128)(2,1)}, f32[8,128]{1,0:T(8,128)}) custom-call(bf16[1024,4096]{1,0:T(8,128)(2,1)} %get-tuple-element.90.refs_0_, bf16[1024,4096]{1,0:T(8,128)(2,1)} %get-tuple-element.91.refs_1_, bf16[1024,2048]{1,0:T(8,128)(2,1)} %get-tuple-element.92.refs_2_, bf16[1024,2048]{1,0:T(8,128)(2,1)} %get-tuple-element.93.refs_3_, ...), custom_call_target="tpu_custom_call" | custom-call | flops 34359738368 | bytes 41943040 | tf_op jit(solution)/shard_map/dw1/pallas_call | solution.py:32
  454.1 0.9 copy-done.1
  455.0 7.1 %norm.7 = (bf16[128,4096]{1,0:T(8,128)(2,1)}, f32[8,128]{1,0:T(8,128)}) custom-call(s32[3]{0:T(128)} %pad_add_fusion.refs_0_, f32[128,4096]{1,0:T(8,128)} %get-tuple-element.86.refs_1_, bf16[128,4096]{1,0:T(8,128)(2,1)} %copy-done.1, bf16[128,4096]{1,0:T(8,128)(2,1)} %collective-permute-done.7.refs_3_, bf16[128,4096]{1,0:T(8,128)(2,1)} %collective-permute-done.8.refs_4_, ...), custom_call_target="tpu_custom_call" | custom-call | flops 10485760 | bytes 24141824 | tf_op jit(solution)/shard_map/norm/pallas_call | solution.py:32
  462.1 13.7 %dwo.1 = (bf16[512,4096]{1,0:T(8,128)(2,1)}, f32[8,128]{1,0:T(8,128)}) custom-call(bf16[1024,512]{1,0:T(8,128)(2,1)} %get-tuple-element.114.refs_0_, bf16[1024,512]{1,0:T(8,128)(2,1)} %get-tuple-element.115.refs_1_, bf16[1024,4096]{1,0:T(8,128)(2,1)} %all-gather.7.cloned.1.call-done.refs_0_.refs_2_, ...), custom_call_target="tpu_custom_call" | custom-call | flops 8589934592 | bytes 23068672 | tf_op jit(solution)/shard_map/dwo/pallas_call | solution.py:32
  475.8 34.9 %dqkvw.1 = (bf16[4096,3,4,128]{3,2,1,0:T(4,128)(2,1)}, bf16[2,1024,4096]{2,1,0:T(8,128)(2,1)}, f32[8,128]{1,0:T(8,128)}) custom-call(bf16[1024,4096]{1,0:T(8,128)(2,1)} %get-tuple-element.105.refs_0_, bf16[1024,4096]{1,0:T(8,128)(2,1)} %get-tuple-element.106.refs_1_, bf16[1024,512]{1,0:T(8,128)(2,1)} %get-tuple-element.107.refs_2_, ...), custom_call_target="tpu_custom_call" | custom-call | flops 25769803776 | bytes 60817408 | tf_op jit(solution)/shard_map/dqkvw/pallas_call | solution.py:32
  510.7 6.4 %copy.21 = (bf16[2,1024,4096]{2,1,0:T(8,128)(2,1)}, f32[8,128]{1,0:T(8,128)}) custom-call(bf16[1024,4096]{1,0:T(8,128)(2,1)} %all-gather.9.cloned.1.call-done.refs_0_, bf16[2,1024,4096]{2,1,0:T(8,128)(2,1)} %get-tuple-element.118.refs_1_, f32[8,128]{1,0:T(8,128)} %get-tuple-element.119.refs_2_), custom_call_target="tpu_custom_call", output_to_operand_aliasing={{0}: (1, {})} | custom-call | flops 4194304 | bytes 41943040 | tf_op jit(solution)/shard_map/copy/pallas_call | solution.py:32
  (34 shorter events, 0.9 us)
Async XLA Ops:
  7.2 250.7 %all-gather.7.cloned.1.call-start = ((), (), s32[]{:S(2)}) async-start(), calls=%async_computation.1 | async-start | bytes 9437184 | tf_op jit(solution)/shard_map/all_gather | solution.py:537
  82.4 77.0 %collective-permute-start.3 = (bf16[128,4096]{1,0:T(8,128)(2,1)}, bf16[128,4096]{1,0:T(8,128)(2,1)S(1)}, u32[]{:S(2)}, u32[]{:S(2)}) collective-permute-start(bf16[128,4096]{1,0:T(8,128)(2,1)} %get-tuple-element.71), channel_id=1, source_target_pairs={{0,2},{1,3},{2,0},{3,1},{4,6},{5,7},{6,4},{7,5}} | collective-permute-start | bytes 3145736 | tf_op jit(solution)/shard_map/ppermute | solution.py:514
  85.0 74.4 %collective-permute-start.4 = (bf16[128,4096]{1,0:T(8,128)(2,1)}, bf16[128,4096]{1,0:T(8,128)(2,1)}, u32[]{:S(2)}, u32[]{:S(2)}) collective-permute-start(bf16[128,4096]{1,0:T(8,128)(2,1)} %get-tuple-element.72), channel_id=1, source_target_pairs={{0,4},{1,5},{2,6},{3,7},{4,0},{5,1},{6,2},{7,3}} | collective-permute-start | bytes 3145736 | tf_op jit(solution)/shard_map/ppermute | solution.py:514
  86.5 72.9 %collective-permute-start.5 = (bf16[128,4096]{1,0:T(8,128)(2,1)}, bf16[128,4096]{1,0:T(8,128)(2,1)}, u32[]{:S(2)}, u32[]{:S(2)}) collective-permute-start(bf16[128,4096]{1,0:T(8,128)(2,1)} %get-tuple-element.73), channel_id=1, source_target_pairs={{0,6},{1,7},{2,4},{3,5},{4,2},{5,3},{6,0},{7,1}} | collective-permute-start | bytes 3145736 | tf_op jit(solution)/shard_map/ppermute | solution.py:514
  159.4 1.0 copy-start
  160.4 10.8 %copy-start.4 = (bf16[4096]{0:T(1024)(128)(2,1)S(1)}, bf16[4096]{0:T(1024)(128)(2,1)}, u32[]{:S(2)}) copy-start(bf16[4096]{0:T(1024)(128)(2,1)} %param.20) | copy-start | bytes 24580
  167.6 142.8 %all-gather.5.cloned.1.call-start = ((), (), s32[]{:S(2)}) async-start(), calls=%async_computation | async-start | bytes 9437184 | tf_op jit(solution)/shard_map/all_gather | solution.py:537
  167.6 60.0 %collective-permute-start = (bf16[128,4096]{1,0:T(8,128)(2,1)}, bf16[128,4096]{1,0:T(8,128)(2,1)S(1)}, u32[]{:S(2)}, u32[]{:S(2)}) collective-permute-start(bf16[128,4096]{1,0:T(8,128)(2,1)} %get-tuple-element.67), channel_id=1, source_target_pairs={{0,2},{1,3},{2,0},{3,1},{4,6},{5,7},{6,4},{7,5}} | collective-permute-start | bytes 3145736 | tf_op jit(solution)/shard_map/ppermute | solution.py:514
  169.6 58.1 %collective-permute-start.1 = (bf16[128,4096]{1,0:T(8,128)(2,1)}, bf16[128,4096]{1,0:T(8,128)(2,1)}, u32[]{:S(2)}, u32[]{:S(2)}) collective-permute-start(bf16[128,4096]{1,0:T(8,128)(2,1)} %get-tuple-element.68), channel_id=1, source_target_pairs={{0,4},{1,5},{2,6},{3,7},{4,0},{5,1},{6,2},{7,3}} | collective-permute-start | bytes 3145736 | tf_op jit(solution)/shard_map/ppermute | solution.py:514
  171.1 79.6 %collective-permute-start.2 = (bf16[128,4096]{1,0:T(8,128)(2,1)}, bf16[128,4096]{1,0:T(8,128)(2,1)}, u32[]{:S(2)}, u32[]{:S(2)}) collective-permute-start(bf16[128,4096]{1,0:T(8,128)(2,1)} %get-tuple-element.69), channel_id=1, source_target_pairs={{0,6},{1,7},{2,4},{3,5},{4,2},{5,3},{6,0},{7,1}} | collective-permute-start | bytes 3145736 | tf_op jit(solution)/shard_map/ppermute | solution.py:514
  227.7 23.1 %copy-start.2 = (bf16[128,4096]{1,0:T(8,128)(2,1)}, bf16[128,4096]{1,0:T(8,128)(2,1)S(1)}, u32[]{:S(2)}) copy-start(bf16[128,4096]{1,0:T(8,128)(2,1)S(1)} %collective-permute-done.refs_2_) | copy-start | bytes 3145732
  257.8 217.9 %all-gather.11.cloned.1.call-start = ((), (), s32[]{:S(2)}) async-start(), calls=%async_computation.3 | async-start | bytes 9437184 | tf_op jit(solution)/shard_map/all_gather | solution.py:537
  306.9 52.5 %collective-permute-start.10 = (bf16[128,4096]{1,0:T(8,128)(2,1)}, bf16[128,4096]{1,0:T(8,128)(2,1)S(1)}, u32[]{:S(2)}, u32[]{:S(2)}) collective-permute-start(bf16[128,4096]{1,0:T(8,128)(2,1)} %get-tuple-element.98), channel_id=1, source_target_pairs={{0,4},{1,5},{2,6},{3,7},{4,0},{5,1},{6,2},{7,3}} | collective-permute-start | bytes 3145736 | tf_op jit(solution)/shard_map/ppermute | solution.py:514
  307.0 52.4 %collective-permute-start.11 = (bf16[128,4096]{1,0:T(8,128)(2,1)}, bf16[128,4096]{1,0:T(8,128)(2,1)}, u32[]{:S(2)}, u32[]{:S(2)}) collective-permute-start(bf16[128,4096]{1,0:T(8,128)(2,1)} %get-tuple-element.99), channel_id=1, source_target_pairs={{0,6},{1,7},{2,4},{3,5},{4,2},{5,3},{6,0},{7,1}} | collective-permute-start | bytes 3145736 | tf_op jit(solution)/shard_map/ppermute | solution.py:514
  310.0 49.5 %collective-permute-start.9 = (bf16[128,4096]{1,0:T(8,128)(2,1)}, bf16[128,4096]{1,0:T(8,128)(2,1)}, u32[]{:S(2)}, u32[]{:S(2)}) collective-permute-start(bf16[128,4096]{1,0:T(8,128)(2,1)} %get-tuple-element.97), channel_id=1, source_target_pairs={{0,2},{1,3},{2,0},{3,1},{4,6},{5,7},{6,4},{7,5}} | collective-permute-start | bytes 3145736 | tf_op jit(solution)/shard_map/ppermute | solution.py:514
  359.4 1.0 copy-start.3
  367.5 143.3 %all-gather.9.cloned.1.call-start = ((), (), s32[]{:S(2)}) async-start(), calls=%async_computation.2 | async-start | bytes 9437184 | tf_op jit(solution)/shard_map/all_gather | solution.py:537
  367.5 86.5 %collective-permute-start.6 = (bf16[128,4096]{1,0:T(8,128)(2,1)}, bf16[128,4096]{1,0:T(8,128)(2,1)S(1)}, u32[]{:S(2)}, u32[]{:S(2)}) collective-permute-start(bf16[128,4096]{1,0:T(8,128)(2,1)} %get-tuple-element.87), channel_id=1, source_target_pairs={{0,2},{1,3},{2,0},{3,1},{4,6},{5,7},{6,4},{7,5}} | collective-permute-start | bytes 3145736 | tf_op jit(solution)/shard_map/ppermute | solution.py:514
  369.1 85.0 %collective-permute-start.7 = (bf16[128,4096]{1,0:T(8,128)(2,1)}, bf16[128,4096]{1,0:T(8,128)(2,1)}, u32[]{:S(2)}, u32[]{:S(2)}) collective-permute-start(bf16[128,4096]{1,0:T(8,128)(2,1)} %get-tuple-element.88), channel_id=1, source_target_pairs={{0,4},{1,5},{2,6},{3,7},{4,0},{5,1},{6,2},{7,3}} | collective-permute-start | bytes 3145736 | tf_op jit(solution)/shard_map/ppermute | solution.py:514
  369.6 84.5 %collective-permute-start.8 = (bf16[128,4096]{1,0:T(8,128)(2,1)}, bf16[128,4096]{1,0:T(8,128)(2,1)}, u32[]{:S(2)}, u32[]{:S(2)}) collective-permute-start(bf16[128,4096]{1,0:T(8,128)(2,1)} %get-tuple-element.89), channel_id=1, source_target_pairs={{0,6},{1,7},{2,4},{3,5},{4,2},{5,3},{6,0},{7,1}} | collective-permute-start | bytes 3145736 | tf_op jit(solution)/shard_map/ppermute | solution.py:514
  454.0 1.0 copy-start.1
Sparse Core Ops, SparseCore 0:
  167.7 85.0 all-gather.6
  258.0 48.4 all-gather.4
  367.6 84.6 all-gather.10
  462.2 48.4 all-gather.8

commit v5 on v4

--- a/solution.py
+++ b/solution.py
@@ -169,10 +169,11 @@
             rows = pl.ds(pl.multiple_of(r * part, part), part)
             h_copy, dy_copy = load(r)
             h_copy.wait()
-            n_v[rows, :] = normed(n_v[rows, :], mu_ref[m:m + 1, rows], rs_ref[m:m + 1, rows], g_ref[...])
             dy_copy.wait()
-            a_v[rows, :] = mm(n_v[rows, :], up_ref[...])
             b_v[rows, :] = mm(dy_v[rows, :], down_ref[...], NT)
+            hat = normed(n_v[rows, :], mu_ref[m:m + 1, rows], rs_ref[m:m + 1, rows], g_ref[...])
+            n_v[rows, :] = hat
+            a_v[rows, :] = mm(hat, up_ref[...])
 
         n_out.start()
 

time: 532 us -> 528 us (level)
  no operation moved by 1% of the time
where the time goes in v5:
time: 528 us; the launch traced here: 521 us
  Pallas kernels  462 us (88%)
  waiting for transfers between devices  23.2 us (4%)
  starting transfers between devices  14.8 us (3%)
  between operations  14.4 us (3%)
  local copies, waits for them, and re-layouts  5.36 us (1%)
    pallas_call x16, Pallas kernels, call(): pl.pallas_call(kernel, grid_spec=pltpu.PrefetchScalarGridSpec(num_scalar_...  462 us
    ppermute x12, waiting for transfers between devices, swap(): return lax.ppermute(arr, 'tp', [(i, i ^ bit) for i in range(8)])  23.1 us
    ppermute x12, starting transfers between devices, swap(): return lax.ppermute(arr, 'tp', [(i, i ^ bit) for i in range(8)])  14.6 us
  transfers between devices with their start and end apart: 16, of which 1 were waited for; matrix products, arithmetic and copies ran while one was open for 0% of the time, Pallas kernels for 71%

profile of v5, /device:TPU:0, one launch (start us, length us, event | category | flops | bytes accessed | tf_op | source)
XLA Modules:
  0.0 520.5 jit_solution(17359874507501784982)
XLA Ops:
  7.2 1.3 reshape.22.refs_4_.refs_9_
  8.5 0.6 broadcast_in_dim.3.refs_8_
  9.1 71.2 %mlp.2 = (bf16[1024,4096]{1,0:T(8,128)(2,1)}, bf16[1024,2048]{1,0:T(8,128)(2,1)}, bf16[1024,2048]{1,0:T(8,128)(2,1)}, f32[128,4096]{1,0:T(8,128)}, bf16[128,4096...) custom-call(bf16[2,1024,4096]{2,1,0:T(8,128)(2,1)} %refs_5_.9, ...), custom_call_target="tpu_custom_call" | custom-call | flops 51539607552 | bytes 105930752 | tf_op jit(solution)/shard_map/mlp/pallas_call | solution.py:32
  80.3 2.6 collective-permute-start.3
  82.9 1.5 collective-permute-start.4
  84.4 70.7 %mlp.3 = (bf16[1024,4096]{1,0:T(8,128)(2,1)}, bf16[1024,2048]{1,0:T(8,128)(2,1)}, bf16[1024,2048]{1,0:T(8,128)(2,1)}, f32[128,4096]{1,0:T(8,128)}, bf16[128,4096...) custom-call(bf16[2,1024,4096]{2,1,0:T(8,128)(2,1)} %refs_5_.9, ...), custom_call_target="tpu_custom_call" | custom-call | flops 51539607552 | bytes 105930752 | tf_op jit(solution)/shard_map/mlp/pallas_call | solution.py:32
  155.2 0.6 pad_add_fusion.refs_0_
  155.8 1.0 copy-done
  156.7 7.2 %norm.4 = (bf16[128,4096]{1,0:T(8,128)(2,1)}, f32[8,128]{1,0:T(8,128)}) custom-call(s32[3]{0:T(128)} %pad_add_fusion.refs_0_, f32[128,4096]{1,0:T(8,128)} %get-tuple-element.70.refs_1_, bf16[128,4096]{1,0:T(8,128)(2,1)} %copy-done, bf16[128,4096]{1,0:T(8,128)(2,1)} %collective-permute-done.4.refs_3_, bf16[128,4096]{1,0:T(8,128)(2,1)} %collective-permute-done.5.refs_4_, ...), custom_call_target="tpu_custom_call" | custom-call | flops 10485760 | bytes 39870464 | tf_op jit(solution)/shard_map/norm/pallas_call | solution.py:32
  164.0 2.0 collective-permute-start
  166.0 1.5 collective-permute-start.1
  167.5 0.6 reshape.23.refs_3_.refs_9_
  168.1 13.0 %flat.1 = (bf16[4096,1536]{1,0:T(8,128)(2,1)}, f32[8,128]{1,0:T(8,128)}) custom-call(bf16[4096,3,4,128]{3,2,1,0:T(4,128)(2,1)} %bitcast.7, f32[8,128]{1,0:T(8,128)} %get-tuple-element.75.refs_1_), custom_call_target="tpu_custom_call" | custom-call | flops 6291456 | bytes 25165824 | tf_op jit(solution)/shard_map/flat/pallas_call | solution.py:32
  181.1 21.4 %qkv.2 = (bf16[1024,4096]{1,0:T(8,128)(2,1)}, bf16[1024,1536]{1,0:T(8,128)(2,1)}, f32[8,128]{1,0:T(8,128)}) custom-call(bf16[2,1024,4096]{2,1,0:T(8,128)(2,1)} %refs_5_.11, f32[2,1024]{1,0:T(2,128)} %refs_7_.11, f32[2,1024]{1,0:T(2,128)} %refs_8_.7, bf16[1,4096]{1,0:T(2,128)(2,1)} %reshape.23.refs_3_.refs_9_, ...), custom_call_target="tpu_custom_call" | custom-call | flops 12884901888 | bytes 40919040 | tf_op jit(solution)/shard_map/qkv/pallas_call | solution.py:32
  202.6 21.5 %qkv.3 = (bf16[1024,4096]{1,0:T(8,128)(2,1)}, bf16[1024,1536]{1,0:T(8,128)(2,1)}, f32[8,128]{1,0:T(8,128)}) custom-call(bf16[2,1024,4096]{2,1,0:T(8,128)(2,1)} %refs_5_.11, f32[2,1024]{1,0:T(2,128)} %refs_7_.11, f32[2,1024]{1,0:T(2,128)} %refs_8_.7, bf16[1,4096]{1,0:T(2,128)(2,1)} %reshape.23.refs_3_.refs_9_, ...), custom_call_target="tpu_custom_call" | custom-call | flops 12884901888 | bytes 40919040 | tf_op jit(solution)/shard_map/qkv/pallas_call | solution.py:32
  224.1 23.0 %collective-permute-done.2.refs_4_ = bf16[128,4096]{1,0:T(8,128)(2,1)} collective-permute-done((bf16[128,4096]{1,0:T(8,128)(2,1)}, bf16[128,4096]{1,0:T(8,128)(2,1)}, u32[]{:S(2)}, u32[]{:S(2)}) %collective-permute-start.2) | collective-permute-done | bytes 1048608 | tf_op jit(solution)/shard_map/ppermute | solution.py:515
  247.1 7.1 %norm.5 = (bf16[128,4096]{1,0:T(8,128)(2,1)}, f32[8,128]{1,0:T(8,128)}) custom-call(s32[3]{0:T(128)} %pad_add_fusion.refs_0_, f32[128,4096]{1,0:T(8,128)} %get-tuple-element.66.refs_1_, bf16[128,4096]{1,0:T(8,128)(2,1)} %copy-done.2, bf16[128,4096]{1,0:T(8,128)(2,1)} %collective-permute-done.1.refs_3_, bf16[128,4096]{1,0:T(8,128)(2,1)} %collective-permute-done.2.refs_4_, ...), custom_call_target="tpu_custom_call" | custom-call | flops 10485760 | bytes 39870464 | tf_op jit(solution)/shard_map/norm/pallas_call | solution.py:32
  254.3 49.0 %attn.2 = (bf16[1024,512]{1,0:T(8,128)(2,1)}, bf16[1024,512]{1,0:T(8,128)(2,1)}, bf16[1024,512]{1,0:T(8,128)(2,1)}, bf16[1024,512]{1,0:T(8,128)(2,1)}, f32[128,4...) custom-call(bf16[1024,4096]{1,0:T(8,128)(2,1)} %all-gather.7.cloned., ...), custom_call_target="tpu_custom_call" | custom-call | flops 30064771072 | bytes 44040192 | tf_op jit(solution)/shard_map/attn/pallas_call | solution.py:32
  303.4 2.9 collective-permute-start.11
  306.8 49.0 %attn.3 = (bf16[1024,512]{1,0:T(8,128)(2,1)}, bf16[1024,512]{1,0:T(8,128)(2,1)}, bf16[1024,512]{1,0:T(8,128)(2,1)}, bf16[1024,512]{1,0:T(8,128)(2,1)}, f32[128,4...) custom-call(bf16[1024,4096]{1,0:T(8,128)(2,1)} %all-gather.5.cloned., ...), custom_call_target="tpu_custom_call" | custom-call | flops 30064771072 | bytes 44040192 | tf_op jit(solution)/shard_map/attn/pallas_call | solution.py:32
  355.8 0.9 copy-done.3
  356.7 7.1 %norm.6 = (bf16[128,4096]{1,0:T(8,128)(2,1)}, f32[8,128]{1,0:T(8,128)}) custom-call(s32[3]{0:T(128)} %pad_add_fusion.refs_0_, f32[128,4096]{1,0:T(8,128)} %get-tuple-element.96.refs_1_, bf16[128,4096]{1,0:T(8,128)(2,1)} %collective-permute-done.9.refs_2_, bf16[128,4096]{1,0:T(8,128)(2,1)} %copy-done.3, bf16[128,4096]{1,0:T(8,128)(2,1)} %collective-permute-done.11.refs_4_, ...), custom_call_target="tpu_custom_call" | custom-call | flops 10485760 | bytes 24141824 | tf_op jit(solution)/shard_map/norm/pallas_call | solution.py:32
  363.9 1.6 collective-permute-start.6
  365.4 0.5 collective-permute-start.7
  365.9 1.4 collective-permute-start.8
  367.4 41.6 %dw2.1 = (bf16[2048,4096]{1,0:T(8,128)(2,1)}, f32[8,128]{1,0:T(8,128)}) custom-call(bf16[1024,2048]{1,0:T(8,128)(2,1)} %get-tuple-element.94.refs_0_, bf16[1024,2048]{1,0:T(8,128)(2,1)} %get-tuple-element.95.refs_1_, bf16[2,1024,4096]{2,1,0:T(8,128)(2,1)} %refs_3_.5, bf16[2,1024,4096]{2,1,0:T(8,128)(2,1)} %refs_3_.5, f32[8,128]{1,0:T(8,128)} %get-tuple-element.101.refs_4_), custom_call_target="tpu_custom_call" | custom-call | flops 34359738368 | bytes 58720256 | tf_op jit(solution)/shard_map/dw2/pallas_call | solution.py:32
  409.0 41.4 %dw1.1 = (bf16[4096,2048]{1,0:T(8,128)(2,1)}, f32[8,128]{1,0:T(8,128)}) custom-call(bf16[1024,4096]{1,0:T(8,128)(2,1)} %get-tuple-element.90.refs_0_, bf16[1024,4096]{1,0:T(8,128)(2,1)} %get-tuple-element.91.refs_1_, bf16[1024,2048]{1,0:T(8,128)(2,1)} %get-tuple-element.92.refs_2_, bf16[1024,2048]{1,0:T(8,128)(2,1)} %get-tuple-element.93.refs_3_, ...), custom_call_target="tpu_custom_call" | custom-call | flops 34359738368 | bytes 41943040 | tf_op jit(solution)/shard_map/dw1/pallas_call | solution.py:32
  450.4 0.9 copy-done.1
  451.4 7.1 %norm.7 = (bf16[128,4096]{1,0:T(8,128)(2,1)}, f32[8,128]{1,0:T(8,128)}) custom-call(s32[3]{0:T(128)} %pad_add_fusion.refs_0_, f32[128,4096]{1,0:T(8,128)} %get-tuple-element.86.refs_1_, bf16[128,4096]{1,0:T(8,128)(2,1)} %copy-done.1, bf16[128,4096]{1,0:T(8,128)(2,1)} %collective-permute-done.7.refs_3_, bf16[128,4096]{1,0:T(8,128)(2,1)} %collective-permute-done.8.refs_4_, ...), custom_call_target="tpu_custom_call" | custom-call | flops 10485760 | bytes 24141824 | tf_op jit(solution)/shard_map/norm/pallas_call | solution.py:32
  458.5 13.7 %dwo.1 = (bf16[512,4096]{1,0:T(8,128)(2,1)}, f32[8,128]{1,0:T(8,128)}) custom-call(bf16[1024,512]{1,0:T(8,128)(2,1)} %get-tuple-element.114.refs_0_, bf16[1024,512]{1,0:T(8,128)(2,1)} %get-tuple-element.115.refs_1_, bf16[1024,4096]{1,0:T(8,128)(2,1)} %all-gather.7.cloned.1.call-done.refs_0_.refs_2_, ...), custom_call_target="tpu_custom_call" | custom-call | flops 8589934592 | bytes 23068672 | tf_op jit(solution)/shard_map/dwo/pallas_call | solution.py:32
  472.1 34.9 %dqkvw.1 = (bf16[4096,3,4,128]{3,2,1,0:T(4,128)(2,1)}, bf16[2,1024,4096]{2,1,0:T(8,128)(2,1)}, f32[8,128]{1,0:T(8,128)}) custom-call(bf16[1024,4096]{1,0:T(8,128)(2,1)} %get-tuple-element.105.refs_0_, bf16[1024,4096]{1,0:T(8,128)(2,1)} %get-tuple-element.106.refs_1_, bf16[1024,512]{1,0:T(8,128)(2,1)} %get-tuple-element.107.refs_2_, ...), custom_call_target="tpu_custom_call" | custom-call | flops 25769803776 | bytes 60817408 | tf_op jit(solution)/shard_map/dqkvw/pallas_call | solution.py:32
  507.1 6.4 %copy.21 = (bf16[2,1024,4096]{2,1,0:T(8,128)(2,1)}, f32[8,128]{1,0:T(8,128)}) custom-call(bf16[1024,4096]{1,0:T(8,128)(2,1)} %all-gather.9.cloned.1.call-done.refs_0_, bf16[2,1024,4096]{2,1,0:T(8,128)(2,1)} %get-tuple-element.118.refs_1_, f32[8,128]{1,0:T(8,128)} %get-tuple-element.119.refs_2_), custom_call_target="tpu_custom_call", output_to_operand_aliasing={{0}: (1, {})} | custom-call | flops 4194304 | bytes 41943040 | tf_op jit(solution)/shard_map/copy/pallas_call | solution.py:32
  (34 shorter events, 0.9 us)
Async XLA Ops:
  7.2 247.1 %all-gather.7.cloned.1.call-start = ((), (), s32[]{:S(2)}) async-start(), calls=%async_computation.1 | async-start | bytes 9437184 | tf_op jit(solution)/shard_map/all_gather | solution.py:538
  80.3 75.5 %collective-permute-start.3 = (bf16[128,4096]{1,0:T(8,128)(2,1)}, bf16[128,4096]{1,0:T(8,128)(2,1)S(1)}, u32[]{:S(2)}, u32[]{:S(2)}) collective-permute-start(bf16[128,4096]{1,0:T(8,128)(2,1)} %get-tuple-element.71), channel_id=1, source_target_pairs={{0,2},{1,3},{2,0},{3,1},{4,6},{5,7},{6,4},{7,5}} | collective-permute-start | bytes 3145736 | tf_op jit(solution)/shard_map/ppermute | solution.py:515
  82.9 72.9 %collective-permute-start.4 = (bf16[128,4096]{1,0:T(8,128)(2,1)}, bf16[128,4096]{1,0:T(8,128)(2,1)}, u32[]{:S(2)}, u32[]{:S(2)}) collective-permute-start(bf16[128,4096]{1,0:T(8,128)(2,1)} %get-tuple-element.72), channel_id=1, source_target_pairs={{0,4},{1,5},{2,6},{3,7},{4,0},{5,1},{6,2},{7,3}} | collective-permute-start | bytes 3145736 | tf_op jit(solution)/shard_map/ppermute | solution.py:515
  84.4 71.4 %collective-permute-start.5 = (bf16[128,4096]{1,0:T(8,128)(2,1)}, bf16[128,4096]{1,0:T(8,128)(2,1)}, u32[]{:S(2)}, u32[]{:S(2)}) collective-permute-start(bf16[128,4096]{1,0:T(8,128)(2,1)} %get-tuple-element.73), channel_id=1, source_target_pairs={{0,6},{1,7},{2,4},{3,5},{4,2},{5,3},{6,0},{7,1}} | collective-permute-start | bytes 3145736 | tf_op jit(solution)/shard_map/ppermute | solution.py:515
  155.8 1.0 copy-start
  156.7 10.8 %copy-start.4 = (bf16[4096]{0:T(1024)(128)(2,1)S(1)}, bf16[4096]{0:T(1024)(128)(2,1)}, u32[]{:S(2)}) copy-start(bf16[4096]{0:T(1024)(128)(2,1)} %param.20) | copy-start | bytes 24580
  164.0 142.8 %all-gather.5.cloned.1.call-start = ((), (), s32[]{:S(2)}) async-start(), calls=%async_computation | async-start | bytes 9437184 | tf_op jit(solution)/shard_map/all_gather | solution.py:538
  164.0 60.0 %collective-permute-start = (bf16[128,4096]{1,0:T(8,128)(2,1)}, bf16[128,4096]{1,0:T(8,128)(2,1)S(1)}, u32[]{:S(2)}, u32[]{:S(2)}) collective-permute-start(bf16[128,4096]{1,0:T(8,128)(2,1)} %get-tuple-element.67), channel_id=1, source_target_pairs={{0,2},{1,3},{2,0},{3,1},{4,6},{5,7},{6,4},{7,5}} | collective-permute-start | bytes 3145736 | tf_op jit(solution)/shard_map/ppermute | solution.py:515
  166.0 58.1 %collective-permute-start.1 = (bf16[128,4096]{1,0:T(8,128)(2,1)}, bf16[128,4096]{1,0:T(8,128)(2,1)}, u32[]{:S(2)}, u32[]{:S(2)}) collective-permute-start(bf16[128,4096]{1,0:T(8,128)(2,1)} %get-tuple-element.68), channel_id=1, source_target_pairs={{0,4},{1,5},{2,6},{3,7},{4,0},{5,1},{6,2},{7,3}} | collective-permute-start | bytes 3145736 | tf_op jit(solution)/shard_map/ppermute | solution.py:515
  167.5 79.6 %collective-permute-start.2 = (bf16[128,4096]{1,0:T(8,128)(2,1)}, bf16[128,4096]{1,0:T(8,128)(2,1)}, u32[]{:S(2)}, u32[]{:S(2)}) collective-permute-start(bf16[128,4096]{1,0:T(8,128)(2,1)} %get-tuple-element.69), channel_id=1, source_target_pairs={{0,6},{1,7},{2,4},{3,5},{4,2},{5,3},{6,0},{7,1}} | collective-permute-start | bytes 3145736 | tf_op jit(solution)/shard_map/ppermute | solution.py:515
  224.0 23.1 %copy-start.2 = (bf16[128,4096]{1,0:T(8,128)(2,1)}, bf16[128,4096]{1,0:T(8,128)(2,1)S(1)}, u32[]{:S(2)}) copy-start(bf16[128,4096]{1,0:T(8,128)(2,1)S(1)} %collective-permute-done.refs_2_) | copy-start | bytes 3145732
  254.2 218.0 %all-gather.11.cloned.1.call-start = ((), (), s32[]{:S(2)}) async-start(), calls=%async_computation.3 | async-start | bytes 9437184 | tf_op jit(solution)/shard_map/all_gather | solution.py:538
  303.3 52.5 %collective-permute-start.10 = (bf16[128,4096]{1,0:T(8,128)(2,1)}, bf16[128,4096]{1,0:T(8,128)(2,1)S(1)}, u32[]{:S(2)}, u32[]{:S(2)}) collective-permute-start(bf16[128,4096]{1,0:T(8,128)(2,1)} %get-tuple-element.98), channel_id=1, source_target_pairs={{0,4},{1,5},{2,6},{3,7},{4,0},{5,1},{6,2},{7,3}} | collective-permute-start | bytes 3145736 | tf_op jit(solution)/shard_map/ppermute | solution.py:515
  303.4 52.4 %collective-permute-start.11 = (bf16[128,4096]{1,0:T(8,128)(2,1)}, bf16[128,4096]{1,0:T(8,128)(2,1)}, u32[]{:S(2)}, u32[]{:S(2)}) collective-permute-start(bf16[128,4096]{1,0:T(8,128)(2,1)} %get-tuple-element.99), channel_id=1, source_target_pairs={{0,6},{1,7},{2,4},{3,5},{4,2},{5,3},{6,0},{7,1}} | collective-permute-start | bytes 3145736 | tf_op jit(solution)/shard_map/ppermute | solution.py:515
  306.3 49.5 %collective-permute-start.9 = (bf16[128,4096]{1,0:T(8,128)(2,1)}, bf16[128,4096]{1,0:T(8,128)(2,1)}, u32[]{:S(2)}, u32[]{:S(2)}) collective-permute-start(bf16[128,4096]{1,0:T(8,128)(2,1)} %get-tuple-element.97), channel_id=1, source_target_pairs={{0,2},{1,3},{2,0},{3,1},{4,6},{5,7},{6,4},{7,5}} | collective-permute-start | bytes 3145736 | tf_op jit(solution)/shard_map/ppermute | solution.py:515
  355.8 1.0 copy-start.3
  363.8 143.3 %all-gather.9.cloned.1.call-start = ((), (), s32[]{:S(2)}) async-start(), calls=%async_computation.2 | async-start | bytes 9437184 | tf_op jit(solution)/shard_map/all_gather | solution.py:538
  363.9 86.5 %collective-permute-start.6 = (bf16[128,4096]{1,0:T(8,128)(2,1)}, bf16[128,4096]{1,0:T(8,128)(2,1)S(1)}, u32[]{:S(2)}, u32[]{:S(2)}) collective-permute-start(bf16[128,4096]{1,0:T(8,128)(2,1)} %get-tuple-element.87), channel_id=1, source_target_pairs={{0,2},{1,3},{2,0},{3,1},{4,6},{5,7},{6,4},{7,5}} | collective-permute-start | bytes 3145736 | tf_op jit(solution)/shard_map/ppermute | solution.py:515
  365.4 85.0 %collective-permute-start.7 = (bf16[128,4096]{1,0:T(8,128)(2,1)}, bf16[128,4096]{1,0:T(8,128)(2,1)}, u32[]{:S(2)}, u32[]{:S(2)}) collective-permute-start(bf16[128,4096]{1,0:T(8,128)(2,1)} %get-tuple-element.88), channel_id=1, source_target_pairs={{0,4},{1,5},{2,6},{3,7},{4,0},{5,1},{6,2},{7,3}} | collective-permute-start | bytes 3145736 | tf_op jit(solution)/shard_map/ppermute | solution.py:515
  365.9 84.5 %collective-permute-start.8 = (bf16[128,4096]{1,0:T(8,128)(2,1)}, bf16[128,4096]{1,0:T(8,128)(2,1)}, u32[]{:S(2)}, u32[]{:S(2)}) collective-permute-start(bf16[128,4096]{1,0:T(8,128)(2,1)} %get-tuple-element.89), channel_id=1, source_target_pairs={{0,6},{1,7},{2,4},{3,5},{4,2},{5,3},{6,0},{7,1}} | collective-permute-start | bytes 3145736 | tf_op jit(solution)/shard_map/ppermute | solution.py:515
  450.4 1.0 copy-start.1
Sparse Core Ops, SparseCore 0:
  164.1 85.0 all-gather.6
  254.3 48.4 all-gather.4
  363.9 84.6 all-gather.10
  458.6 48.4 all-gather.8
